TPU v7x, 32 devices: a 4x4x1 block of a 4x4x8 slice. The times are simulated.
32 devices in a mesh: dp: 2 (over z, core), tp: 16 (over x, y).
Axes of the slice: x: 4, y: 4, z: 1, core: 2. Of those that a mesh axis runs over, the one named last changes fastest.
The devices are a block of a 4x4x8 slice.
Arguments:
- x: bfloat16 [5120, 7168], P(('dp', 'tp')), parts along dimension 0
- dy: bfloat16 [5120, 7168], P(('dp', 'tp')), parts along dimension 0
- gate: bfloat16 [5120, 20480], P('dp', 'tp'), parts along dimension 0
- up: bfloat16 [5120, 20480], P('dp', 'tp'), parts along dimension 0
- w_gate: bfloat16 [7168, 20480], P(None, 'tp')
- w_up: bfloat16 [7168, 20480], P(None, 'tp')
- w_down: bfloat16 [20480, 7168], P('tp')
Outputs:
- output 1: bfloat16 [5120, 7168], P(('dp', 'tp')), parts along dimension 0
- output 2: bfloat16 [14336, 20480], P('dp', 'tp'), parts along dimension 0
- output 3: bfloat16 [14336, 20480], P('dp', 'tp'), parts along dimension 0
- output 4: bfloat16 [40960, 7168], P(('dp', 'tp')), parts along dimension 0
There are 2 independent parts. A program takes and returns all parts, laid end to end along the dimension named above; an argument that names none is the same for every part.
All inputs are finite; a program needn't handle non-finite values.
Results may differ from a plain program's by a relative error of at most 0.012.
Values are sent between devices in bfloat16 or wider.
A program may use at most 768 MiB of HBM per device.

v0:
```python
import jax
import jax.numpy as jnp


def act(gate, up):
    return jax.nn.silu(gate) * up


def solution(mesh):
    def step(x, dy, gate, up, w_gate, w_up, w_down):
        hidden, back = jax.vjp(act, gate.astype(jnp.float32), up.astype(jnp.float32))
        d_hidden = jnp.dot(dy, w_down.T, preferred_element_type=jnp.float32)
        d_gate, d_up = (g.astype(jnp.bfloat16) for g in back(d_hidden))
        dx = jnp.dot(d_gate, w_gate.T) + jnp.dot(d_up, w_up.T)
        groups = mesh.shape["dp"]

        def by_group(a, b):
            a, b = (t.reshape(groups, -1, t.shape[-1]) for t in (a, b))
            product = jnp.einsum("gta,gtb->gab", a, b, preferred_element_type=jnp.float32)
            return product.astype(jnp.bfloat16).reshape(-1, b.shape[-1])

        return dx, by_group(x, d_gate), by_group(x, d_up), by_group(hidden.astype(jnp.bfloat16), dy)

    return step
```

profile of v0, /device:TPU:97, one launch (start us, length us, event | category | flops | bytes accessed | tf_op | source)
XLA Modules:
  0.0 678.7 jit_solution(18094673797878172332)
XLA Ops:
  7.2 0.1 all-gather.11.cloned.1.call-start
  7.2 0.7 all-gather.11.cloned.1.call-update
  8.0 0.1 all-gather.13.cloned.1.call-start
  8.0 0.7 all-gather.13.cloned.1.call-update
  8.8 0.1 reduce-scatter.4.cloned.1.call-start
  8.9 212.8 %all-gather.11.cloned.1.call-done = bf16[2560,7168]{1,0:T(8,128)(2,1)} async-done(((bf16[160,7168]{1,0:T(8,128)(2,1)}), bf16[2560,7168]{1,0:T(8,128)(2,1)}) %all-gather.11.cloned.1.call-update) | async-done | bytes 36700176 | tf_op args[1]
  221.6 65.6 %fusion.8 = (bf16[2560,1280]{1,0:T(8,128)(2,1)}, f32[2560,1280]{1,0:T(8,128)}) fusion(bf16[2560,1280]{1,0:T(8,128)(2,1)} %param.3, bf16[2560,1280]{1,0:T(8,128)(2,1)} %param.2, bf16[2560,7168]{1,0:T(8,128)(2,1)} %all-gather.11.cloned.1.call-done, bf16[1280,7168]{1,0:T(8,128)(2,1)} %param.1), kind=kOutput, calls=%fused_computation.18 | convolution fusion | flops 47018803200 | bytes 87818240 | tf_op jit(solution)/dot_general | solution.py:12
  287.3 55.9 %fusion.11 = bf16[2560,7168]{1,0:T(8,128)(2,1)} fusion(bf16[2560,1280]{1,0:T(8,128)(2,1)} %get-tuple-element.4, bf16[7168,1280]{1,0:T(8,128)(2,1)} %param.4), kind=kOutput, calls=%fused_computation.21 | convolution fusion | flops 46976204800 | bytes 61603840 | tf_op jit(solution)/dot_general | solution.py:14
  343.1 76.3 %convolution_add_fusion = bf16[2560,7168]{1,0:T(8,128)(2,1)} fusion(bf16[2560,7168]{1,0:T(8,128)(2,1)} %fusion.11, bf16[7168,1280]{1,0:T(8,128)(2,1)} %param.5, f32[2560,1280]{1,0:T(8,128)} %get-tuple-element.5, bf16[2560,1280]{1,0:T(8,128)(2,1)} %param.3), kind=kOutput, calls=%fused_computation | convolution fusion | flops 47017492480 | bytes 111411200 | tf_op jit(solution)/dot_general | solution.py:14
  419.4 0.1 reduce-scatter.4.cloned.1.call-update
  419.5 11.8 %all-gather.13.cloned.1.call-done = bf16[2560,7168]{1,0:T(8,128)(2,1)} async-done(((bf16[160,7168]{1,0:T(8,128)(2,1)}), bf16[2560,7168]{1,0:T(8,128)(2,1)}) %all-gather.13.cloned.1.call-update) | async-done | bytes 36700176 | tf_op jit(solution)/reshape | solution.py:18
  431.2 66.0 %fusion.1 = bf16[7168,1280]{0,1:T(8,128)(2,1)} fusion(bf16[2560,7168]{1,0:T(8,128)(2,1)} %all-gather.13.cloned.1.call-done, f32[2560,1280]{1,0:T(8,128)} %get-tuple-element.5, bf16[2560,1280]{1,0:T(8,128)(2,1)} %param.3), kind=kOutput, calls=%fused_computation.5 | convolution fusion | flops 47008317440 | bytes 74711040 | tf_op jit(solution)/gta,gtb->gab/dot_general | solution.py:19
  497.2 25.0 %copy.1 = bf16[7168,1280]{1,0:T(8,128)(2,1)} copy(bf16[7168,1280]{0,1:T(8,128)(2,1)} %fusion.1) | data formatting | bytes 36700160
  522.2 55.4 %fusion = bf16[7168,1280]{0,1:T(8,128)(2,1)} fusion(bf16[2560,1280]{1,0:T(8,128)(2,1)} %get-tuple-element.4, bf16[2560,7168]{1,0:T(8,128)(2,1)} %all-gather.13.cloned.1.call-done), kind=kOutput, calls=%fused_computation.4 | convolution fusion | flops 46985379840 | bytes 61603840 | tf_op jit(solution)/gta,gtb->gab/dot_general | solution.py:19
  577.6 25.0 %copy = bf16[7168,1280]{1,0:T(8,128)(2,1)} copy(bf16[7168,1280]{0,1:T(8,128)(2,1)} %fusion) | data formatting | bytes 36700160
  602.6 69.0 %convolution_convert_fusion = bf16[1280,7168]{1,0:T(8,128)(2,1)} fusion(bf16[2560,7168]{1,0:T(8,128)(2,1)} %all-gather.11.cloned.1.call-done, bf16[2560,1280]{1,0:T(8,128)(2,1)} %param.2, bf16[2560,1280]{1,0:T(8,128)(2,1)} %param.3), kind=kOutput, calls=%fused_computation.1 | convolution fusion | flops 47011594240 | bytes 68157440 | tf_op jit(solution)/gta,gtb->gab/dot_general | solution.py:19
  671.7 0.0 reduce-scatter.4.cloned.1.call-done
Async XLA Ops:
  7.2 214.4 %all-gather.11.cloned.1.call-start = ((), (), s32[]{:S(2)}) async-start(), calls=%async_computation.1 | async-start | bytes 38993920 | tf_op args[1]
  8.0 423.2 %all-gather.13.cloned.1.call-start = ((), (), s32[]{:S(2)}) async-start(), calls=%async_computation.2 | async-start | bytes 38993920 | tf_op jit(solution)/reshape | solution.py:18
  8.8 662.9 %reduce-scatter.4.cloned.1.call-start = ((), (), s32[]{:S(2)}) async-start(), calls=%async_computation.3 | async-start | bytes 38993920
Sparse Core Ops, SparseCore 0:
  10.0 211.5 all-gather.10
  223.6 207.5 all-gather.12
  435.2 204.8 reduce-scatter.3
where the time goes:
time: 686 us; the launch traced here: 679 us
  matrix products  388 us (57%)
  waiting for transfers between devices  226 us (33%)
  local copies, waits for them, and re-layouts  50 us (7%)
  between operations  14.3 us (2%)
    unnamed x5, waiting for transfers between devices  214 us
    dot_general x3, matrix products, by_group(): jnp.einsum('gta,gtb->gab', a, b, preferred_element_type=jnp.float32)  190 us
    dot_general x2, matrix products, step(): dx = jnp.dot(d_gate, w_gate.T) + jnp.dot(d_up, w_up.T)  132 us
    dot_general x1, matrix products, step(): d_hidden = jnp.dot(dy, w_down.T, preferred_element_type=jnp.float32)  65.6 us
    unnamed x2, local copies, waits for them, and re-layouts  50 us
  transfers between devices with their start and end apart: 3, of which 2 were waited for; matrix products, arithmetic and copies ran while one was open for 65% of the time, Pallas kernels for 0%

commit v1 on v0

v1 whole, which is shorter than its diff:
```python
import functools
import math

import jax
import jax.numpy as jnp
from jax import lax
from jax.experimental import pallas as pl
from jax.experimental.pallas import tpu as pltpu
from jax.sharding import PartitionSpec as P

MESH = pl.DeviceIdType.MESH
LINKS = ((0, 1), (0, -1), (1, 1), (1, -1))
TICKS = 3
FIRST = 3


def tile_of(size, want):
    return want if size % want == 0 else size


def gather_kernel(
    side, dt, nt,
    x_ref, dy_ref, gate_ref, up_ref, wg_ref, wu_ref, wd_ref,
    full_ref, dgu_ref, hid_ref, dxp_ref,
    wd_v, dy_v, g_v, u_v, dg_v, du_v, h_v, wg_t, wu_t, out_t,
    send_sem, recv_sem, wd_sem, in_sem, res_sem, w_sem, out_sem,
):
    rows, d = dy_ref.shape
    ff = gate_ref.shape[1]
    half, cols = rows // 2, d // 2
    ring = side - 1
    slots = side * side - 1
    me = lax.axis_index("tp")
    at = (me // side, me % side)

    def owner(da, db):
        return lax.rem(at[0] + da + 2 * side, side) * side + lax.rem(at[1] + db + 2 * side, side)

    def on_link(link, along, across):
        axis, sign = link
        steps = (sign * along, sign * across)
        return owner(*(steps if axis == 0 else steps[::-1]))

    def unit(link, slot, back):
        array, s = slot // slots, slot % slots
        early = s < 2 * ring
        late = jnp.maximum(s - 2 * ring, 0)
        hop = jnp.where(early, s // 2, late // ring) + 1
        across = jnp.where(early, 0, late % ring + 1)
        second = jnp.where(early, s % 2, 1)
        who = on_link(link, back - hop, -across)
        axis, sign = link
        col = second if axis == 0 else 1 - second
        row = pl.multiple_of(who * rows + (0 if sign == 1 else half), 8)
        return full_ref.at[array, pl.ds(row, half), pl.ds(pl.multiple_of(col * cols, 128), cols)]

    def copy(k, slot, src, dst):
        axis, sign = LINKS[k]
        return pltpu.make_async_remote_copy(
            src_ref=src,
            dst_ref=dst,
            send_sem=send_sem.at[k, slot],
            recv_sem=recv_sem.at[k, slot],
            device_id={"tp": on_link(LINKS[k], 1, 0)},
            device_id_type=MESH,
        )

    def send(slot):
        for k, link in enumerate(LINKS):
            part = unit(link, slot, 1)
            copy(k, slot, part, part).start()

    def arrive(slot):
        for k, link in enumerate(LINKS):
            part = unit(link, slot, 0)
            copy(k, slot, part, part).wait_recv()

    def step(slot):
        arrive(slot)

        @pl.when(slot + 2 < 2 * slots)
        def _():
            send(slot + 2)

    barrier = pltpu.get_barrier_semaphore()
    for link in LINKS:
        pl.semaphore_signal(barrier, inc=1, device_id={"tp": on_link(link, 1, 0)}, device_id_type=MESH)
    pl.semaphore_wait(barrier, len(LINKS))

    for slot in range(2):
        for k, (axis, sign) in enumerate(LINKS):
            col = slot if axis == 0 else 1 - slot
            r = 0 if sign == 1 else half
            part = (pl.ds(r, half), pl.ds(col * cols, cols))
            row = pl.multiple_of(me * rows + r, 8)
            copy(k, slot, dy_ref.at[part], full_ref.at[0, pl.ds(row, half), part[1]]).start()

    wd_copy = pltpu.make_async_copy(wd_ref, wd_v, wd_sem)
    wd_copy.start()

    mine = pl.ds(pl.multiple_of(me * rows, 8), rows)
    own = [dy_v.at[pl.ds(i * rows, rows)] for i in range(2)]
    loads = [pltpu.make_async_copy(ref, own[i], in_sem.at[0, i]) for i, ref in enumerate((dy_ref, x_ref))]
    stores = [pltpu.make_async_copy(own[i], full_ref.at[i, mine], in_sem.at[1, i]) for i in range(2)]
    for load in loads:
        load.start()
    for load, store in zip(loads, stores):
        load.wait()
        store.start()
    for store in stores:
        store.wait()

    tiles = d // dt

    def weights(i, slot):
        part = pl.ds(pl.multiple_of(i * dt, dt), dt)
        return [
            pltpu.make_async_copy(ref.at[part], buf.at[slot], w_sem.at[j, slot])
            for j, (ref, buf) in enumerate(((wg_ref, wg_t), (wu_ref, wu_t)))
        ]

    for c in weights(0, 0):
        c.start()
    lax.fori_loop(0, FIRST, lambda s, _: (step(s), None)[1], None)
    wd_copy.wait()

    groups = side * side // 2

    def group(g, _):
        starts = []
        for i in range(2):
            e = 2 * g + i
            a, b = e % side, e // side
            starts += [owner(-a, -b) * rows, owner(a, b) * rows + half]
        starts = [pl.multiple_of(s, 8) for s in starts]
        local = [pl.ds(i * half, half) for i in range(4)]
        there = [pl.ds(s, half) for s in starts]

        step(FIRST + TICKS * g)
        reads = [
            pltpu.make_async_copy(ref.at[t], buf.at[h], in_sem.at[j, i])
            for j, (ref, buf) in enumerate(((full_ref.at[0], dy_v), (gate_ref, g_v), (up_ref, u_v)))
            for i, (t, h) in enumerate(zip(there, local))
        ]
        for c in reads:
            c.start()
        for c in reads:
            c.wait()

        def hidden_tile(i, _):
            n = pl.ds(pl.multiple_of(i * nt, nt), nt)
            d_hidden = lax.dot_general(
                dy_v[...], wd_v[n, :], (((1,), (1,)), ((), ())), preferred_element_type=jnp.float32
            )
            gate, up = g_v[:, n].astype(jnp.float32), u_v[:, n].astype(jnp.float32)
            s = jax.nn.sigmoid(gate)
            silu = gate * s
            d_silu = d_hidden * up
            dg_v[:, n] = (d_silu * s + d_silu * gate * (s * (1 - s))).astype(dg_v.dtype)
            du_v[:, n] = (d_hidden * silu).astype(du_v.dtype)
            h_v[:, n] = (silu * up).astype(h_v.dtype)

        lax.fori_loop(0, ff // nt, hidden_tile, None)
        results = [
            pltpu.make_async_copy(buf.at[h], ref.at[t, c], res_sem.at[j, i])
            for j, (buf, ref, c) in enumerate((
                (dg_v, dgu_ref, pl.ds(0, ff)), (du_v, dgu_ref, pl.ds(ff, ff)), (h_v, hid_ref, pl.ds(0, ff)),
            ))
            for i, (t, h) in enumerate(zip(there, local))
        ]
        for c in results:
            c.start()

        def stores_of(i, slot):
            n = pl.ds(pl.multiple_of(i * dt, dt), dt)
            return [
                pltpu.make_async_copy(out_t.at[slot, h], dxp_ref.at[t, n], out_sem.at[slot, j])
                for j, (t, h) in enumerate(zip(there, local))
            ]

        def dx_tile(i, _):
            slot = i % 2
            for c in weights(i, slot):
                c.wait()

            @pl.when((i + 1 < tiles) | (g + 1 < groups))
            def _():
                for c in weights((i + 1) % tiles, (i + 1) % 2):
                    c.start()

            @pl.when(i >= 2)
            def _():
                for c in stores_of(i - 2, slot):
                    c.wait()

            nt_dims = (((1,), (1,)), ((), ()))
            term = lax.dot_general(dg_v[...], wg_t[slot], nt_dims, preferred_element_type=jnp.float32)
            term += lax.dot_general(du_v[...], wu_t[slot], nt_dims, preferred_element_type=jnp.float32)
            out_t[slot] = term.astype(out_t.dtype)
            for c in stores_of(i, slot):
                c.start()

        cut = (tiles // 2, tiles)
        step(FIRST + TICKS * g + 1)
        lax.fori_loop(0, cut[0], dx_tile, None)
        step(FIRST + TICKS * g + 2)
        lax.fori_loop(cut[0], cut[1], dx_tile, None)
        for i in (tiles - 2, tiles - 1):
            for c in stores_of(i, i % 2):
                c.wait()
        for c in results:
            c.wait()

    lax.fori_loop(0, groups, group, None)
    lax.fori_loop(FIRST + TICKS * groups, 2 * slots, lambda s, _: (step(s), None)[1], None)

    def sent(slot, _):
        for k, link in enumerate(LINKS):
            part = unit(link, slot, 1)
            copy(k, slot, part, part).wait_send()

    lax.fori_loop(0, 2 * slots, sent, None)


def gather(side, x, dy, gate, up, wg, wu, wd):
    rows, d = dy.shape
    tokens, ff = gate.shape
    n = side * side
    group = 2 * rows
    dt, nt = tile_of(d, 512), tile_of(ff, 256)
    bf16 = jnp.bfloat16
    flops = 6 * tokens * d * ff
    anywhere = pl.BlockSpec(memory_space=pl.ANY)
    return pl.pallas_call(
        functools.partial(gather_kernel, side, dt, nt),
        out_shape=(
            jax.ShapeDtypeStruct((2, tokens, d), bf16),
            jax.ShapeDtypeStruct((tokens, 2 * ff), bf16),
            jax.ShapeDtypeStruct((tokens, ff), bf16),
            jax.ShapeDtypeStruct((tokens, d), bf16),
        ),
        in_specs=[anywhere] * 7,
        out_specs=(anywhere,) * 4,
        scratch_shapes=[
            pltpu.VMEM((ff, d), bf16),
            pltpu.VMEM((group, d), bf16),
            *[pltpu.VMEM((group, ff), bf16)] * 5,
            *[pltpu.VMEM((2, dt, ff), bf16)] * 2,
            pltpu.VMEM((2, group, dt), bf16),
            pltpu.SemaphoreType.DMA((len(LINKS), 2 * (n - 1))),
            pltpu.SemaphoreType.DMA((len(LINKS), 2 * (n - 1))),
            pltpu.SemaphoreType.DMA,
            pltpu.SemaphoreType.DMA((3, 4)),
            pltpu.SemaphoreType.DMA((3, 4)),
            pltpu.SemaphoreType.DMA((2, 2)),
            pltpu.SemaphoreType.DMA((2, 4)),
        ],
        compiler_params=pltpu.CompilerParams(
            collective_id=0, has_side_effects=True, vmem_limit_bytes=60 * 1024 * 1024
        ),
        cost_estimate=pl.CostEstimate(
            flops=flops, bytes_accessed=2 * (8 * 2 * d * ff + 6 * tokens * d), transcendentals=tokens * ff
        ),
        name="gather_and_dx",
    )(x, dy, gate, up, wg, wu, wd)


def dw_in_kernel(x_ref, d_ref, dwg_ref, dwu_ref):
    ff = dwg_ref.shape[1]
    dw = lax.dot_general(
        x_ref[...], d_ref[...], (((0,), (0,)), ((), ())), preferred_element_type=jnp.float32
    )
    dwg_ref[...] = dw[:, :ff].astype(dwg_ref.dtype)
    dwu_ref[...] = dw[:, ff:].astype(dwu_ref.dtype)


def dw_in(full, dgu):
    _, tokens, d = full.shape
    ff = dgu.shape[1] // 2
    bd = tile_of(d, 256)
    out = jax.ShapeDtypeStruct((d, ff), full.dtype)
    return pl.pallas_call(
        dw_in_kernel,
        grid=(d // bd,),
        out_shape=(out, out),
        in_specs=[
            pl.BlockSpec((pl.squeezed, tokens, bd), lambda i: (1, 0, i)),
            pl.BlockSpec((tokens, 2 * ff), lambda i: (0, 0), pipeline_mode=pl.Buffered(1)),
        ],
        out_specs=[pl.BlockSpec((bd, ff), lambda i: (i, 0))] * 2,
        compiler_params=pltpu.CompilerParams(vmem_limit_bytes=60 * 1024 * 1024),
        cost_estimate=pl.CostEstimate(
            flops=4 * tokens * d * ff, bytes_accessed=2 * (tokens * d + 2 * ff * (tokens + d)), transcendentals=0
        ),
        name="dw_in",
    )(full, dgu)


def dw_out_kernel(h_ref, dy_ref, dw_ref, ht):
    @pl.when(pl.program_id(0) == 0)
    def _():
        ht[...] = h_ref[...].T

    dw = jnp.dot(ht[...], dy_ref[...], preferred_element_type=jnp.float32)
    dw_ref[...] = dw.astype(dw_ref.dtype)


def dw_out(full, hidden):
    _, tokens, d = full.shape
    ff = hidden.shape[1]
    bd = tile_of(d, 512)
    return pl.pallas_call(
        dw_out_kernel,
        grid=(d // bd,),
        out_shape=jax.ShapeDtypeStruct((ff, d), full.dtype),
        in_specs=[
            pl.BlockSpec((tokens, ff), lambda i: (0, 0), pipeline_mode=pl.Buffered(1)),
            pl.BlockSpec((pl.squeezed, tokens, bd), lambda i: (0, 0, i)),
        ],
        out_specs=pl.BlockSpec((ff, bd), lambda i: (0, i)),
        scratch_shapes=[pltpu.VMEM((ff, tokens), full.dtype)],
        compiler_params=pltpu.CompilerParams(vmem_limit_bytes=60 * 1024 * 1024),
        cost_estimate=pl.CostEstimate(
            flops=2 * tokens * d * ff, bytes_accessed=2 * (tokens * d + ff * (tokens + d)), transcendentals=0
        ),
        name="dw_out",
    )(hidden, full)


def solution(mesh):
    side = math.isqrt(mesh.shape["tp"])

    def device_step(x, dy, gate, up, w_gate, w_up, w_down):
        full, dgu, hidden, dx_terms = gather(side, x, dy, gate, up, w_gate, w_up, w_down)
        dx = lax.psum_scatter(dx_terms, "tp", scatter_dimension=0, tiled=True)
        dw_gate, dw_up = dw_in(full, dgu)
        dw_down = dw_out(full, hidden)
        return dx, dw_gate, dw_up, dw_down

    rows, both, cols = P(("dp", "tp"), None), P("dp", "tp"), P(None, "tp")
    return jax.shard_map(
        device_step,
        mesh=mesh,
        in_specs=(rows, rows, both, both, cols, cols, P("tp", None)),
        out_specs=(rows, both, both, rows),
        check_vma=False,
    )
```

time: 686 us -> 603 us (0.88)
  Pallas kernels: 0 us -> 543 us
  matrix products: 388 us -> 0 us
  waiting for transfers between devices: 226 us -> 41.6 us
  local copies, waits for them, and re-layouts: 50 us -> 0 us
    pallas_call x0 -> x3, Pallas kernels: none -> 543 us  [the longest x1 380 us: gather(): pl.pallas_call(functools.partial(gather_kernel, side, dt, nt), out_shape=...]
    dot_general x6 -> x0, matrix products: 388 us -> none  [the longest x3 190 us: by_group(): jnp.einsum('gta,gtb->gab', a, b, preferred_element_type=jnp.float32)]
    unnamed x5 -> x1, waiting for transfers between devices: 214 us -> 0.05 us
    unnamed x2 -> x0, local copies, waits for them, and re-layouts: 50 us -> none
    reduce_scatter x0 -> x1, waiting for transfers between devices: none -> 41.6 us  [device_step(): dx = lax.psum_scatter(dx_terms, 'tp', scatter_dimension=0, tiled=True)]
    reshape x1 -> x0, waiting for transfers between devices: 11.8 us -> none  [by_group(): a, b = (t.reshape(groups, -1, t.shape[-1]) for t in (a, b))]
  transfers between devices with their start and end apart: 3 -> 1, of which waited for: 2 -> 1; matrix products, arithmetic and copies ran while one was open for 65% -> 0% of each run, Pallas kernels for 0% -> 27%
where the time goes in v1:
time: 603 us; the launch traced here: 599 us
  Pallas kernels  543 us (90%)
  waiting for transfers between devices  41.6 us (7%)
  between operations  14.1 us (2%)
    pallas_call x1, Pallas kernels, gather(): pl.pallas_call(functools.partial(gather_kernel, side, dt, nt), out_shape=...  380 us
    pallas_call x1, Pallas kernels, dw_in(): pl.pallas_call(dw_in_kernel, grid=(d // bd,), out_shape=(out, out), in_sp...  107 us
    pallas_call x1, Pallas kernels, dw_out(): pl.pallas_call(dw_out_kernel, grid=(d // bd,), out_shape=jax.ShapeDtypeSt...  56.5 us
    reduce_scatter x1, waiting for transfers between devices, device_step(): dx = lax.psum_scatter(dx_terms, 'tp', scatter_dimension=0, tiled=True)  41.6 us
  transfers between devices with their start and end apart: 1, of which 1 were waited for; matrix products, arithmetic and copies ran while one was open for 0% of the time, Pallas kernels for 27%

profile of v1, /device:TPU:97, one launch (start us, length us, event | category | flops | bytes accessed | tf_op | source)
XLA Modules:
  0.0 599.0 jit_solution(14355034826222060945)
XLA Ops:
  7.2 0.1 reduce-scatter.2.cloned.1.call-start
  7.2 380.1 %gather_and_dx.1 = (bf16[2,2560,7168]{2,1,0:T(8,128)(2,1)}, bf16[2560,2560]{1,0:T(8,128)(2,1)}, bf16[2560,1280]{1,0:T(8,128)(2,1)}, bf16[2560,7168]{1,0:T(8,128)(2,1)}) custom-call(bf16[160,7168]{1,0:T(8,128)(2,1)} %x_ref.1, bf16[160,7168]{1,0:T(8,128)(2,1)} %dy_ref.1, bf16[2560,1280]{1,0:T(8,128)(2,1)} %gate_ref.1, bf16[2560,1280]{1,0:T(8,128)(2,1)} %up_ref.1, ...), custom_call_target="tpu_custom_call" | custom-call | flops 140928614400 | bytes 513802240 | tf_op jit(solution)/shard_map/gather_and_dx/pallas_call | solution.py:234
  387.3 0.1 reduce-scatter.2.cloned.1.call-update
  387.4 56.5 %dw_out.1 = bf16[1280,7168]{1,0:T(8,128)(2,1)} custom-call(bf16[2560,1280]{1,0:T(8,128)(2,1)} %get-tuple-element.15.h_ref, bf16[2,2560,7168]{2,1,0:T(8,128)(2,1)} %get-tuple-element.11.x_ref.dy_ref), custom_call_target="tpu_custom_call" | custom-call | flops 46976204800 | bytes 61603840 | tf_op jit(solution)/shard_map/dw_out/pallas_call | solution.py:312
  443.9 106.7 %dw_in.1 = (bf16[7168,1280]{1,0:T(8,128)(2,1)}, bf16[7168,1280]{1,0:T(8,128)(2,1)}) custom-call(bf16[2,2560,7168]{2,1,0:T(8,128)(2,1)} %get-tuple-element.11.x_ref.dy_ref, bf16[2560,2560]{1,0:T(8,128)(2,1)} %get-tuple-element.12.d_ref), custom_call_target="tpu_custom_call" | custom-call | flops 93952409600 | bytes 86507520 | tf_op jit(solution)/shard_map/dw_in/pallas_call | solution.py:282
  550.6 41.6 %reduce-scatter.2.cloned.1.call-done = bf16[160,7168]{1,0:T(8,128)(2,1)} async-done(((bf16[2560,7168]{1,0:T(8,128)(2,1)}), bf16[160,7168]{1,0:T(8,128)(2,1)}) %reduce-scatter.2.cloned.1.call-update) | async-done | bytes 2293776 | tf_op jit(solution)/shard_map/reduce_scatter | solution.py:335
Async XLA Ops:
  7.2 585.0 %reduce-scatter.2.cloned.1.call-start = ((), (), s32[]{:S(2)}) async-start(), calls=%async_computation.1 | async-start | bytes 38993920 | tf_op jit(solution)/shard_map/reduce_scatter | solution.py:335
Sparse Core Ops, SparseCore 0:
  387.5 204.6 reduce-scatter.1

commit v2 on v1

--- a/solution.py
+++ b/solution.py
@@ -21,10 +21,13 @@
 def gather_kernel(
     side, dt, nt,
     x_ref, dy_ref, gate_ref, up_ref, wg_ref, wu_ref, wd_ref,
-    full_ref, dgu_ref, hid_ref, dxp_ref,
+    full_ref, dgu_ref, hid_ref, *rest,
+):
+    terms, scratch = rest[: 4 * side], rest[4 * side :]
+    (
     wd_v, dy_v, g_v, u_v, dg_v, du_v, h_v, wg_t, wu_t, out_t,
     send_sem, recv_sem, wd_sem, in_sem, res_sem, w_sem, out_sem,
-):
+    ) = scratch
     rows, d = dy_ref.shape
     ff = gate_ref.shape[1]
     half, cols = rows // 2, d // 2
@@ -111,6 +114,7 @@
         store.wait()
 
     tiles = d // dt
+    cut = tiles // 2
 
     def weights(i, slot):
         part = pl.ds(pl.multiple_of(i * dt, dt), dt)
@@ -124,19 +128,16 @@
     lax.fori_loop(0, FIRST, lambda s, _: (step(s), None)[1], None)
     wd_copy.wait()
 
-    groups = side * side // 2
-
-    def group(g, _):
+    def group(q, p):
+        offsets = [2 * p, 2 * p + 1]
         starts = []
-        for i in range(2):
-            e = 2 * g + i
-            a, b = e % side, e // side
-            starts += [owner(-a, -b) * rows, owner(a, b) * rows + half]
-        starts = [pl.multiple_of(s, 8) for s in starts]
+        for a in offsets:
+            starts += [owner(-a, -q) * rows, owner(a, q) * rows + half]
         local = [pl.ds(i * half, half) for i in range(4)]
-        there = [pl.ds(s, half) for s in starts]
-
-        step(FIRST + TICKS * g)
+        there = [pl.ds(pl.multiple_of(s, 8), half) for s in starts]
+        first = FIRST + TICKS * (q * (side // 2) + p)
+
+        step(first)
         reads = [
             pltpu.make_async_copy(ref.at[t], buf.at[h], in_sem.at[j, i])
             for j, (ref, buf) in enumerate(((full_ref.at[0], dy_v), (gate_ref, g_v), (up_ref, u_v)))
@@ -171,48 +172,73 @@
         for c in results:
             c.start()
 
-        def stores_of(i, slot):
-            n = pl.ds(pl.multiple_of(i * dt, dt), dt)
-            return [
-                pltpu.make_async_copy(out_t.at[slot, h], dxp_ref.at[t, n], out_sem.at[slot, j])
-                for j, (t, h) in enumerate(zip(there, local))
-            ]
-
-        def dx_tile(i, _):
-            slot = i % 2
-            for c in weights(i, slot):
-                c.wait()
-
-            @pl.when((i + 1 < tiles) | (g + 1 < groups))
-            def _():
-                for c in weights((i + 1) % tiles, (i + 1) % 2):
-                    c.start()
-
-            @pl.when(i >= 2)
-            def _():
-                for c in stores_of(i - 2, slot):
+        def stores_of(i, slot, second, b):
+            n = pl.ds(pl.multiple_of((i - second * cut) * dt, dt), dt)
+            copies = []
+            for j, a in enumerate(offsets):
+                for r in range(2):
+                    da, db = ((-a) % side, (side - b) % side) if r == 0 else (a, b)
+                    key, at_ = (2 * side + 2 * db + r, da) if second else (2 * da + r, db)
+                    k = 2 * j + r
+                    copies.append(pltpu.make_async_copy(
+                        out_t.at[slot, local[k]], terms[key].at[at_, :, n], out_sem.at[slot, k]
+                    ))
+            return copies
+
+        def for_stores(i, slot, second, act):
+            if not second:
+                for c in stores_of(i, slot, second, q):
+                    act(c)
+                return
+            for b in range(side):
+
+                @pl.when(q == b)
+                def _():
+                    for c in stores_of(i, slot, second, b):
+                        act(c)
+
+        def dx_tile(second):
+            begin = cut if second else 0
+
+            def body(i, _):
+                slot = i % 2
+                for c in weights(i, slot):
                     c.wait()
 
-            nt_dims = (((1,), (1,)), ((), ()))
-            term = lax.dot_general(dg_v[...], wg_t[slot], nt_dims, preferred_element_type=jnp.float32)
-            term += lax.dot_general(du_v[...], wu_t[slot], nt_dims, preferred_element_type=jnp.float32)
-            out_t[slot] = term.astype(out_t.dtype)
-            for c in stores_of(i, slot):
-                c.start()
-
-        cut = (tiles // 2, tiles)
-        step(FIRST + TICKS * g + 1)
-        lax.fori_loop(0, cut[0], dx_tile, None)
-        step(FIRST + TICKS * g + 2)
-        lax.fori_loop(cut[0], cut[1], dx_tile, None)
-        for i in (tiles - 2, tiles - 1):
-            for c in stores_of(i, i % 2):
-                c.wait()
+                @pl.when((i + 1 < tiles) | (q + 1 < side) | (p + 1 < side // 2))
+                def _():
+                    for c in weights((i + 1) % tiles, (i + 1) % 2):
+                        c.start()
+
+                @pl.when(i >= begin + 2)
+                def _():
+                    for_stores(i - 2, slot, second, lambda c: c.wait())
+
+                nt_dims = (((1,), (1,)), ((), ()))
+                term = lax.dot_general(dg_v[...], wg_t[slot], nt_dims, preferred_element_type=jnp.float32)
+                term += lax.dot_general(du_v[...], wu_t[slot], nt_dims, preferred_element_type=jnp.float32)
+                out_t[slot] = term.astype(out_t.dtype)
+                for_stores(i, slot, second, lambda c: c.start())
+
+            end = tiles if second else cut
+            lax.fori_loop(begin, end, body, None)
+            for i in range(max(begin, end - 2), end):
+                for_stores(i, i % 2, second, lambda c: c.wait())
+
+        step(first + 1)
+        dx_tile(False)
+        step(first + 2)
+        dx_tile(True)
         for c in results:
             c.wait()
 
-    lax.fori_loop(0, groups, group, None)
-    lax.fori_loop(FIRST + TICKS * groups, 2 * slots, lambda s, _: (step(s), None)[1], None)
+    def groups(q, _):
+        for p in range(side // 2):
+            group(q, p)
+
+    lax.fori_loop(0, side, groups, None)
+    done = FIRST + TICKS * side * (side // 2)
+    lax.fori_loop(done, 2 * slots, lambda s, _: (step(s), None)[1], None)
 
     def sent(slot, _):
         for k, link in enumerate(LINKS):
@@ -227,7 +253,7 @@
     tokens, ff = gate.shape
     n = side * side
     group = 2 * rows
-    dt, nt = tile_of(d, 512), tile_of(ff, 256)
+    dt, nt = tile_of(d // 2, 512), tile_of(ff, 256)
     bf16 = jnp.bfloat16
     flops = 6 * tokens * d * ff
     anywhere = pl.BlockSpec(memory_space=pl.ANY)
@@ -237,10 +263,10 @@
             jax.ShapeDtypeStruct((2, tokens, d), bf16),
             jax.ShapeDtypeStruct((tokens, 2 * ff), bf16),
             jax.ShapeDtypeStruct((tokens, ff), bf16),
-            jax.ShapeDtypeStruct((tokens, d), bf16),
+            *[jax.ShapeDtypeStruct((side, rows // 2, d // 2), bf16)] * (4 * side),
         ),
         in_specs=[anywhere] * 7,
-        out_specs=(anywhere,) * 4,
+        out_specs=(anywhere,) * (3 + 4 * side),
         scratch_shapes=[
             pltpu.VMEM((ff, d), bf16),
             pltpu.VMEM((group, d), bf16),
@@ -265,7 +291,9 @@
     )(x, dy, gate, up, wg, wu, wd)
 
 
-def dw_in_kernel(x_ref, d_ref, dwg_ref, dwu_ref):
+def dw_in_kernel(after, *refs):
+    x_ref, d_ref = refs[:2]
+    dwg_ref, dwu_ref = refs[-2:]
     ff = dwg_ref.shape[1]
     dw = lax.dot_general(
         x_ref[...], d_ref[...], (((0,), (0,)), ((), ())), preferred_element_type=jnp.float32
@@ -274,26 +302,30 @@
     dwu_ref[...] = dw[:, ff:].astype(dwu_ref.dtype)
 
 
-def dw_in(full, dgu):
+def dw_in(full, dgu, first, last, so_far=(), after=()):
     _, tokens, d = full.shape
     ff = dgu.shape[1] // 2
     bd = tile_of(d, 256)
     out = jax.ShapeDtypeStruct((d, ff), full.dtype)
+    anywhere = pl.BlockSpec(memory_space=pl.ANY)
+    n = last - first
     return pl.pallas_call(
-        dw_in_kernel,
-        grid=(d // bd,),
+        functools.partial(dw_in_kernel, len(after)),
+        grid=(n,),
         out_shape=(out, out),
         in_specs=[
-            pl.BlockSpec((pl.squeezed, tokens, bd), lambda i: (1, 0, i)),
+            pl.BlockSpec((pl.squeezed, tokens, bd), lambda i: (1, 0, i + first)),
             pl.BlockSpec((tokens, 2 * ff), lambda i: (0, 0), pipeline_mode=pl.Buffered(1)),
+            *[anywhere] * (len(so_far) + len(after)),
         ],
-        out_specs=[pl.BlockSpec((bd, ff), lambda i: (i, 0))] * 2,
+        out_specs=[pl.BlockSpec((bd, ff), lambda i: (i + first, 0))] * 2,
+        input_output_aliases={2 + i: i for i in range(len(so_far))},
         compiler_params=pltpu.CompilerParams(vmem_limit_bytes=60 * 1024 * 1024),
         cost_estimate=pl.CostEstimate(
-            flops=4 * tokens * d * ff, bytes_accessed=2 * (tokens * d + 2 * ff * (tokens + d)), transcendentals=0
+            flops=4 * tokens * n * bd * ff, bytes_accessed=2 * (tokens * n * bd + 2 * ff * (tokens + n * bd)), transcendentals=0
         ),
         name="dw_in",
-    )(full, dgu)
+    )(full, dgu, *so_far, *after)
 
 
 def dw_out_kernel(h_ref, dy_ref, dw_ref, ht):
@@ -327,15 +359,106 @@
     )(hidden, full)
 
 
+def f32(v):
+    return v.astype(jnp.float32)
+
+
+def bf16(v):
+    return v.astype(jnp.bfloat16)
+
+
+def exchange(hop, t, one, two):
+    far = [hop(t[2][0], one, 1), hop(t[2][1], one, -1)]
+    raw = [hop(t[1][1], one, 1), hop(t[3][0], one, -1)]
+    near = [bf16(f32(t[1][0]) + f32(far[0])), bf16(f32(t[3][1]) + f32(far[1]))]
+    yield near
+    near = [hop(near[0], one, 1), hop(near[1], one, -1)]
+    plus, minus = [near[0], raw[0]], [raw[1], near[1]]
+
+    def piece(j, r):
+        return f32(t[0][r][j]) + f32(plus[r][j]) + f32(minus[r][j])
+
+    far = [bf16(piece(2, 0)), bf16(piece(2, 1))]
+    raw = [bf16(piece(1, 1)), bf16(piece(3, 0))]
+    yield [*far, *raw]
+    far = [hop(far[0], two, 1), hop(far[1], two, -1)]
+    raw = [hop(raw[0], two, 1), hop(raw[1], two, -1)]
+    near = [bf16(piece(1, 0) + f32(far[0])), bf16(piece(3, 1) + f32(far[1]))]
+    yield near
+    near = [hop(near[0], two, 1), hop(near[1], two, -1)]
+    last_plus, last_minus = [near[0], raw[0]], [raw[1], near[1]]
+    yield [(t[0][r], plus[r], minus[r], last_plus[r], last_minus[r]) for r in range(2)]
+
+
+def total_kernel(chunks, *refs):
+    *ins, out_ref = refs
+    half = ins[0].shape[0]
+    for h in range(2):
+
+        @pl.when(pl.program_id(0) // chunks == h)
+        def _():
+            for r in range(2):
+                parts = ins[10 * h + 5 * r :][:5]
+                total = f32(parts[0][...])
+                for part in parts[1:]:
+                    total += f32(part[...])
+                out_ref[r * half : (r + 1) * half, :] = bf16(total)
+
+
+def total(halves):
+    half, cols = halves[0][0][-1].shape
+    chunk = tile_of(cols, 896)
+    chunks = cols // chunk
+    specs, args = [], []
+    for h, parts in enumerate(halves):
+        col = (lambda i: jnp.minimum(i, chunks - 1)) if h == 0 else (lambda i: jnp.maximum(i - chunks, 0))
+        for r in range(2):
+            for v in parts[r]:
+                args.append(v)
+                if v.ndim == 3:
+                    specs.append(pl.BlockSpec((pl.squeezed, half, chunk), lambda i, col=col: (0, 0, col(i))))
+                else:
+                    specs.append(pl.BlockSpec((half, chunk), lambda i, col=col: (0, col(i))))
+    return pl.pallas_call(
+        functools.partial(total_kernel, chunks),
+        grid=(2 * chunks,),
+        out_shape=jax.ShapeDtypeStruct((2 * half, 2 * cols), jnp.bfloat16),
+        in_specs=specs,
+        out_specs=pl.BlockSpec((2 * half, chunk), lambda i: (0, i)),
+        cost_estimate=pl.CostEstimate(flops=16 * half * cols, bytes_accessed=48 * half * cols, transcendentals=0),
+        compiler_params=pltpu.CompilerParams(vmem_limit_bytes=60 * 1024 * 1024),
+        name="dx_total",
+    )(*args)
+
+
 def solution(mesh):
     side = math.isqrt(mesh.shape["tp"])
 
+    def hop(v, axis, sign):
+        pairs = []
+        for i in range(side * side):
+            at = [i // side, i % side]
+            at[axis] = (at[axis] + sign) % side
+            pairs.append((i, at[0] * side + at[1]))
+        return lax.ppermute(v, "tp", pairs)
+
     def device_step(x, dy, gate, up, w_gate, w_up, w_down):
-        full, dgu, hidden, dx_terms = gather(side, x, dy, gate, up, w_gate, w_up, w_down)
-        dx = lax.psum_scatter(dx_terms, "tp", scatter_dimension=0, tiled=True)
-        dw_gate, dw_up = dw_in(full, dgu)
+        full, dgu, hidden, *terms = gather(side, x, dy, gate, up, w_gate, w_up, w_down)
+        blocks = x.shape[1] // tile_of(x.shape[1], 256)
+        cuts = [0, blocks * 5 // 7, blocks * 6 // 7, blocks]
+        halves = [
+            exchange(hop, [terms[4 * side // 2 * h + 2 * k :][:2] for k in range(side)], h, 1 - h)
+            for h in range(2)
+        ]
         dw_down = dw_out(full, hidden)
-        return dx, dw_gate, dw_up, dw_down
+        near = [next(e) for e in halves]
+        dw = dw_in(full, dgu, cuts[0], cuts[1], after=[v for n in near for v in n])
+        turn = [next(e) for e in halves]
+        dw = dw_in(full, dgu, cuts[1], cuts[2], dw, after=[v for n in turn for v in n])
+        near = [next(e) for e in halves]
+        dw = dw_in(full, dgu, cuts[2], cuts[3], dw, after=[v for n in near for v in n])
+        dx = total([next(e) for e in halves])
+        return dx, *dw, dw_down
 
     rows, both, cols = P(("dp", "tp"), None), P("dp", "tp"), P(None, "tp")
     return jax.shard_map(

time: 603 us -> 725 us (1.20)
  the two profiles are of different devices: /device:TPU:97 before, /device:TPU:96 now
where the time goes in v2:
time: 725 us; the launch traced here: 721 us
  Pallas kernels  563 us (78%)
  waiting for transfers between devices  85.6 us (12%)
  starting transfers between devices  35.1 us (5%)
  other arithmetic  32.3 us (4%)
    pallas_call x1, Pallas kernels, gather(): pl.pallas_call(functools.partial(gather_kernel, side, dt, nt), out_shape=...  380 us
    pallas_call x3, Pallas kernels, dw_in(): pl.pallas_call(functools.partial(dw_in_kernel, len(after)), grid=(n,), ou...  119 us
    ppermute x24, waiting for transfers between devices, hop(): return lax.ppermute(v, 'tp', pairs)  85.6 us
    pallas_call x1, Pallas kernels, dw_out(): pl.pallas_call(dw_out_kernel, grid=(d // bd,), out_shape=jax.ShapeDtypeSt...  56.5 us
    ppermute x24, starting transfers between devices, hop(): return lax.ppermute(v, 'tp', pairs)  35.1 us
    convert_element_type x12, other arithmetic, bf16(): return v.astype(jnp.bfloat16)  32.3 us
  transfers between devices with their start and end apart: 24, of which 4 were waited for; matrix products, arithmetic and copies ran while one was open for 4% of the time, Pallas kernels for 24%

profile of v2, /device:TPU:96, one launch (start us, length us, event | category | flops | bytes accessed | tf_op | source)
XLA Modules:
  0.0 721.1 jit_solution(14810027902108532556)
XLA Ops:
  0.6 379.5 %gather_and_dx.1 = (bf16[2,2560,7168]{2,1,0:T(8,128)(2,1)}, bf16[2560,2560]{1,0:T(8,128)(2,1)}, bf16[2560,1280]{1,0:T(8,128)(2,1)}, bf16[4,80,3584]{2,1,0:T(8,12...) custom-call(bf16[160,7168]{1,0:T(8,128)(2,1)} %x_ref.1, ...), custom_call_target="tpu_custom_call" | custom-call | flops 140928614400 | bytes 513802240 | tf_op jit(solution)/shard_map/gather_and_dx/pallas_call | solution.py:260
  380.3 3.1 collective-permute-start.2
  383.5 3.2 collective-permute-start.7
  386.7 56.5 %dw_out.1 = bf16[1280,7168]{1,0:T(8,128)(2,1)} custom-call(bf16[2560,1280]{1,0:T(8,128)(2,1)} %get-tuple-element.53.h_ref, bf16[2,2560,7168]{2,1,0:T(8,128)(2,1)} %get-tuple-element.45.refs_0_.dy_ref), custom_call_target="tpu_custom_call" | custom-call | flops 46976204800 | bytes 61603840 | tf_op jit(solution)/shard_map/dw_out/pallas_call | solution.py:344
  443.3 3.2 collective-permute-start.19
  446.5 4.4 add_convert_fusion.3.refs_2_
  450.9 30.1 %collective-permute-done.7 = bf16[4,80,3584]{2,1,0:T(8,128)(2,1)} collective-permute-done((bf16[4,80,3584]{2,1,0:T(8,128)(2,1)}, bf16[4,80,3584]{2,1,0:T(8,128)(2,1)}, u32[]{:S(2)}, u32[]{:S(2)}) %collective-permute-start.7) | collective-permute-done | bytes 2293792 | tf_op jit(solution)/shard_map/ppermute | solution.py:443
  482.2 3.8 add_convert_fusion.2.refs_3_
  487.3 3.7 add_convert_fusion.1.refs_4_
  491.0 6.0 collective-permute-done.19
  500.3 77.9 %dw_in.3 = (bf16[7168,1280]{1,0:T(8,128)(2,1)}, bf16[7168,1280]{1,0:T(8,128)(2,1)}) custom-call(bf16[2,2560,7168]{2,1,0:T(8,128)(2,1)} %get-tuple-element.45.refs_0_.dy_ref, bf16[2560,2560]{1,0:T(8,128)(2,1)} %get-tuple-element.46.refs_1_, bf16[4,80,3584]{2,1,0:T(8,128)(2,1)} %add_convert_fusion.3.refs_2_, bf16[4,80,3584]{2,1,0:T(8,128)(2,1)} %add_convert_fusion.2.refs_3_, ...), custom_call_target="tpu_custom_call" | custom-call | flops 67108864000 | bytes 65536000 | tf_op jit(solution)/shard_map/dw_in/pallas_call | solution.py:312
  578.8 3.1 collective-permute-start.20
  581.9 2.9 fusion.5
  584.9 3.1 fusion.7
  588.0 3.2 collective-permute-start.5
  591.2 3.2 fusion.9
  594.5 38.2 %collective-permute-done.18.refs_16_ = bf16[4,80,3584]{2,1,0:T(8,128)(2,1)S(1)} collective-permute-done((bf16[4,80,3584]{2,1,0:T(8,128)(2,1)}, bf16[4,80,3584]{2,1,0:T(8,128)(2,1)S(1)}, u32[]{:S(2)}, u32[]{:S(2)}) %collective-permute-start.18) | collective-permute-done | bytes 2293792 | tf_op jit(solution)/shard_map/ppermute | solution.py:443
  638.2 20.4 %dw_in.4 = (bf16[7168,1280]{1,0:T(8,128)(2,1)}, bf16[7168,1280]{1,0:T(8,128)(2,1)}) custom-call(bf16[2,2560,7168]{2,1,0:T(8,128)(2,1)} %get-tuple-element.45.refs_0_.dy_ref, bf16[2560,2560]{1,0:T(8,128)(2,1)} %get-tuple-element.46.refs_1_, bf16[7168,1280]{1,0:T(8,128)(2,1)} %get-tuple-element.47.refs_2_, ...), custom_call_target="tpu_custom_call", output_to_operand_aliasing={{0}: (2, {}), {1}: (3, {})} | custom-call | flops 13421772800 | bytes 23592960 | tf_op jit(solution)/shard_map/dw_in/pallas_call | solution.py:312
  659.9 2.5 fusion.3.refs_4_
  669.4 11.3 %collective-permute-done.22 = bf16[80,3584]{1,0:T(8,128)(2,1)S(1)} collective-permute-done((bf16[80,3584]{1,0:T(8,128)(2,1)S(1)}, bf16[80,3584]{1,0:T(8,128)(2,1)S(1)}, u32[]{:S(2)}, u32[]{:S(2)}) %collective-permute-start.22) | collective-permute-done | bytes 573472 | tf_op jit(solution)/shard_map/ppermute | solution.py:443
  682.5 3.3 collective-permute-start.11
  687.2 2.6 collective-permute-start.23
  689.8 20.3 %dw_in.5 = (bf16[7168,1280]{1,0:T(8,128)(2,1)}, bf16[7168,1280]{1,0:T(8,128)(2,1)}) custom-call(bf16[2,2560,7168]{2,1,0:T(8,128)(2,1)} %get-tuple-element.45.refs_0_.dy_ref, bf16[2560,2560]{1,0:T(8,128)(2,1)} %get-tuple-element.46.refs_1_, bf16[7168,1280]{1,0:T(8,128)(2,1)} %get-tuple-element.49.refs_2_, ...), custom_call_target="tpu_custom_call", output_to_operand_aliasing={{0}: (2, {}), {1}: (3, {})} | custom-call | flops 13421772800 | bytes 23592960 | tf_op jit(solution)/shard_map/dw_in/pallas_call | solution.py:312
  712.2 8.7 %dx_total.1 = bf16[160,7168]{1,0:T(8,128)(2,1)} custom-call(bf16[4,80,3584]{2,1,0:T(8,128)(2,1)} %get-tuple-element.29.refs_0_, bf16[4,80,3584]{2,1,0:T(8,128)(2,1)} %collective-permute-done.1.refs_1_, bf16[4,80,3584]{2,1,0:T(8,128)(2,1)} %copy-done.4, bf16[80,3584]{1,0:T(8,128)(2,1)} %collective-permute-done.4.refs_3_, ...), custom_call_target="tpu_custom_call" | custom-call | flops 4587520 | bytes 13762560 | tf_op jit(solution)/shard_map/dx_total/pallas_call | solution.py:422
  (86 shorter events, 25.6 us)
Async XLA Ops:
  380.2 63.1 %collective-permute-start = (bf16[4,80,3584]{2,1,0:T(8,128)(2,1)}, bf16[4,80,3584]{2,1,0:T(8,128)(2,1)}, u32[]{:S(2)}, u32[]{:S(2)}) collective-permute-start(bf16[4,80,3584]{2,1,0:T(8,128)(2,1)} %get-tuple-element.31), channel_id=1, source_target_pairs={{0,4},{1,5},{2,6},{3,7},{4,8},{5,9},{6,10},{7,11},{8,12},{9,13},{1... | collective-permute-start | bytes 6881288 | tf_op jit(solution)/shard_map/ppermute | solution.py:443
  380.3 118.6 %collective-permute-start.2 = (bf16[4,80,3584]{2,1,0:T(8,128)(2,1)}, bf16[4,80,3584]{2,1,0:T(8,128)(2,1)S(1)}, u32[]{:S(2)}, u32[]{:S(2)}) collective-permute-start(bf16[4,80,3584]{2,1,0:T(8,128)(2,1)} %get-tuple-element.32), channel_id=1, source_target_pairs={{0,12},{1,13},{2,14},{3,15},{4,0},{5,1},{6,2},{7,3},{8,4},{9,5},{1... | collective-permute-start | bytes 6881288 | tf_op jit(solution)/shard_map/ppermute | solution.py:443
  383.5 194.7 %collective-permute-start.6 = (bf16[4,80,3584]{2,1,0:T(8,128)(2,1)}, bf16[4,80,3584]{2,1,0:T(8,128)(2,1)}, u32[]{:S(2)}, u32[]{:S(2)}) collective-permute-start(bf16[4,80,3584]{2,1,0:T(8,128)(2,1)} %get-tuple-element.34), channel_id=1, source_target_pairs={{0,4},{1,5},{2,6},{3,7},{4,8},{5,9},{6,10},{7,11},{8,12},{9,13},{1... | collective-permute-start | bytes 6881288 | tf_op jit(solution)/shard_map/ppermute | solution.py:443
  383.5 97.5 %collective-permute-start.7 = (bf16[4,80,3584]{2,1,0:T(8,128)(2,1)}, bf16[4,80,3584]{2,1,0:T(8,128)(2,1)}, u32[]{:S(2)}, u32[]{:S(2)}) collective-permute-start(bf16[4,80,3584]{2,1,0:T(8,128)(2,1)} %get-tuple-element.36), channel_id=1, source_target_pairs={{0,12},{1,13},{2,14},{3,15},{4,0},{5,1},{6,2},{7,3},{8,4},{9,5},{1... | collective-permute-start | bytes 6881288 | tf_op jit(solution)/shard_map/ppermute | solution.py:443
  386.7 99.3 %collective-permute-start.12 = (bf16[4,80,3584]{2,1,0:T(8,128)(2,1)}, bf16[4,80,3584]{2,1,0:T(8,128)(2,1)}, u32[]{:S(2)}, u32[]{:S(2)}) collective-permute-start(bf16[4,80,3584]{2,1,0:T(8,128)(2,1)} %get-tuple-element.39), channel_id=1, source_target_pairs={{0,1},{1,2},{2,3},{3,0},{4,5},{5,6},{6,7},{7,4},{8,9},{9,10},{10,1... | collective-permute-start | bytes 6881288 | tf_op jit(solution)/shard_map/ppermute | solution.py:443
  443.3 53.8 %collective-permute-start.19 = (bf16[4,80,3584]{2,1,0:T(8,128)(2,1)}, bf16[4,80,3584]{2,1,0:T(8,128)(2,1)S(1)}, u32[]{:S(2)}, u32[]{:S(2)}) collective-permute-start(bf16[4,80,3584]{2,1,0:T(8,128)(2,1)} %get-tuple-element.44), channel_id=1, source_target_pairs={{0,3},{1,0},{2,1},{3,2},{4,7},{5,4},{6,5},{7,6},{8,11},{9,8},{10,9... | collective-permute-start | bytes 6881288 | tf_op jit(solution)/shard_map/ppermute | solution.py:443
  481.0 107.0 %collective-permute-start.14 = (bf16[4,80,3584]{2,1,0:T(8,128)(2,1)}, bf16[4,80,3584]{2,1,0:T(8,128)(2,1)}, u32[]{:S(2)}, u32[]{:S(2)}) collective-permute-start(bf16[4,80,3584]{2,1,0:T(8,128)(2,1)} %get-tuple-element.40), channel_id=1, source_target_pairs={{0,3},{1,0},{2,1},{3,2},{4,7},{5,4},{6,5},{7,6},{8,11},{9,8},{10,9... | collective-permute-start | bytes 6881288 | tf_op jit(solution)/shard_map/ppermute | solution.py:443
  486.0 92.8 %collective-permute-start.1 = (bf16[4,80,3584]{2,1,0:T(8,128)(2,1)}, bf16[4,80,3584]{2,1,0:T(8,128)(2,1)}, u32[]{:S(2)}, u32[]{:S(2)}) collective-permute-start(bf16[4,80,3584]{2,1,0:T(8,128)(2,1)} %add_convert_fusion.3.refs_2_), channel_id=1, source_target_pairs={{0,4},{1,5},{2,6},{3,7},{4,8},{5,9},{6,10},{7,11},{8,12},{9,13},{1... | collective-permute-start | bytes 6881288 | tf_op jit(solution)/shard_map/ppermute | solution.py:443
  497.0 87.8 %collective-permute-start.8 = (bf16[4,80,3584]{2,1,0:T(8,128)(2,1)}, bf16[4,80,3584]{2,1,0:T(8,128)(2,1)}, u32[]{:S(2)}, u32[]{:S(2)}) collective-permute-start(bf16[4,80,3584]{2,1,0:T(8,128)(2,1)} %add_convert_fusion.2.refs_3_), channel_id=1, source_target_pairs={{0,12},{1,13},{2,14},{3,15},{4,0},{5,1},{6,2},{7,3},{8,4},{9,5},{1... | collective-permute-start | bytes 6881288 | tf_op jit(solution)/shard_map/ppermute | solution.py:443
  498.9 92.3 %collective-permute-start.13 = (bf16[4,80,3584]{2,1,0:T(8,128)(2,1)}, bf16[4,80,3584]{2,1,0:T(8,128)(2,1)}, u32[]{:S(2)}, u32[]{:S(2)}) collective-permute-start(bf16[4,80,3584]{2,1,0:T(8,128)(2,1)} %add_convert_fusion.1.refs_4_), channel_id=1, source_target_pairs={{0,1},{1,2},{2,3},{3,0},{4,5},{5,6},{6,7},{7,4},{8,9},{9,10},{10,1... | collective-permute-start | bytes 6881288 | tf_op jit(solution)/shard_map/ppermute | solution.py:443
  578.2 54.5 %collective-permute-start.18 = (bf16[4,80,3584]{2,1,0:T(8,128)(2,1)}, bf16[4,80,3584]{2,1,0:T(8,128)(2,1)S(1)}, u32[]{:S(2)}, u32[]{:S(2)}) collective-permute-start(bf16[4,80,3584]{2,1,0:T(8,128)(2,1)} %get-tuple-element.42), channel_id=1, source_target_pairs={{0,1},{1,2},{2,3},{3,0},{4,5},{5,6},{6,7},{7,4},{8,9},{9,10},{10,1... | collective-permute-start | bytes 6881288 | tf_op jit(solution)/shard_map/ppermute | solution.py:443
  578.8 55.9 %collective-permute-start.20 = (bf16[4,80,3584]{2,1,0:T(8,128)(2,1)}, bf16[4,80,3584]{2,1,0:T(8,128)(2,1)S(1)}, u32[]{:S(2)}, u32[]{:S(2)}) collective-permute-start(bf16[4,80,3584]{2,1,0:T(8,128)(2,1)} %add_convert_fusion.refs_5_), channel_id=1, source_target_pairs={{0,3},{1,0},{2,1},{3,2},{4,7},{5,4},{6,5},{7,6},{8,11},{9,8},{10,9... | collective-permute-start | bytes 6881288 | tf_op jit(solution)/shard_map/ppermute | solution.py:443
  584.8 73.8 %collective-permute-start.3 = (bf16[80,3584]{1,0:T(8,128)(2,1)}, bf16[80,3584]{1,0:T(8,128)(2,1)}, u32[]{:S(2)}, u32[]{:S(2)}) collective-permute-start(bf16[80,3584]{1,0:T(8,128)(2,1)} %get-tuple-element.61.refs_4_), channel_id=1, source_target_pairs={{0,1},{1,2},{2,3},{3,0},{4,5},{5,6},{6,7},{7,4},{8,9},{9,10},{10,1... | collective-permute-start | bytes 1720328 | tf_op jit(solution)/shard_map/ppermute | solution.py:443
  588.0 94.4 %collective-permute-start.5 = (bf16[80,3584]{1,0:T(8,128)(2,1)S(1)}, bf16[80,3584]{1,0:T(8,128)(2,1)}, u32[]{:S(2)}, u32[]{:S(2)}) collective-permute-start(bf16[80,3584]{1,0:T(8,128)(2,1)S(1)} %get-tuple-element.60.refs_7_), channel_id=1, source_target_pairs={{0,3},{1,0},{2,1},{3,2},{4,7},{5,4},{6,5},{7,6},{8,11},{9,8},{10,9... | collective-permute-start | bytes 1720328 | tf_op jit(solution)/shard_map/ppermute | solution.py:443
  591.2 94.5 %collective-permute-start.9 = (bf16[80,3584]{1,0:T(8,128)(2,1)S(1)}, bf16[80,3584]{1,0:T(8,128)(2,1)}, u32[]{:S(2)}, u32[]{:S(2)}) collective-permute-start(bf16[80,3584]{1,0:T(8,128)(2,1)S(1)} %get-tuple-element.59.refs_6_), channel_id=1, source_target_pairs={{0,1},{1,2},{2,3},{3,0},{4,5},{5,6},{6,7},{7,4},{8,9},{9,10},{10,1... | collective-permute-start | bytes 1720328 | tf_op jit(solution)/shard_map/ppermute | solution.py:443
  632.7 29.7 %collective-permute-start.10 = (bf16[80,3584]{1,0:T(8,128)(2,1)}, bf16[80,3584]{1,0:T(8,128)(2,1)}, u32[]{:S(2)}, u32[]{:S(2)}) collective-permute-start(bf16[80,3584]{1,0:T(8,128)(2,1)} %get-tuple-element.58.refs_5_), channel_id=1, source_target_pairs={{0,3},{1,0},{2,1},{3,2},{4,7},{5,4},{6,5},{7,6},{8,11},{9,8},{10,9... | collective-permute-start | bytes 1720328 | tf_op jit(solution)/shard_map/ppermute | solution.py:443
  634.7 30.4 %collective-permute-start.15 = (bf16[80,3584]{1,0:T(8,128)(2,1)}, bf16[80,3584]{1,0:T(8,128)(2,1)}, u32[]{:S(2)}, u32[]{:S(2)}) collective-permute-start(bf16[80,3584]{1,0:T(8,128)(2,1)} %get-tuple-element.57.refs_8_), channel_id=1, source_target_pairs={{0,4},{1,5},{2,6},{3,7},{4,8},{5,9},{6,10},{7,11},{8,12},{9,13},{1... | collective-permute-start | bytes 1720328 | tf_op jit(solution)/shard_map/ppermute | solution.py:443
  658.6 27.8 %collective-permute-start.17 = (bf16[80,3584]{1,0:T(8,128)(2,1)S(1)}, bf16[80,3584]{1,0:T(8,128)(2,1)S(1)}, u32[]{:S(2)}, u32[]{:S(2)}) collective-permute-start(bf16[80,3584]{1,0:T(8,128)(2,1)S(1)} %copy-done.9), channel_id=1, source_target_pairs={{0,12},{1,13},{2,14},{3,15},{4,0},{5,1},{6,2},{7,3},{8,4},{9,5},{1... | collective-permute-start | bytes 1720328 | tf_op jit(solution)/shard_map/ppermute | solution.py:443
  662.4 47.8 %collective-permute-start.21 = (bf16[80,3584]{1,0:T(8,128)(2,1)}, bf16[80,3584]{1,0:T(8,128)(2,1)S(1)}, u32[]{:S(2)}, u32[]{:S(2)}) collective-permute-start(bf16[80,3584]{1,0:T(8,128)(2,1)} %get-tuple-element.55.refs_10_), channel_id=1, source_target_pairs={{0,4},{1,5},{2,6},{3,7},{4,8},{5,9},{6,10},{7,11},{8,12},{9,13},{1... | collective-permute-start | bytes 1720328 | tf_op jit(solution)/shard_map/ppermute | solution.py:443
  665.1 15.6 %collective-permute-start.22 = (bf16[80,3584]{1,0:T(8,128)(2,1)S(1)}, bf16[80,3584]{1,0:T(8,128)(2,1)S(1)}, u32[]{:S(2)}, u32[]{:S(2)}) collective-permute-start(bf16[80,3584]{1,0:T(8,128)(2,1)S(1)} %copy-done.10), channel_id=1, source_target_pairs={{0,12},{1,13},{2,14},{3,15},{4,0},{5,1},{6,2},{7,3},{8,4},{9,5},{1... | collective-permute-start | bytes 1720328 | tf_op jit(solution)/shard_map/ppermute | solution.py:443
  680.7 29.4 %collective-permute-start.4 = (bf16[80,3584]{1,0:T(8,128)(2,1)}, bf16[80,3584]{1,0:T(8,128)(2,1)}, u32[]{:S(2)}, u32[]{:S(2)}) collective-permute-start(bf16[80,3584]{1,0:T(8,128)(2,1)} %fusion.3.refs_4_), channel_id=1, source_target_pairs={{0,1},{1,2},{2,3},{3,0},{4,5},{5,6},{6,7},{7,4},{8,9},{9,10},{10,1... | collective-permute-start | bytes 1720328 | tf_op jit(solution)/shard_map/ppermute | solution.py:443
  682.5 27.7 %collective-permute-start.11 = (bf16[80,3584]{1,0:T(8,128)(2,1)S(1)}, bf16[80,3584]{1,0:T(8,128)(2,1)S(1)}, u32[]{:S(2)}, u32[]{:S(2)}) collective-permute-start(bf16[80,3584]{1,0:T(8,128)(2,1)S(1)} %fusion.2.refs_5_), channel_id=1, source_target_pairs={{0,3},{1,0},{2,1},{3,2},{4,7},{5,4},{6,5},{7,6},{8,11},{9,8},{10,9... | collective-permute-start | bytes 1720328 | tf_op jit(solution)/shard_map/ppermute | solution.py:443
  685.8 24.4 %collective-permute-start.16 = (bf16[80,3584]{1,0:T(8,128)(2,1)S(1)}, bf16[80,3584]{1,0:T(8,128)(2,1)S(1)}, u32[]{:S(2)}, u32[]{:S(2)}) collective-permute-start(bf16[80,3584]{1,0:T(8,128)(2,1)S(1)} %fusion.1.refs_6_), channel_id=1, source_target_pairs={{0,4},{1,5},{2,6},{3,7},{4,8},{5,9},{6,10},{7,11},{8,12},{9,13},{1... | collective-permute-start | bytes 1720328 | tf_op jit(solution)/shard_map/ppermute | solution.py:443
  687.2 23.0 %collective-permute-start.23 = (bf16[80,3584]{1,0:T(8,128)(2,1)S(1)}, bf16[80,3584]{1,0:T(8,128)(2,1)S(1)}, u32[]{:S(2)}, u32[]{:S(2)}) collective-permute-start(bf16[80,3584]{1,0:T(8,128)(2,1)S(1)} %fusion.refs_7_), channel_id=1, source_target_pairs={{0,12},{1,13},{2,14},{3,15},{4,0},{5,1},{6,2},{7,3},{8,4},{9,5},{1... | collective-permute-start | bytes 1720328 | tf_op jit(solution)/shard_map/ppermute | solution.py:443
  (22 other events, 283.8 us)

commit v3 on v2

--- a/solution.py
+++ b/solution.py
@@ -10,8 +10,10 @@
 
 MESH = pl.DeviceIdType.MESH
 LINKS = ((0, 1), (0, -1), (1, 1), (1, -1))
-TICKS = 3
-FIRST = 3
+TICKS = 2
+FIRST = 6
+VMEM = 65400 * 1024
+PARTS = 3
 
 
 def tile_of(size, want):
@@ -21,12 +23,12 @@
 def gather_kernel(
     side, dt, nt,
     x_ref, dy_ref, gate_ref, up_ref, wg_ref, wu_ref, wd_ref,
-    full_ref, dgu_ref, hid_ref, *rest,
+    full_ref, dgu_ref, hid_ref, dwd_ref, *rest,
 ):
     terms, scratch = rest[: 4 * side], rest[4 * side :]
     (
-    wd_v, dy_v, g_v, u_v, dg_v, du_v, h_v, wg_t, wu_t, out_t,
-    send_sem, recv_sem, wd_sem, in_sem, res_sem, w_sem, out_sem,
+    wd_v, dy_v, g_v, u_v, dg_v, du_v, h_v, wg_t, wu_t, out_t, hid_v, ht_v, dy_t, dwd_t,
+    send_sem, recv_sem, wd_sem, in_sem, res_sem, w_sem, out_sem, hid_sem, dyt_sem, dwd_sem,
     ) = scratch
     rows, d = dy_ref.shape
     ff = gate_ref.shape[1]
@@ -58,7 +60,6 @@
         return full_ref.at[array, pl.ds(row, half), pl.ds(pl.multiple_of(col * cols, 128), cols)]
 
     def copy(k, slot, src, dst):
-        axis, sign = LINKS[k]
         return pltpu.make_async_remote_copy(
             src_ref=src,
             dst_ref=dst,
@@ -227,7 +228,6 @@
 
         step(first + 1)
         dx_tile(False)
-        step(first + 2)
         dx_tile(True)
         for c in results:
             c.wait()
@@ -238,7 +238,55 @@
 
     lax.fori_loop(0, side, groups, None)
     done = FIRST + TICKS * side * (side // 2)
-    lax.fori_loop(done, 2 * slots, lambda s, _: (step(s), None)[1], None)
+
+    fm = ff // 2
+    tokens = hid_ref.shape[0]
+    tb = tile_of(tokens, 512)
+    per = -(-tiles // PARTS)
+
+    def dy_tile(i):
+        n = pl.ds(pl.multiple_of(i * dt, dt), dt)
+        return pltpu.make_async_copy(full_ref.at[0, :, n], dy_t.at[i % 2], dyt_sem.at[i % 2])
+
+    def dwd_tile(m, i):
+        n = pl.ds(pl.multiple_of(i * dt, dt), dt)
+        row = pl.ds(pl.multiple_of(m * fm, fm), fm)
+        return pltpu.make_async_copy(dwd_t.at[i % 2], dwd_ref.at[row, n], dwd_sem.at[i % 2])
+
+    dy_tile(0).start()
+
+    def down(m, _):
+        load = pltpu.make_async_copy(hid_ref.at[:, pl.ds(pl.multiple_of(m * fm, fm), fm)], hid_v, hid_sem)
+        load.start()
+        load.wait()
+        for b in range(tokens // tb):
+            ht_v[:, b * tb : (b + 1) * tb] = hid_v[b * tb : (b + 1) * tb, :].T
+
+        def tile(i, _):
+            dy_tile(i).wait()
+
+            @pl.when((i + 1 < tiles) | (m == 0))
+            def _():
+                dy_tile((i + 1) % tiles).start()
+
+            @pl.when((i >= 2) | (m == 1))
+            def _():
+                dwd_tile(m, i).wait()
+
+            dw = jnp.dot(ht_v[...], dy_t[i % 2], preferred_element_type=jnp.float32)
+            dwd_t[i % 2] = dw.astype(dwd_t.dtype)
+            dwd_tile(m, i).start()
+
+        def part(k, _):
+            step(done + m * PARTS + k)
+            lax.fori_loop(k * per, jnp.minimum((k + 1) * per, tiles), tile, None)
+
+        lax.fori_loop(0, PARTS, part, None)
+
+    lax.fori_loop(0, 2, down, None)
+    for i in (tiles - 2, tiles - 1):
+        dwd_tile(1, i).wait()
+    lax.fori_loop(done + 2 * PARTS, 2 * slots, lambda s, _: (step(s), None)[1], None)
 
     def sent(slot, _):
         for k, link in enumerate(LINKS):
@@ -255,24 +303,29 @@
     group = 2 * rows
     dt, nt = tile_of(d // 2, 512), tile_of(ff, 256)
     bf16 = jnp.bfloat16
-    flops = 6 * tokens * d * ff
-    anywhere = pl.BlockSpec(memory_space=pl.ANY)
+    flops = 8 * tokens * d * ff
+    anywhere = pl.BlockSpec(memory_space=pltpu.HBM)
     return pl.pallas_call(
         functools.partial(gather_kernel, side, dt, nt),
         out_shape=(
             jax.ShapeDtypeStruct((2, tokens, d), bf16),
             jax.ShapeDtypeStruct((tokens, 2 * ff), bf16),
             jax.ShapeDtypeStruct((tokens, ff), bf16),
+            jax.ShapeDtypeStruct((ff, d), bf16),
             *[jax.ShapeDtypeStruct((side, rows // 2, d // 2), bf16)] * (4 * side),
         ),
         in_specs=[anywhere] * 7,
-        out_specs=(anywhere,) * (3 + 4 * side),
+        out_specs=(anywhere,) * (4 + 4 * side),
         scratch_shapes=[
             pltpu.VMEM((ff, d), bf16),
             pltpu.VMEM((group, d), bf16),
             *[pltpu.VMEM((group, ff), bf16)] * 5,
             *[pltpu.VMEM((2, dt, ff), bf16)] * 2,
             pltpu.VMEM((2, group, dt), bf16),
+            pltpu.VMEM((tokens, ff // 2), bf16),
+            pltpu.VMEM((ff // 2, tokens), bf16),
+            pltpu.VMEM((2, tokens, dt), bf16),
+            pltpu.VMEM((2, ff // 2, dt), bf16),
             pltpu.SemaphoreType.DMA((len(LINKS), 2 * (n - 1))),
             pltpu.SemaphoreType.DMA((len(LINKS), 2 * (n - 1))),
             pltpu.SemaphoreType.DMA,
@@ -280,9 +333,12 @@
             pltpu.SemaphoreType.DMA((3, 4)),
             pltpu.SemaphoreType.DMA((2, 2)),
             pltpu.SemaphoreType.DMA((2, 4)),
+            pltpu.SemaphoreType.DMA,
+            pltpu.SemaphoreType.DMA((2,)),
+            pltpu.SemaphoreType.DMA((2,)),
         ],
         compiler_params=pltpu.CompilerParams(
-            collective_id=0, has_side_effects=True, vmem_limit_bytes=60 * 1024 * 1024
+            collective_id=0, has_side_effects=True, vmem_limit_bytes=VMEM
         ),
         cost_estimate=pl.CostEstimate(
             flops=flops, bytes_accessed=2 * (8 * 2 * d * ff + 6 * tokens * d), transcendentals=tokens * ff
@@ -291,72 +347,54 @@
     )(x, dy, gate, up, wg, wu, wd)
 
 
-def dw_in_kernel(after, *refs):
-    x_ref, d_ref = refs[:2]
-    dwg_ref, dwu_ref = refs[-2:]
+def dw_in_kernel(sums, moved, *refs):
+    x_ref, d_ref, *rest = refs
+    outs = rest[len(rest) - 2 - sums - moved :]
+    dwg_ref, dwu_ref = outs[:2]
     ff = dwg_ref.shape[1]
     dw = lax.dot_general(
         x_ref[...], d_ref[...], (((0,), (0,)), ((), ())), preferred_element_type=jnp.float32
     )
     dwg_ref[...] = dw[:, :ff].astype(dwg_ref.dtype)
     dwu_ref[...] = dw[:, ff:].astype(dwu_ref.dtype)
-
-
-def dw_in(full, dgu, first, last, so_far=(), after=()):
+    for k in range(sums):
+        mine, came = rest[2 * k : 2 * k + 2]
+        outs[2 + k][...] = bf16(f32(mine[...]) + f32(came[...]))
+    for k in range(moved):
+        outs[2 + sums + k][...] = rest[2 * sums + k][...]
+
+
+def dw_in(full, dgu, first, last, so_far=(), pairs=(), moved=()):
     _, tokens, d = full.shape
     ff = dgu.shape[1] // 2
     bd = tile_of(d, 256)
-    out = jax.ShapeDtypeStruct((d, ff), full.dtype)
-    anywhere = pl.BlockSpec(memory_space=pl.ANY)
     n = last - first
+    flat = [v for pair in pairs for v in pair]
+
+    def along(v):
+        lead = v.shape[:-1]
+        return pl.BlockSpec((*lead, v.shape[-1] // n), lambda i: (*[0] * len(lead), i))
+
+    extra = [a for a, _ in pairs] + list(moved)
+    new = [jax.ShapeDtypeStruct((d, ff), full.dtype)] * 2 + [jax.ShapeDtypeStruct(v.shape, v.dtype) for v in extra]
     return pl.pallas_call(
-        functools.partial(dw_in_kernel, len(after)),
+        functools.partial(dw_in_kernel, len(pairs), len(moved)),
         grid=(n,),
-        out_shape=(out, out),
+        out_shape=new,
         in_specs=[
             pl.BlockSpec((pl.squeezed, tokens, bd), lambda i: (1, 0, i + first)),
             pl.BlockSpec((tokens, 2 * ff), lambda i: (0, 0), pipeline_mode=pl.Buffered(1)),
-            *[anywhere] * (len(so_far) + len(after)),
+            *[along(v) for v in (*flat, *moved)],
+            *[pl.BlockSpec(memory_space=pltpu.HBM)] * len(so_far),
         ],
-        out_specs=[pl.BlockSpec((bd, ff), lambda i: (i + first, 0))] * 2,
-        input_output_aliases={2 + i: i for i in range(len(so_far))},
-        compiler_params=pltpu.CompilerParams(vmem_limit_bytes=60 * 1024 * 1024),
+        out_specs=[*[pl.BlockSpec((bd, ff), lambda i: (i + first, 0))] * 2, *[along(v) for v in extra]],
+        input_output_aliases={2 + len(flat) + len(moved) + i: i for i in range(len(so_far))},
+        compiler_params=pltpu.CompilerParams(vmem_limit_bytes=VMEM),
         cost_estimate=pl.CostEstimate(
             flops=4 * tokens * n * bd * ff, bytes_accessed=2 * (tokens * n * bd + 2 * ff * (tokens + n * bd)), transcendentals=0
         ),
         name="dw_in",
-    )(full, dgu, *so_far, *after)
-
-
-def dw_out_kernel(h_ref, dy_ref, dw_ref, ht):
-    @pl.when(pl.program_id(0) == 0)
-    def _():
-        ht[...] = h_ref[...].T
-
-    dw = jnp.dot(ht[...], dy_ref[...], preferred_element_type=jnp.float32)
-    dw_ref[...] = dw.astype(dw_ref.dtype)
-
-
-def dw_out(full, hidden):
-    _, tokens, d = full.shape
-    ff = hidden.shape[1]
-    bd = tile_of(d, 512)
-    return pl.pallas_call(
-        dw_out_kernel,
-        grid=(d // bd,),
-        out_shape=jax.ShapeDtypeStruct((ff, d), full.dtype),
-        in_specs=[
-            pl.BlockSpec((tokens, ff), lambda i: (0, 0), pipeline_mode=pl.Buffered(1)),
-            pl.BlockSpec((pl.squeezed, tokens, bd), lambda i: (0, 0, i)),
-        ],
-        out_specs=pl.BlockSpec((ff, bd), lambda i: (0, i)),
-        scratch_shapes=[pltpu.VMEM((ff, tokens), full.dtype)],
-        compiler_params=pltpu.CompilerParams(vmem_limit_bytes=60 * 1024 * 1024),
-        cost_estimate=pl.CostEstimate(
-            flops=2 * tokens * d * ff, bytes_accessed=2 * (tokens * d + ff * (tokens + d)), transcendentals=0
-        ),
-        name="dw_out",
-    )(hidden, full)
+    )(full, dgu, *flat, *moved, *so_far)
 
 
 def f32(v):
@@ -367,68 +405,111 @@
     return v.astype(jnp.bfloat16)
 
 
-def exchange(hop, t, one, two):
-    far = [hop(t[2][0], one, 1), hop(t[2][1], one, -1)]
-    raw = [hop(t[1][1], one, 1), hop(t[3][0], one, -1)]
-    near = [bf16(f32(t[1][0]) + f32(far[0])), bf16(f32(t[3][1]) + f32(far[1]))]
-    yield near
-    near = [hop(near[0], one, 1), hop(near[1], one, -1)]
-    plus, minus = [near[0], raw[0]], [raw[1], near[1]]
-
-    def piece(j, r):
-        return f32(t[0][r][j]) + f32(plus[r][j]) + f32(minus[r][j])
-
-    far = [bf16(piece(2, 0)), bf16(piece(2, 1))]
-    raw = [bf16(piece(1, 1)), bf16(piece(3, 0))]
-    yield [*far, *raw]
-    far = [hop(far[0], two, 1), hop(far[1], two, -1)]
-    raw = [hop(raw[0], two, 1), hop(raw[1], two, -1)]
-    near = [bf16(piece(1, 0) + f32(far[0])), bf16(piece(3, 1) + f32(far[1]))]
-    yield near
-    near = [hop(near[0], two, 1), hop(near[1], two, -1)]
-    last_plus, last_minus = [near[0], raw[0]], [raw[1], near[1]]
-    yield [(t[0][r], plus[r], minus[r], last_plus[r], last_minus[r]) for r in range(2)]
-
-
-def total_kernel(chunks, *refs):
-    *ins, out_ref = refs
-    half = ins[0].shape[0]
+def finish_kernel(side, *refs):
+    ins, (out_ref, in_v, send_v, recv_v, out_v, in_sem, send_sem, recv_sem, out_sem) = refs[:12], refs[12:]
+    half, cols = out_v.shape[0] // 2, out_v.shape[1] // 2
+    me = lax.axis_index("tp")
+    at = (me // side, me % side)
+
+    def neighbour(axis, sign):
+        to = [at[0], at[1]]
+        to[axis] = lax.rem(to[axis] + sign + side, side)
+        return {"tp": to[0] * side + to[1]}
+
+    barrier = pltpu.get_barrier_semaphore()
+    for axis, sign in LINKS:
+        pl.semaphore_signal(barrier, inc=1, device_id=neighbour(axis, sign), device_id_type=MESH)
+
+    order = (((2, 0), (2, 1)), ((1, 1), (3, 0)), ((1, 0), (3, 1)))
+
+    def loads(h, j, r):
+        return [
+            pltpu.make_async_copy(ins[6 * h + 3 * r + k].at[j], in_v.at[h, j, r, k], in_sem.at[h, j, r, k])
+            for k in range(3)
+        ]
+
+    pieces = [p for step in order for p in step] + [(0, 0), (0, 1)]
+    for j, r in pieces:
+        for h in range(2):
+            for c in loads(h, j, r):
+                c.start()
+
+    def piece(h, j, r):
+        for c in loads(h, j, r):
+            c.wait()
+        return f32(in_v[h, j, r, 0]) + f32(in_v[h, j, r, 1]) + f32(in_v[h, j, r, 2])
+
+    def message(h, step, way):
+        return pltpu.make_async_remote_copy(
+            src_ref=send_v.at[h, step, way],
+            dst_ref=recv_v.at[h, step, way],
+            send_sem=send_sem.at[h, step, way],
+            recv_sem=recv_sem.at[h, step, way],
+            device_id=neighbour(1 - h, 1 - 2 * way),
+            device_id_type=MESH,
+        )
+
+    ready = False
+    for step, steps in enumerate(order):
+        for h in range(2):
+            for way, (j, r) in enumerate(steps):
+                total = piece(h, j, r)
+                if step == 2:
+                    message(h, 0, way).wait_recv()
+                    total += f32(recv_v[h, 0, way])
+                send_v[h, step, way] = bf16(total)
+                if not ready:
+                    pl.semaphore_wait(barrier, len(LINKS))
+                    ready = True
+                message(h, step, way).start()
+    stores = []
+    for step in (1, 2):
+        for h in range(2):
+            for way in range(2):
+                message(h, step, way).wait_recv()
     for h in range(2):
-
-        @pl.when(pl.program_id(0) // chunks == h)
-        def _():
-            for r in range(2):
-                parts = ins[10 * h + 5 * r :][:5]
-                total = f32(parts[0][...])
-                for part in parts[1:]:
-                    total += f32(part[...])
-                out_ref[r * half : (r + 1) * half, :] = bf16(total)
-
-
-def total(halves):
-    half, cols = halves[0][0][-1].shape
-    chunk = tile_of(cols, 896)
-    chunks = cols // chunk
-    specs, args = [], []
-    for h, parts in enumerate(halves):
-        col = (lambda i: jnp.minimum(i, chunks - 1)) if h == 0 else (lambda i: jnp.maximum(i - chunks, 0))
         for r in range(2):
-            for v in parts[r]:
-                args.append(v)
-                if v.ndim == 3:
-                    specs.append(pl.BlockSpec((pl.squeezed, half, chunk), lambda i, col=col: (0, 0, col(i))))
-                else:
-                    specs.append(pl.BlockSpec((half, chunk), lambda i, col=col: (0, col(i))))
+            total = piece(h, 0, r)
+            total += f32(recv_v[h, 2 if r == 0 else 1, 0]) + f32(recv_v[h, 1 if r == 0 else 2, 1])
+            part = (pl.ds(r * half, half), pl.ds(h * cols, cols))
+            out_v[part] = bf16(total)
+            stores.append(pltpu.make_async_copy(out_v.at[part], out_ref.at[part], out_sem.at[h, r]))
+            stores[-1].start()
+    for c in stores:
+        c.wait()
+    for step in range(3):
+        for h in range(2):
+            for way in range(2):
+                message(h, step, way).wait_send()
+
+
+def finish(side, ins):
+    _, half, cols = ins[0].shape
+    anywhere = pl.BlockSpec(memory_space=pltpu.HBM)
+    dtype = jnp.bfloat16
     return pl.pallas_call(
-        functools.partial(total_kernel, chunks),
-        grid=(2 * chunks,),
-        out_shape=jax.ShapeDtypeStruct((2 * half, 2 * cols), jnp.bfloat16),
-        in_specs=specs,
-        out_specs=pl.BlockSpec((2 * half, chunk), lambda i: (0, i)),
-        cost_estimate=pl.CostEstimate(flops=16 * half * cols, bytes_accessed=48 * half * cols, transcendentals=0),
-        compiler_params=pltpu.CompilerParams(vmem_limit_bytes=60 * 1024 * 1024),
-        name="dx_total",
-    )(*args)
+        functools.partial(finish_kernel, side),
+        out_shape=jax.ShapeDtypeStruct((2 * half, 2 * cols), dtype),
+        in_specs=[anywhere] * len(ins),
+        out_specs=anywhere,
+        scratch_shapes=[
+            pltpu.VMEM((2, side, 2, 3, half, cols), dtype),
+            pltpu.VMEM((2, 3, 2, half, cols), dtype),
+            pltpu.VMEM((2, 3, 2, half, cols), dtype),
+            pltpu.VMEM((2 * half, 2 * cols), dtype),
+            pltpu.SemaphoreType.DMA((2, side, 2, 3)),
+            pltpu.SemaphoreType.DMA((2, 3, 2)),
+            pltpu.SemaphoreType.DMA((2, 3, 2)),
+            pltpu.SemaphoreType.DMA((2, 2)),
+        ],
+        compiler_params=pltpu.CompilerParams(
+            collective_id=1, has_side_effects=True, vmem_limit_bytes=VMEM
+        ),
+        cost_estimate=pl.CostEstimate(
+            flops=64 * half * cols, bytes_accessed=2 * 52 * half * cols, transcendentals=0
+        ),
+        name="finish_dx",
+    )(*ins)
 
 
 def solution(mesh):
@@ -443,21 +524,21 @@
         return lax.ppermute(v, "tp", pairs)
 
     def device_step(x, dy, gate, up, w_gate, w_up, w_down):
-        full, dgu, hidden, *terms = gather(side, x, dy, gate, up, w_gate, w_up, w_down)
+        full, dgu, _, dw_down, *terms = gather(side, x, dy, gate, up, w_gate, w_up, w_down)
+        t = [[terms[2 * (h * side + k) :][:2] for k in range(side)] for h in range(2)]
         blocks = x.shape[1] // tile_of(x.shape[1], 256)
-        cuts = [0, blocks * 5 // 7, blocks * 6 // 7, blocks]
-        halves = [
-            exchange(hop, [terms[4 * side // 2 * h + 2 * k :][:2] for k in range(side)], h, 1 - h)
-            for h in range(2)
-        ]
-        dw_down = dw_out(full, hidden)
-        near = [next(e) for e in halves]
-        dw = dw_in(full, dgu, cuts[0], cuts[1], after=[v for n in near for v in n])
-        turn = [next(e) for e in halves]
-        dw = dw_in(full, dgu, cuts[1], cuts[2], dw, after=[v for n in turn for v in n])
-        near = [next(e) for e in halves]
-        dw = dw_in(full, dgu, cuts[2], cuts[3], dw, after=[v for n in near for v in n])
-        dx = total([next(e) for e in halves])
+        cuts = [0, blocks * 10 // 28, blocks * 14 // 28, blocks]
+        far = [(hop(v[2][0], h, 1), hop(v[2][1], h, -1)) for h, v in enumerate(t)]
+        raw = [(hop(v[1][1], h, 1), hop(v[3][0], h, -1)) for h, v in enumerate(t)]
+        dw = dw_in(full, dgu, cuts[0], cuts[1])
+        pairs = [(v[1][0], f[0]) for v, f in zip(t, far)] + [(v[3][1], f[1]) for v, f in zip(t, far)]
+        *dw, a, b, c, d = dw_in(full, dgu, cuts[1], cuts[2], dw, pairs)
+        near = [(hop(up_, h, 1), hop(down, h, -1)) for h, (up_, down) in enumerate(((a, c), (b, d)))]
+        *dw, dw_down = dw_in(full, dgu, cuts[2], cuts[3], dw, moved=[dw_down])
+        ins = []
+        for v, r, n in zip(t, raw, near):
+            ins += [v[0][0], n[0], r[1], v[0][1], r[0], n[1]]
+        dx = finish(side, ins)
         return dx, *dw, dw_down
 
     rows, both, cols = P(("dp", "tp"), None), P("dp", "tp"), P(None, "tp")

time: 725 us -> 703 us (0.970)
  the two profiles are of different devices: /device:TPU:96 before, /device:TPU:97 now
where the time goes in v3:
time: 703 us; the launch traced here: 693 us
  Pallas kernels  623 us (89%)
  waiting for transfers between devices  52.6 us (7%)
  starting transfers between devices  13.7 us (2%)
    pallas_call x1, Pallas kernels, gather(): pl.pallas_call(functools.partial(gather_kernel, side, dt, nt), out_shape=...  457 us
    pallas_call x3, Pallas kernels, dw_in(): pl.pallas_call(functools.partial(dw_in_kernel, len(pairs), len(moved)), g...  126 us
    ppermute x12, waiting for transfers between devices, hop(): return lax.ppermute(v, 'tp', pairs)  52.6 us
    pallas_call x1, Pallas kernels, finish(): pl.pallas_call(functools.partial(finish_kernel, side), out_shape=jax.Shap...  40 us
  transfers between devices with their start and end apart: 12, of which 3 were waited for; matrix products, arithmetic and copies ran while one was open for 0% of the time, Pallas kernels for 18%

profile of v3, /device:TPU:97, one launch (start us, length us, event | category | flops | bytes accessed | tf_op | source)
XLA Modules:
  0.0 693.4 jit_solution(2362302416829055116)
XLA Ops:
  0.6 457.3 %gather_and_dx.1 = (bf16[2,2560,7168]{2,1,0:T(8,128)(2,1)}, bf16[2560,2560]{1,0:T(8,128)(2,1)}, bf16[2560,1280]{1,0:T(8,128)(2,1)}, bf16[1280,7168]{1,0:T(8,128)...) custom-call(bf16[160,7168]{1,0:T(8,128)(2,1)} %x_ref.1, ...), custom_call_target="tpu_custom_call" | custom-call | flops 187904819200 | bytes 513802240 | tf_op jit(solution)/shard_map/gather_and_dx/pallas_call | solution.py:308
  458.0 1.2 collective-permute-start
  459.2 0.1 collective-permute-start.1
  459.3 2.6 collective-permute-start.2
  461.8 1.6 collective-permute-start.3
  463.4 1.2 collective-permute-start.5
  464.6 43.4 %collective-permute-done.refs_3_ = bf16[4,80,3584]{2,1,0:T(8,128)(2,1)} collective-permute-done((bf16[4,80,3584]{2,1,0:T(8,128)(2,1)}, bf16[4,80,3584]{2,1,0:T(8,128)(2,1)}, u32[]{:S(2)}, u32[]{:S(2)}) %collective-permute-start) | collective-permute-done | bytes 2293792 | tf_op jit(solution)/shard_map/ppermute | solution.py:524
  508.0 0.0 collective-permute-start.6
  508.0 0.8 collective-permute-done.1.refs_5_
  508.8 1.5 collective-permute-start.9
  510.4 41.9 %dw_in.3 = (bf16[7168,1280]{1,0:T(8,128)(2,1)}, bf16[7168,1280]{1,0:T(8,128)(2,1)}) custom-call(bf16[2,2560,7168]{2,1,0:T(8,128)(2,1)} %get-tuple-element.35.refs_0_, bf16[2560,2560]{1,0:T(8,128)(2,1)} %get-tuple-element.36.refs_1_), custom_call_target="tpu_custom_call" | custom-call | flops 33554432000 | bytes 39321600 | tf_op jit(solution)/shard_map/dw_in/pallas_call | solution.py:380
  552.2 0.0 collective-permute-done.2.refs_7_
  552.2 0.0 collective-permute-start.10
  552.3 0.0 collective-permute-done.3.refs_9_
  552.3 26.4 %dw_in.4 = (bf16[7168,1280]{1,0:T(8,128)(2,1)}, bf16[7168,1280]{1,0:T(8,128)(2,1)}, bf16[4,80,3584]{2,1,0:T(8,128)(2,1)}, bf16[4,80,3584]{2,1,0:T(8,128)(2,1)}, ...) custom-call(bf16[2,2560,7168]{2,1,0:T(8,128)(2,1)} %get-tuple-element.3, ...), custom_call_target="tpu_custom_call", output_to_operand_aliasing={{0}: (10, {}), {1}: (11, {})} | custom-call | flops 13421772800 | bytes 23592960 | tf_op jit(solution)/shard_map/dw_in/pallas_call | solution.py:380
  578.7 1.0 collective-permute-start.4
  579.7 1.9 collective-permute-start.7
  581.6 0.0 collective-permute-done.6.refs_4_
  581.6 0.2 collective-permute-start.8
  581.7 2.5 collective-permute-start.11
  584.3 57.6 %dw_in.5 = (bf16[7168,1280]{1,0:T(8,128)(2,1)}, bf16[7168,1280]{1,0:T(8,128)(2,1)}, bf16[1280,7168]{1,0:T(8,128)(2,1)}) custom-call(bf16[2,2560,7168]{2,1,0:T(8,128)(2,1)} %get-tuple-element.35.refs_0_, bf16[2560,2560]{1,0:T(8,128)(2,1)} %get-tuple-element.36.refs_1_, ...), custom_call_target="tpu_custom_call", output_to_operand_aliasing={{0}: (3, {}), {1}: (4, {})} | custom-call | flops 46976204800 | bytes 49807360 | tf_op jit(solution)/shard_map/dw_in/pallas_call | solution.py:380
  641.9 8.3 %collective-permute-done.8.refs_7_ = bf16[4,80,3584]{2,1,0:T(8,128)(2,1)} collective-permute-done((bf16[4,80,3584]{2,1,0:T(8,128)(2,1)}, bf16[4,80,3584]{2,1,0:T(8,128)(2,1)}, u32[]{:S(2)}, u32[]{:S(2)}) %collective-permute-start.8) | collective-permute-done | bytes 2293792 | tf_op jit(solution)/shard_map/ppermute | solution.py:524
  650.2 40.0 %finish_dx.1 = bf16[160,7168]{1,0:T(8,128)(2,1)} custom-call(bf16[4,80,3584]{2,1,0:T(8,128)(2,1)} %get-tuple-element.34.refs_0_, bf16[4,80,3584]{2,1,0:T(8,128)(2,1)} %collective-permute-done.4.refs_1_, bf16[4,80,3584]{2,1,0:T(8,128)(2,1)} %collective-permute-done.5.refs_2_, bf16[4,80,3584]{2,1,0:T(8,128)(2,1)} %get-tuple-element.49.refs_3_, ...), custom_call_target="tpu_custom_call" | custom-call | flops 18350080 | bytes 29818880 | tf_op jit(solution)/shard_map/finish_dx/pallas_call | solution.py:490
  690.2 3.2 copy.20
  (6 shorter events, 0.0 us)
Async XLA Ops:
  458.0 50.1 %collective-permute-start = (bf16[4,80,3584]{2,1,0:T(8,128)(2,1)}, bf16[4,80,3584]{2,1,0:T(8,128)(2,1)}, u32[]{:S(2)}, u32[]{:S(2)}) collective-permute-start(bf16[4,80,3584]{2,1,0:T(8,128)(2,1)} %get-tuple-element.38), channel_id=1, source_target_pairs={{0,4},{1,5},{2,6},{3,7},{4,8},{5,9},{6,10},{7,11},{8,12},{9,13},{1... | collective-permute-start | bytes 6881288 | tf_op jit(solution)/shard_map/ppermute | solution.py:524
  459.2 49.7 %collective-permute-start.1 = (bf16[4,80,3584]{2,1,0:T(8,128)(2,1)}, bf16[4,80,3584]{2,1,0:T(8,128)(2,1)}, u32[]{:S(2)}, u32[]{:S(2)}) collective-permute-start(bf16[4,80,3584]{2,1,0:T(8,128)(2,1)} %get-tuple-element.40), channel_id=1, source_target_pairs={{0,1},{1,2},{2,3},{3,0},{4,5},{5,6},{6,7},{7,4},{8,9},{9,10},{10,1... | collective-permute-start | bytes 6881288 | tf_op jit(solution)/shard_map/ppermute | solution.py:524
  459.3 93.0 %collective-permute-start.2 = (bf16[4,80,3584]{2,1,0:T(8,128)(2,1)}, bf16[4,80,3584]{2,1,0:T(8,128)(2,1)}, u32[]{:S(2)}, u32[]{:S(2)}) collective-permute-start(bf16[4,80,3584]{2,1,0:T(8,128)(2,1)} %get-tuple-element.42), channel_id=1, source_target_pairs={{0,12},{1,13},{2,14},{3,15},{4,0},{5,1},{6,2},{7,3},{8,4},{9,5},{1... | collective-permute-start | bytes 6881288 | tf_op jit(solution)/shard_map/ppermute | solution.py:524
  461.8 90.4 %collective-permute-start.3 = (bf16[4,80,3584]{2,1,0:T(8,128)(2,1)}, bf16[4,80,3584]{2,1,0:T(8,128)(2,1)}, u32[]{:S(2)}, u32[]{:S(2)}) collective-permute-start(bf16[4,80,3584]{2,1,0:T(8,128)(2,1)} %get-tuple-element.44), channel_id=1, source_target_pairs={{0,3},{1,0},{2,1},{3,2},{4,7},{5,4},{6,5},{7,6},{8,11},{9,8},{10,9... | collective-permute-start | bytes 6881288 | tf_op jit(solution)/shard_map/ppermute | solution.py:524
  463.4 116.3 %collective-permute-start.5 = (bf16[4,80,3584]{2,1,0:T(8,128)(2,1)}, bf16[4,80,3584]{2,1,0:T(8,128)(2,1)}, u32[]{:S(2)}, u32[]{:S(2)}) collective-permute-start(bf16[4,80,3584]{2,1,0:T(8,128)(2,1)} %get-tuple-element.48), channel_id=1, source_target_pairs={{0,12},{1,13},{2,14},{3,15},{4,0},{5,1},{6,2},{7,3},{8,4},{9,5},{1... | collective-permute-start | bytes 6881288 | tf_op jit(solution)/shard_map/ppermute | solution.py:524
  508.0 73.5 %collective-permute-start.6 = (bf16[4,80,3584]{2,1,0:T(8,128)(2,1)}, bf16[4,80,3584]{2,1,0:T(8,128)(2,1)}, u32[]{:S(2)}, u32[]{:S(2)}) collective-permute-start(bf16[4,80,3584]{2,1,0:T(8,128)(2,1)} %get-tuple-element.50), channel_id=1, source_target_pairs={{0,4},{1,5},{2,6},{3,7},{4,8},{5,9},{6,10},{7,11},{8,12},{9,13},{1... | collective-permute-start | bytes 6881288 | tf_op jit(solution)/shard_map/ppermute | solution.py:524
  508.8 72.9 %collective-permute-start.9 = (bf16[4,80,3584]{2,1,0:T(8,128)(2,1)}, bf16[4,80,3584]{2,1,0:T(8,128)(2,1)}, u32[]{:S(2)}, u32[]{:S(2)}) collective-permute-start(bf16[4,80,3584]{2,1,0:T(8,128)(2,1)} %get-tuple-element.54), channel_id=1, source_target_pairs={{0,3},{1,0},{2,1},{3,2},{4,7},{5,4},{6,5},{7,6},{8,11},{9,8},{10,9... | collective-permute-start | bytes 6881288 | tf_op jit(solution)/shard_map/ppermute | solution.py:524
  552.2 89.7 %collective-permute-start.10 = (bf16[4,80,3584]{2,1,0:T(8,128)(2,1)}, bf16[4,80,3584]{2,1,0:T(8,128)(2,1)}, u32[]{:S(2)}, u32[]{:S(2)}) collective-permute-start(bf16[4,80,3584]{2,1,0:T(8,128)(2,1)} %get-tuple-element.56), channel_id=1, source_target_pairs={{0,1},{1,2},{2,3},{3,0},{4,5},{5,6},{6,7},{7,4},{8,9},{9,10},{10,1... | collective-permute-start | bytes 6881288 | tf_op jit(solution)/shard_map/ppermute | solution.py:524
  578.7 63.2 %collective-permute-start.4 = (bf16[4,80,3584]{2,1,0:T(8,128)(2,1)}, bf16[4,80,3584]{2,1,0:T(8,128)(2,1)}, u32[]{:S(2)}, u32[]{:S(2)}) collective-permute-start(bf16[4,80,3584]{2,1,0:T(8,128)(2,1)} %get-tuple-element.47), channel_id=1, source_target_pairs={{0,4},{1,5},{2,6},{3,7},{4,8},{5,9},{6,10},{7,11},{8,12},{9,13},{1... | collective-permute-start | bytes 6881288 | tf_op jit(solution)/shard_map/ppermute | solution.py:524
  579.7 62.2 %collective-permute-start.7 = (bf16[4,80,3584]{2,1,0:T(8,128)(2,1)}, bf16[4,80,3584]{2,1,0:T(8,128)(2,1)}, u32[]{:S(2)}, u32[]{:S(2)}) collective-permute-start(bf16[4,80,3584]{2,1,0:T(8,128)(2,1)} %get-tuple-element.51), channel_id=1, source_target_pairs={{0,12},{1,13},{2,14},{3,15},{4,0},{5,1},{6,2},{7,3},{8,4},{9,5},{1... | collective-permute-start | bytes 6881288 | tf_op jit(solution)/shard_map/ppermute | solution.py:524
  581.6 68.7 %collective-permute-start.8 = (bf16[4,80,3584]{2,1,0:T(8,128)(2,1)}, bf16[4,80,3584]{2,1,0:T(8,128)(2,1)}, u32[]{:S(2)}, u32[]{:S(2)}) collective-permute-start(bf16[4,80,3584]{2,1,0:T(8,128)(2,1)} %get-tuple-element.53), channel_id=1, source_target_pairs={{0,1},{1,2},{2,3},{3,0},{4,5},{5,6},{6,7},{7,4},{8,9},{9,10},{10,1... | collective-permute-start | bytes 6881288 | tf_op jit(solution)/shard_map/ppermute | solution.py:524
  581.7 68.5 %collective-permute-start.11 = (bf16[4,80,3584]{2,1,0:T(8,128)(2,1)}, bf16[4,80,3584]{2,1,0:T(8,128)(2,1)}, u32[]{:S(2)}, u32[]{:S(2)}) collective-permute-start(bf16[4,80,3584]{2,1,0:T(8,128)(2,1)} %get-tuple-element.57), channel_id=1, source_target_pairs={{0,3},{1,0},{2,1},{3,2},{4,7},{5,4},{6,5},{7,6},{8,11},{9,8},{10,9... | collective-permute-start | bytes 6881288 | tf_op jit(solution)/shard_map/ppermute | solution.py:524

commit v4 on v3

--- a/solution.py
+++ b/solution.py
@@ -11,8 +11,10 @@
 MESH = pl.DeviceIdType.MESH
 LINKS = ((0, 1), (0, -1), (1, 1), (1, -1))
 TICKS = 2
-FIRST = 6
+FIRST = 7
 VMEM = 65400 * 1024
+DEPTH = 4
+DEEP = 3
 PARTS = 3
 
 
@@ -117,6 +119,8 @@
     tiles = d // dt
     cut = tiles // 2
 
+    count = side * (side // 2) * tiles
+
     def weights(i, slot):
         part = pl.ds(pl.multiple_of(i * dt, dt), dt)
         return [
@@ -124,29 +128,35 @@
             for j, (ref, buf) in enumerate(((wg_ref, wg_t), (wu_ref, wu_t)))
         ]
 
-    for c in weights(0, 0):
-        c.start()
+    for i in range(DEPTH - 1):
+        for c in weights(i % tiles, i):
+            c.start()
     lax.fori_loop(0, FIRST, lambda s, _: (step(s), None)[1], None)
     wd_copy.wait()
 
+    local = [pl.ds(i * half, half) for i in range(4)]
+
+    def rows_of(q, p):
+        starts = []
+        for a in (2 * p, 2 * p + 1):
+            starts += [owner(-a, -q) * rows, owner(a, q) * rows + half]
+        return [pl.ds(pl.multiple_of(s, 8), half) for s in starts]
+
+    def reads(q, p):
+        return [
+            pltpu.make_async_copy(ref.at[t], buf.at[h], in_sem.at[j, i])
+            for j, (ref, buf) in enumerate(((full_ref.at[0], dy_v), (gate_ref, g_v), (up_ref, u_v)))
+            for i, (t, h) in enumerate(zip(rows_of(q, p), local))
+        ]
+
     def group(q, p):
         offsets = [2 * p, 2 * p + 1]
-        starts = []
-        for a in offsets:
-            starts += [owner(-a, -q) * rows, owner(a, q) * rows + half]
-        local = [pl.ds(i * half, half) for i in range(4)]
-        there = [pl.ds(pl.multiple_of(s, 8), half) for s in starts]
-        first = FIRST + TICKS * (q * (side // 2) + p)
+        there = rows_of(q, p)
+        which = q * (side // 2) + p
+        first = FIRST + TICKS * which
 
         step(first)
-        reads = [
-            pltpu.make_async_copy(ref.at[t], buf.at[h], in_sem.at[j, i])
-            for j, (ref, buf) in enumerate(((full_ref.at[0], dy_v), (gate_ref, g_v), (up_ref, u_v)))
-            for i, (t, h) in enumerate(zip(there, local))
-        ]
-        for c in reads:
-            c.start()
-        for c in reads:
+        for c in reads(q, p):
             c.wait()
 
         def hidden_tile(i, _):
@@ -172,6 +182,12 @@
         ]
         for c in results:
             c.start()
+        step(first + 1)
+
+        @pl.when(which + 1 < side * (side // 2))
+        def _():
+            for c in reads(q + (p + 1) // (side // 2), (p + 1) % (side // 2)):
+                c.start()
 
         def stores_of(i, slot, second, b):
             n = pl.ds(pl.multiple_of((i - second * cut) * dt, dt), dt)
@@ -202,18 +218,20 @@
             begin = cut if second else 0
 
             def body(i, _):
-                slot = i % 2
+                at_ = which * tiles + i
+                slot = at_ % DEPTH
                 for c in weights(i, slot):
                     c.wait()
 
-                @pl.when((i + 1 < tiles) | (q + 1 < side) | (p + 1 < side // 2))
+                @pl.when(at_ + DEPTH - 1 < count)
                 def _():
-                    for c in weights((i + 1) % tiles, (i + 1) % 2):
+                    for c in weights((i + DEPTH - 1) % tiles, (at_ + DEPTH - 1) % DEPTH):
                         c.start()
 
-                @pl.when(i >= begin + 2)
+                @pl.when(at_ >= DEPTH)
                 def _():
-                    for_stores(i - 2, slot, second, lambda c: c.wait())
+                    for c in stores_of(0, slot, False, q):
+                        c.wait()
 
                 nt_dims = (((1,), (1,)), ((), ()))
                 term = lax.dot_general(dg_v[...], wg_t[slot], nt_dims, preferred_element_type=jnp.float32)
@@ -221,21 +239,27 @@
                 out_t[slot] = term.astype(out_t.dtype)
                 for_stores(i, slot, second, lambda c: c.start())
 
-            end = tiles if second else cut
-            lax.fori_loop(begin, end, body, None)
-            for i in range(max(begin, end - 2), end):
-                for_stores(i, i % 2, second, lambda c: c.wait())
-
-        step(first + 1)
+            lax.fori_loop(begin, tiles if second else cut, body, None)
+
         dx_tile(False)
         dx_tile(True)
         for c in results:
             c.wait()
 
+        if p == side // 2 - 1:
+
+            @pl.when(q == side - 1)
+            def _():
+                for slot in range(DEPTH):
+                    for c in stores_of(0, slot, False, q):
+                        c.wait()
+
     def groups(q, _):
         for p in range(side // 2):
             group(q, p)
 
+    for c in reads(0, 0):
+        c.start()
     lax.fori_loop(0, side, groups, None)
     done = FIRST + TICKS * side * (side // 2)
 
@@ -244,16 +268,17 @@
     tb = tile_of(tokens, 512)
     per = -(-tiles // PARTS)
 
-    def dy_tile(i):
+    def dy_tile(i, slot):
         n = pl.ds(pl.multiple_of(i * dt, dt), dt)
-        return pltpu.make_async_copy(full_ref.at[0, :, n], dy_t.at[i % 2], dyt_sem.at[i % 2])
-
-    def dwd_tile(m, i):
+        return pltpu.make_async_copy(full_ref.at[0, :, n], dy_t.at[slot], dyt_sem.at[slot])
+
+    def dwd_tile(m, i, slot):
         n = pl.ds(pl.multiple_of(i * dt, dt), dt)
         row = pl.ds(pl.multiple_of(m * fm, fm), fm)
-        return pltpu.make_async_copy(dwd_t.at[i % 2], dwd_ref.at[row, n], dwd_sem.at[i % 2])
-
-    dy_tile(0).start()
+        return pltpu.make_async_copy(dwd_t.at[slot], dwd_ref.at[row, n], dwd_sem.at[slot])
+
+    for i in range(DEEP - 1):
+        dy_tile(i % tiles, i).start()
 
     def down(m, _):
         load = pltpu.make_async_copy(hid_ref.at[:, pl.ds(pl.multiple_of(m * fm, fm), fm)], hid_v, hid_sem)
@@ -263,19 +288,21 @@
             ht_v[:, b * tb : (b + 1) * tb] = hid_v[b * tb : (b + 1) * tb, :].T
 
         def tile(i, _):
-            dy_tile(i).wait()
-
-            @pl.when((i + 1 < tiles) | (m == 0))
+            at_ = m * tiles + i
+            slot = at_ % DEEP
+            dy_tile(i, slot).wait()
+
+            @pl.when(at_ + DEEP - 1 < 2 * tiles)
             def _():
-                dy_tile((i + 1) % tiles).start()
-
-            @pl.when((i >= 2) | (m == 1))
+                dy_tile((i + DEEP - 1) % tiles, (at_ + DEEP - 1) % DEEP).start()
+
+            @pl.when(at_ >= DEEP)
             def _():
-                dwd_tile(m, i).wait()
-
-            dw = jnp.dot(ht_v[...], dy_t[i % 2], preferred_element_type=jnp.float32)
-            dwd_t[i % 2] = dw.astype(dwd_t.dtype)
-            dwd_tile(m, i).start()
+                dwd_tile(m, i, slot).wait()
+
+            dw = jnp.dot(ht_v[...], dy_t[slot], preferred_element_type=jnp.float32)
+            dwd_t[slot] = dw.astype(dwd_t.dtype)
+            dwd_tile(m, i, slot).start()
 
         def part(k, _):
             step(done + m * PARTS + k)
@@ -284,8 +311,8 @@
         lax.fori_loop(0, PARTS, part, None)
 
     lax.fori_loop(0, 2, down, None)
-    for i in (tiles - 2, tiles - 1):
-        dwd_tile(1, i).wait()
+    for slot in range(DEEP):
+        dwd_tile(1, 0, slot).wait()
     lax.fori_loop(done + 2 * PARTS, 2 * slots, lambda s, _: (step(s), None)[1], None)
 
     def sent(slot, _):
@@ -320,22 +347,22 @@
             pltpu.VMEM((ff, d), bf16),
             pltpu.VMEM((group, d), bf16),
             *[pltpu.VMEM((group, ff), bf16)] * 5,
-            *[pltpu.VMEM((2, dt, ff), bf16)] * 2,
-            pltpu.VMEM((2, group, dt), bf16),
+            *[pltpu.VMEM((DEPTH, dt, ff), bf16)] * 2,
+            pltpu.VMEM((DEPTH, group, dt), bf16),
             pltpu.VMEM((tokens, ff // 2), bf16),
             pltpu.VMEM((ff // 2, tokens), bf16),
-            pltpu.VMEM((2, tokens, dt), bf16),
-            pltpu.VMEM((2, ff // 2, dt), bf16),
+            pltpu.VMEM((DEEP, tokens, dt), bf16),
+            pltpu.VMEM((DEEP, ff // 2, dt), bf16),
             pltpu.SemaphoreType.DMA((len(LINKS), 2 * (n - 1))),
             pltpu.SemaphoreType.DMA((len(LINKS), 2 * (n - 1))),
             pltpu.SemaphoreType.DMA,
             pltpu.SemaphoreType.DMA((3, 4)),
             pltpu.SemaphoreType.DMA((3, 4)),
-            pltpu.SemaphoreType.DMA((2, 2)),
-            pltpu.SemaphoreType.DMA((2, 4)),
+            pltpu.SemaphoreType.DMA((2, DEPTH)),
+            pltpu.SemaphoreType.DMA((DEPTH, 4)),
             pltpu.SemaphoreType.DMA,
-            pltpu.SemaphoreType.DMA((2,)),
-            pltpu.SemaphoreType.DMA((2,)),
+            pltpu.SemaphoreType.DMA((DEEP,)),
+            pltpu.SemaphoreType.DMA((DEEP,)),
         ],
         compiler_params=pltpu.CompilerParams(
             collective_id=0, has_side_effects=True, vmem_limit_bytes=VMEM

time: 703 us -> 622 us (0.88)
  Pallas kernels: 623 us -> 548 us
    pallas_call x1, Pallas kernels: 457 us -> 380 us  [gather(): pl.pallas_call(functools.partial(gather_kernel, side, dt, nt), out_shape=...]
  transfers between devices with their start and end apart: 12 -> 12, of which waited for: 3 -> 3; matrix products, arithmetic and copies ran while one was open for 0% -> 0% of each run, Pallas kernels for 18% -> 20%
where the time goes in v4:
time: 622 us; the launch traced here: 619 us
  Pallas kernels  548 us (88%)
  waiting for transfers between devices  54.6 us (9%)
  starting transfers between devices  12.3 us (2%)
    pallas_call x1, Pallas kernels, gather(): pl.pallas_call(functools.partial(gather_kernel, side, dt, nt), out_shape=...  380 us
    pallas_call x3, Pallas kernels, dw_in(): pl.pallas_call(functools.partial(dw_in_kernel, len(pairs), len(moved)), g...  126 us
    ppermute x12, waiting for transfers between devices, hop(): return lax.ppermute(v, 'tp', pairs)  54.6 us
    pallas_call x1, Pallas kernels, finish(): pl.pallas_call(functools.partial(finish_kernel, side), out_shape=jax.Shap...  42.3 us
  transfers between devices with their start and end apart: 12, of which 3 were waited for; matrix products, arithmetic and copies ran while one was open for 0% of the time, Pallas kernels for 20%

profile of v4, /device:TPU:97, one launch (start us, length us, event | category | flops | bytes accessed | tf_op | source)
XLA Modules:
  0.0 619.2 jit_solution(18298182718855661057)
XLA Ops:
  0.6 380.3 %gather_and_dx.1 = (bf16[2,2560,7168]{2,1,0:T(8,128)(2,1)}, bf16[2560,2560]{1,0:T(8,128)(2,1)}, bf16[2560,1280]{1,0:T(8,128)(2,1)}, bf16[1280,7168]{1,0:T(8,128)...) custom-call(bf16[160,7168]{1,0:T(8,128)(2,1)} %x_ref.1, ...), custom_call_target="tpu_custom_call" | custom-call | flops 187904819200 | bytes 513802240 | tf_op jit(solution)/shard_map/gather_and_dx/pallas_call | solution.py:335
  380.9 0.1 collective-permute-start
  381.0 0.1 collective-permute-start.1
  381.1 2.5 collective-permute-start.2
  383.7 2.7 collective-permute-start.3
  386.3 46.1 %collective-permute-done.refs_3_ = bf16[4,80,3584]{2,1,0:T(8,128)(2,1)} collective-permute-done((bf16[4,80,3584]{2,1,0:T(8,128)(2,1)}, bf16[4,80,3584]{2,1,0:T(8,128)(2,1)}, u32[]{:S(2)}, u32[]{:S(2)}) %collective-permute-start) | collective-permute-done | bytes 2293792 | tf_op jit(solution)/shard_map/ppermute | solution.py:551
  432.5 0.1 collective-permute-done.1.refs_5_
  432.6 0.1 collective-permute-start.9
  432.7 41.8 %dw_in.3 = (bf16[7168,1280]{1,0:T(8,128)(2,1)}, bf16[7168,1280]{1,0:T(8,128)(2,1)}) custom-call(bf16[2,2560,7168]{2,1,0:T(8,128)(2,1)} %get-tuple-element.35.refs_0_, bf16[2560,2560]{1,0:T(8,128)(2,1)} %get-tuple-element.36.refs_1_), custom_call_target="tpu_custom_call" | custom-call | flops 33554432000 | bytes 39321600 | tf_op jit(solution)/shard_map/dw_in/pallas_call | solution.py:407
  474.5 0.0 collective-permute-done.2.refs_7_
  474.5 1.4 collective-permute-start.10
  475.9 0.0 collective-permute-done.3.refs_9_
  475.9 26.4 %dw_in.4 = (bf16[7168,1280]{1,0:T(8,128)(2,1)}, bf16[7168,1280]{1,0:T(8,128)(2,1)}, bf16[4,80,3584]{2,1,0:T(8,128)(2,1)}, bf16[4,80,3584]{2,1,0:T(8,128)(2,1)}, ...) custom-call(bf16[2,2560,7168]{2,1,0:T(8,128)(2,1)} %get-tuple-element.3, ...), custom_call_target="tpu_custom_call", output_to_operand_aliasing={{0}: (10, {}), {1}: (11, {})} | custom-call | flops 13421772800 | bytes 23592960 | tf_op jit(solution)/shard_map/dw_in/pallas_call | solution.py:407
  502.3 0.5 collective-permute-start.4
  502.8 0.0 collective-permute-done.5.refs_2_
  502.8 2.2 collective-permute-start.7
  505.1 0.0 collective-permute-done.6.refs_4_
  505.1 0.1 collective-permute-start.8
  505.1 0.0 collective-permute-done.9.refs_8_
  505.1 2.6 collective-permute-start.11
  507.8 57.6 %dw_in.5 = (bf16[7168,1280]{1,0:T(8,128)(2,1)}, bf16[7168,1280]{1,0:T(8,128)(2,1)}, bf16[1280,7168]{1,0:T(8,128)(2,1)}) custom-call(bf16[2,2560,7168]{2,1,0:T(8,128)(2,1)} %get-tuple-element.35.refs_0_, bf16[2560,2560]{1,0:T(8,128)(2,1)} %get-tuple-element.36.refs_1_, ...), custom_call_target="tpu_custom_call", output_to_operand_aliasing={{0}: (3, {}), {1}: (4, {})} | custom-call | flops 46976204800 | bytes 49807360 | tf_op jit(solution)/shard_map/dw_in/pallas_call | solution.py:407
  565.3 8.4 %collective-permute-done.8.refs_7_ = bf16[4,80,3584]{2,1,0:T(8,128)(2,1)} collective-permute-done((bf16[4,80,3584]{2,1,0:T(8,128)(2,1)}, bf16[4,80,3584]{2,1,0:T(8,128)(2,1)}, u32[]{:S(2)}, u32[]{:S(2)}) %collective-permute-start.8) | collective-permute-done | bytes 2293792 | tf_op jit(solution)/shard_map/ppermute | solution.py:551
  573.7 42.3 %finish_dx.1 = bf16[160,7168]{1,0:T(8,128)(2,1)} custom-call(bf16[4,80,3584]{2,1,0:T(8,128)(2,1)} %get-tuple-element.34.refs_0_, bf16[4,80,3584]{2,1,0:T(8,128)(2,1)} %collective-permute-done.4.refs_1_, bf16[4,80,3584]{2,1,0:T(8,128)(2,1)} %collective-permute-done.5.refs_2_, bf16[4,80,3584]{2,1,0:T(8,128)(2,1)} %get-tuple-element.49.refs_3_, ...), custom_call_target="tpu_custom_call" | custom-call | flops 18350080 | bytes 29818880 | tf_op jit(solution)/shard_map/finish_dx/pallas_call | solution.py:517
  616.0 3.2 copy.20
  (6 shorter events, 0.0 us)
Async XLA Ops:
  380.9 51.6 %collective-permute-start = (bf16[4,80,3584]{2,1,0:T(8,128)(2,1)}, bf16[4,80,3584]{2,1,0:T(8,128)(2,1)}, u32[]{:S(2)}, u32[]{:S(2)}) collective-permute-start(bf16[4,80,3584]{2,1,0:T(8,128)(2,1)} %get-tuple-element.38), channel_id=1, source_target_pairs={{0,4},{1,5},{2,6},{3,7},{4,8},{5,9},{6,10},{7,11},{8,12},{9,13},{1... | collective-permute-start | bytes 6881288 | tf_op jit(solution)/shard_map/ppermute | solution.py:551
  381.0 51.6 %collective-permute-start.1 = (bf16[4,80,3584]{2,1,0:T(8,128)(2,1)}, bf16[4,80,3584]{2,1,0:T(8,128)(2,1)}, u32[]{:S(2)}, u32[]{:S(2)}) collective-permute-start(bf16[4,80,3584]{2,1,0:T(8,128)(2,1)} %get-tuple-element.40), channel_id=1, source_target_pairs={{0,1},{1,2},{2,3},{3,0},{4,5},{5,6},{6,7},{7,4},{8,9},{9,10},{10,1... | collective-permute-start | bytes 6881288 | tf_op jit(solution)/shard_map/ppermute | solution.py:551
  381.1 93.4 %collective-permute-start.2 = (bf16[4,80,3584]{2,1,0:T(8,128)(2,1)}, bf16[4,80,3584]{2,1,0:T(8,128)(2,1)}, u32[]{:S(2)}, u32[]{:S(2)}) collective-permute-start(bf16[4,80,3584]{2,1,0:T(8,128)(2,1)} %get-tuple-element.42), channel_id=1, source_target_pairs={{0,12},{1,13},{2,14},{3,15},{4,0},{5,1},{6,2},{7,3},{8,4},{9,5},{1... | collective-permute-start | bytes 6881288 | tf_op jit(solution)/shard_map/ppermute | solution.py:551
  383.7 92.2 %collective-permute-start.3 = (bf16[4,80,3584]{2,1,0:T(8,128)(2,1)}, bf16[4,80,3584]{2,1,0:T(8,128)(2,1)}, u32[]{:S(2)}, u32[]{:S(2)}) collective-permute-start(bf16[4,80,3584]{2,1,0:T(8,128)(2,1)} %get-tuple-element.44), channel_id=1, source_target_pairs={{0,3},{1,0},{2,1},{3,2},{4,7},{5,4},{6,5},{7,6},{8,11},{9,8},{10,9... | collective-permute-start | bytes 6881288 | tf_op jit(solution)/shard_map/ppermute | solution.py:551
  386.3 116.5 %collective-permute-start.5 = (bf16[4,80,3584]{2,1,0:T(8,128)(2,1)}, bf16[4,80,3584]{2,1,0:T(8,128)(2,1)}, u32[]{:S(2)}, u32[]{:S(2)}) collective-permute-start(bf16[4,80,3584]{2,1,0:T(8,128)(2,1)} %get-tuple-element.48), channel_id=1, source_target_pairs={{0,12},{1,13},{2,14},{3,15},{4,0},{5,1},{6,2},{7,3},{8,4},{9,5},{1... | collective-permute-start | bytes 6881288 | tf_op jit(solution)/shard_map/ppermute | solution.py:551
  432.5 72.6 %collective-permute-start.6 = (bf16[4,80,3584]{2,1,0:T(8,128)(2,1)}, bf16[4,80,3584]{2,1,0:T(8,128)(2,1)}, u32[]{:S(2)}, u32[]{:S(2)}) collective-permute-start(bf16[4,80,3584]{2,1,0:T(8,128)(2,1)} %get-tuple-element.50), channel_id=1, source_target_pairs={{0,4},{1,5},{2,6},{3,7},{4,8},{5,9},{6,10},{7,11},{8,12},{9,13},{1... | collective-permute-start | bytes 6881288 | tf_op jit(solution)/shard_map/ppermute | solution.py:551
  432.6 72.6 %collective-permute-start.9 = (bf16[4,80,3584]{2,1,0:T(8,128)(2,1)}, bf16[4,80,3584]{2,1,0:T(8,128)(2,1)}, u32[]{:S(2)}, u32[]{:S(2)}) collective-permute-start(bf16[4,80,3584]{2,1,0:T(8,128)(2,1)} %get-tuple-element.54), channel_id=1, source_target_pairs={{0,3},{1,0},{2,1},{3,2},{4,7},{5,4},{6,5},{7,6},{8,11},{9,8},{10,9... | collective-permute-start | bytes 6881288 | tf_op jit(solution)/shard_map/ppermute | solution.py:551
  474.5 90.8 %collective-permute-start.10 = (bf16[4,80,3584]{2,1,0:T(8,128)(2,1)}, bf16[4,80,3584]{2,1,0:T(8,128)(2,1)}, u32[]{:S(2)}, u32[]{:S(2)}) collective-permute-start(bf16[4,80,3584]{2,1,0:T(8,128)(2,1)} %get-tuple-element.56), channel_id=1, source_target_pairs={{0,1},{1,2},{2,3},{3,0},{4,5},{5,6},{6,7},{7,4},{8,9},{9,10},{10,1... | collective-permute-start | bytes 6881288 | tf_op jit(solution)/shard_map/ppermute | solution.py:551
  502.3 63.0 %collective-permute-start.4 = (bf16[4,80,3584]{2,1,0:T(8,128)(2,1)}, bf16[4,80,3584]{2,1,0:T(8,128)(2,1)}, u32[]{:S(2)}, u32[]{:S(2)}) collective-permute-start(bf16[4,80,3584]{2,1,0:T(8,128)(2,1)} %get-tuple-element.47), channel_id=1, source_target_pairs={{0,4},{1,5},{2,6},{3,7},{4,8},{5,9},{6,10},{7,11},{8,12},{9,13},{1... | collective-permute-start | bytes 6881288 | tf_op jit(solution)/shard_map/ppermute | solution.py:551
  502.8 62.5 %collective-permute-start.7 = (bf16[4,80,3584]{2,1,0:T(8,128)(2,1)}, bf16[4,80,3584]{2,1,0:T(8,128)(2,1)}, u32[]{:S(2)}, u32[]{:S(2)}) collective-permute-start(bf16[4,80,3584]{2,1,0:T(8,128)(2,1)} %get-tuple-element.51), channel_id=1, source_target_pairs={{0,12},{1,13},{2,14},{3,15},{4,0},{5,1},{6,2},{7,3},{8,4},{9,5},{1... | collective-permute-start | bytes 6881288 | tf_op jit(solution)/shard_map/ppermute | solution.py:551
  505.1 68.6 %collective-permute-start.8 = (bf16[4,80,3584]{2,1,0:T(8,128)(2,1)}, bf16[4,80,3584]{2,1,0:T(8,128)(2,1)}, u32[]{:S(2)}, u32[]{:S(2)}) collective-permute-start(bf16[4,80,3584]{2,1,0:T(8,128)(2,1)} %get-tuple-element.53), channel_id=1, source_target_pairs={{0,1},{1,2},{2,3},{3,0},{4,5},{5,6},{6,7},{7,4},{8,9},{9,10},{10,1... | collective-permute-start | bytes 6881288 | tf_op jit(solution)/shard_map/ppermute | solution.py:551
  505.1 68.6 %collective-permute-start.11 = (bf16[4,80,3584]{2,1,0:T(8,128)(2,1)}, bf16[4,80,3584]{2,1,0:T(8,128)(2,1)}, u32[]{:S(2)}, u32[]{:S(2)}) collective-permute-start(bf16[4,80,3584]{2,1,0:T(8,128)(2,1)} %get-tuple-element.57), channel_id=1, source_target_pairs={{0,3},{1,0},{2,1},{3,2},{4,7},{5,4},{6,5},{7,6},{8,11},{9,8},{10,9... | collective-permute-start | bytes 6881288 | tf_op jit(solution)/shard_map/ppermute | solution.py:551

commit v5 on v4

--- a/solution.py
+++ b/solution.py
@@ -376,7 +376,7 @@
 
 def dw_in_kernel(sums, moved, *refs):
     x_ref, d_ref, *rest = refs
-    outs = rest[len(rest) - 2 - sums - moved :]
+    outs = rest[len(rest) - 2 - 2 * sums - moved :]
     dwg_ref, dwu_ref = outs[:2]
     ff = dwg_ref.shape[1]
     dw = lax.dot_general(
@@ -386,9 +386,11 @@
     dwu_ref[...] = dw[:, ff:].astype(dwu_ref.dtype)
     for k in range(sums):
         mine, came = rest[2 * k : 2 * k + 2]
-        outs[2 + k][...] = bf16(f32(mine[...]) + f32(came[...]))
+        total = bf16(f32(mine[...]) + f32(came[...]))
+        outs[2 + 2 * k][...] = total[:1]
+        outs[3 + 2 * k][...] = total[1:]
     for k in range(moved):
-        outs[2 + sums + k][...] = rest[2 * sums + k][...]
+        outs[2 + 2 * sums + k][...] = rest[2 * sums + k][...]
 
 
 def dw_in(full, dgu, first, last, so_far=(), pairs=(), moved=()):
@@ -402,7 +404,8 @@
         lead = v.shape[:-1]
         return pl.BlockSpec((*lead, v.shape[-1] // n), lambda i: (*[0] * len(lead), i))
 
-    extra = [a for a, _ in pairs] + list(moved)
+    cut = [jax.ShapeDtypeStruct((k, *a.shape[1:]), a.dtype) for a, _ in pairs for k in (1, a.shape[0] - 1)]
+    extra = [*cut, *moved]
     new = [jax.ShapeDtypeStruct((d, ff), full.dtype)] * 2 + [jax.ShapeDtypeStruct(v.shape, v.dtype) for v in extra]
     return pl.pallas_call(
         functools.partial(dw_in_kernel, len(pairs), len(moved)),
@@ -433,8 +436,9 @@
 
 
 def finish_kernel(side, *refs):
-    ins, (out_ref, in_v, send_v, recv_v, out_v, in_sem, send_sem, recv_sem, out_sem) = refs[:12], refs[12:]
-    half, cols = out_v.shape[0] // 2, out_v.shape[1] // 2
+    ins, own, rest = refs[:12], refs[12:16], refs[16:]
+    out_ref, in_v, send_v, recv_v, own_v, in_sem, send_sem, recv_sem, own_send, own_recv = rest
+    half, cols = out_ref.shape[0] // 2, out_ref.shape[1] // 2
     me = lax.axis_index("tp")
     at = (me // side, me % side)
 
@@ -450,21 +454,24 @@
     order = (((2, 0), (2, 1)), ((1, 1), (3, 0)), ((1, 0), (3, 1)))
 
     def loads(h, j, r):
-        return [
-            pltpu.make_async_copy(ins[6 * h + 3 * r + k].at[j], in_v.at[h, j, r, k], in_sem.at[h, j, r, k])
-            for k in range(3)
-        ]
-
-    pieces = [p for step in order for p in step] + [(0, 0), (0, 1)]
-    for j, r in pieces:
-        for h in range(2):
-            for c in loads(h, j, r):
-                c.start()
-
-    def piece(h, j, r):
-        for c in loads(h, j, r):
-            c.wait()
-        return f32(in_v[h, j, r, 0]) + f32(in_v[h, j, r, 1]) + f32(in_v[h, j, r, 2])
+        copies = []
+        for k in range(3):
+            late = k == 1 + r
+            if late and j == 0:
+                continue
+            src = ins[6 * h + 3 * r + k].at[j - 1 if late else j]
+            copies.append(pltpu.make_async_copy(src, in_v.at[h, j, r, k], in_sem.at[h, j, r, k]))
+        return copies
+
+    def own_message(h, way):
+        return pltpu.make_async_remote_copy(
+            src_ref=own[2 * h + way].at[0],
+            dst_ref=own_v.at[h, way],
+            send_sem=own_send.at[h, way],
+            recv_sem=own_recv.at[h, way],
+            device_id=neighbour(h, 1 - 2 * way),
+            device_id_type=MESH,
+        )
 
     def message(h, step, way):
         return pltpu.make_async_remote_copy(
@@ -476,7 +483,27 @@
             device_id_type=MESH,
         )
 
-    ready = False
+    def piece(h, j, r):
+        for c in loads(h, j, r):
+            c.wait()
+        total = f32(in_v[h, j, r, 0])
+        for k in (1, 2):
+            if k == 1 + r and j == 0:
+                own_message(h, r).wait_recv()
+                total += f32(own_v[h, r])
+            else:
+                total += f32(in_v[h, j, r, k])
+        return total
+
+    pieces = [p for step in order for p in step] + [(0, 0), (0, 1)]
+    for j, r in pieces:
+        for h in range(2):
+            for c in loads(h, j, r):
+                c.start()
+    pl.semaphore_wait(barrier, len(LINKS))
+    for h in range(2):
+        for way in range(2):
+            own_message(h, way).start()
     for step, steps in enumerate(order):
         for h in range(2):
             for way, (j, r) in enumerate(steps):
@@ -485,58 +512,50 @@
                     message(h, 0, way).wait_recv()
                     total += f32(recv_v[h, 0, way])
                 send_v[h, step, way] = bf16(total)
-                if not ready:
-                    pl.semaphore_wait(barrier, len(LINKS))
-                    ready = True
                 message(h, step, way).start()
-    stores = []
-    for step in (1, 2):
-        for h in range(2):
-            for way in range(2):
-                message(h, step, way).wait_recv()
     for h in range(2):
         for r in range(2):
             total = piece(h, 0, r)
-            total += f32(recv_v[h, 2 if r == 0 else 1, 0]) + f32(recv_v[h, 1 if r == 0 else 2, 1])
-            part = (pl.ds(r * half, half), pl.ds(h * cols, cols))
-            out_v[part] = bf16(total)
-            stores.append(pltpu.make_async_copy(out_v.at[part], out_ref.at[part], out_sem.at[h, r]))
-            stores[-1].start()
-    for c in stores:
-        c.wait()
-    for step in range(3):
-        for h in range(2):
-            for way in range(2):
+            message(h, 1, 1 - r).wait_recv()
+            total += f32(recv_v[h, 1, 1 - r])
+            message(h, 2, r).wait_recv()
+            total += f32(recv_v[h, 2, r])
+            out_ref[r * half : (r + 1) * half, h * cols : (h + 1) * cols] = bf16(total)
+    for h in range(2):
+        for way in range(2):
+            own_message(h, way).wait_send()
+            for step in range(3):
                 message(h, step, way).wait_send()
 
 
-def finish(side, ins):
+def finish(side, ins, own):
     _, half, cols = ins[0].shape
-    anywhere = pl.BlockSpec(memory_space=pltpu.HBM)
+    hbm = pl.BlockSpec(memory_space=pltpu.HBM)
     dtype = jnp.bfloat16
     return pl.pallas_call(
         functools.partial(finish_kernel, side),
-        out_shape=jax.ShapeDtypeStruct((2 * half, 2 * cols), dtype),
-        in_specs=[anywhere] * len(ins),
-        out_specs=anywhere,
+        out_shape=pltpu.VMEM((2 * half, 2 * cols), dtype),
+        in_specs=[hbm] * (len(ins) + len(own)),
+        out_specs=pl.BlockSpec(memory_space=pltpu.VMEM),
         scratch_shapes=[
             pltpu.VMEM((2, side, 2, 3, half, cols), dtype),
             pltpu.VMEM((2, 3, 2, half, cols), dtype),
             pltpu.VMEM((2, 3, 2, half, cols), dtype),
-            pltpu.VMEM((2 * half, 2 * cols), dtype),
+            pltpu.VMEM((2, 2, half, cols), dtype),
             pltpu.SemaphoreType.DMA((2, side, 2, 3)),
             pltpu.SemaphoreType.DMA((2, 3, 2)),
             pltpu.SemaphoreType.DMA((2, 3, 2)),
             pltpu.SemaphoreType.DMA((2, 2)),
+            pltpu.SemaphoreType.DMA((2, 2)),
         ],
         compiler_params=pltpu.CompilerParams(
-            collective_id=1, has_side_effects=True, vmem_limit_bytes=VMEM
+            collective_id=1, has_side_effects=True, vmem_limit_bytes=54 * 1024 * 1024
         ),
         cost_estimate=pl.CostEstimate(
             flops=64 * half * cols, bytes_accessed=2 * 52 * half * cols, transcendentals=0
         ),
         name="finish_dx",
-    )(*ins)
+    )(*ins, *own)
 
 
 def solution(mesh):
@@ -559,13 +578,13 @@
         raw = [(hop(v[1][1], h, 1), hop(v[3][0], h, -1)) for h, v in enumerate(t)]
         dw = dw_in(full, dgu, cuts[0], cuts[1])
         pairs = [(v[1][0], f[0]) for v, f in zip(t, far)] + [(v[3][1], f[1]) for v, f in zip(t, far)]
-        *dw, a, b, c, d = dw_in(full, dgu, cuts[1], cuts[2], dw, pairs)
+        *dw, a0, a, b0, b, c0, c, d0, d = dw_in(full, dgu, cuts[1], cuts[2], dw, pairs)
         near = [(hop(up_, h, 1), hop(down, h, -1)) for h, (up_, down) in enumerate(((a, c), (b, d)))]
         *dw, dw_down = dw_in(full, dgu, cuts[2], cuts[3], dw, moved=[dw_down])
         ins = []
         for v, r, n in zip(t, raw, near):
             ins += [v[0][0], n[0], r[1], v[0][1], r[0], n[1]]
-        dx = finish(side, ins)
+        dx = finish(side, ins, [a0, c0, b0, d0])
         return dx, *dw, dw_down
 
     rows, both, cols = P(("dp", "tp"), None), P("dp", "tp"), P(None, "tp")

time: 622 us -> 621 us (level)
  Pallas kernels: 548 us -> 558 us
  waiting for transfers between devices: 54.6 us -> 46.2 us
    pallas_call x1, Pallas kernels: 42.3 us -> 51.8 us  [finish(): pl.pallas_call(functools.partial(finish_kernel, side), out_shape=pltpu.VM...]
    ppermute x12, waiting for transfers between devices: 54.6 us -> 46.2 us  [hop(): return lax.ppermute(v, 'tp', pairs)]
  transfers between devices with their start and end apart: 12 -> 12, of which waited for: 3 -> 2; matrix products, arithmetic and copies ran while one was open for 0% -> 0% of each run, Pallas kernels for 20% -> 20%
where the time goes in v5:
time: 621 us; the launch traced here: 618 us
  Pallas kernels  558 us (90%)
  waiting for transfers between devices  46.2 us (7%)
  starting transfers between devices  12.3 us (2%)
    pallas_call x1, Pallas kernels, gather(): pl.pallas_call(functools.partial(gather_kernel, side, dt, nt), out_shape=...  380 us
    pallas_call x3, Pallas kernels, dw_in(): pl.pallas_call(functools.partial(dw_in_kernel, len(pairs), len(moved)), g...  126 us
    pallas_call x1, Pallas kernels, finish(): pl.pallas_call(functools.partial(finish_kernel, side), out_shape=pltpu.VM...  51.8 us
    ppermute x12, waiting for transfers between devices, hop(): return lax.ppermute(v, 'tp', pairs)  46.2 us
  transfers between devices with their start and end apart: 12, of which 2 were waited for; matrix products, arithmetic and copies ran while one was open for 0% of the time, Pallas kernels for 20%

profile of v5, /device:TPU:97, one launch (start us, length us, event | category | flops | bytes accessed | tf_op | source)
XLA Modules:
  0.0 618.4 jit_solution(93417859371152445)
XLA Ops:
  0.6 380.3 %gather_and_dx.1 = (bf16[2,2560,7168]{2,1,0:T(8,128)(2,1)}, bf16[2560,2560]{1,0:T(8,128)(2,1)}, bf16[2560,1280]{1,0:T(8,128)(2,1)}, bf16[1280,7168]{1,0:T(8,128)...) custom-call(bf16[160,7168]{1,0:T(8,128)(2,1)} %x_ref.1, ...), custom_call_target="tpu_custom_call" | custom-call | flops 187904819200 | bytes 513802240 | tf_op jit(solution)/shard_map/gather_and_dx/pallas_call | solution.py:335
  380.9 0.1 collective-permute-start
  381.0 0.1 collective-permute-start.1
  381.1 2.5 collective-permute-start.2
  383.7 2.7 collective-permute-start.3
  386.3 46.1 %collective-permute-done.refs_3_ = bf16[4,80,3584]{2,1,0:T(8,128)(2,1)} collective-permute-done((bf16[4,80,3584]{2,1,0:T(8,128)(2,1)}, bf16[4,80,3584]{2,1,0:T(8,128)(2,1)}, u32[]{:S(2)}, u32[]{:S(2)}) %collective-permute-start) | collective-permute-done | bytes 2293792 | tf_op jit(solution)/shard_map/ppermute | solution.py:570
  432.5 0.1 collective-permute-done.1.refs_5_
  432.6 0.1 collective-permute-start.9
  432.7 41.8 %dw_in.3 = (bf16[7168,1280]{1,0:T(8,128)(2,1)}, bf16[7168,1280]{1,0:T(8,128)(2,1)}) custom-call(bf16[2,2560,7168]{2,1,0:T(8,128)(2,1)} %get-tuple-element.39.refs_0_, bf16[2560,2560]{1,0:T(8,128)(2,1)} %get-tuple-element.40.refs_1_), custom_call_target="tpu_custom_call" | custom-call | flops 33554432000 | bytes 39321600 | tf_op jit(solution)/shard_map/dw_in/pallas_call | solution.py:410
  474.5 0.0 collective-permute-done.2.refs_7_
  474.5 1.4 collective-permute-start.10
  475.9 0.0 collective-permute-done.3.refs_9_
  475.9 26.2 %dw_in.4 = (bf16[7168,1280]{1,0:T(8,128)(2,1)}, bf16[7168,1280]{1,0:T(8,128)(2,1)}, bf16[1,80,3584]{2,1,0:T(8,128)(2,1)}, bf16[3,80,3584]{2,1,0:T(8,128)(2,1)}, ...) custom-call(bf16[2,2560,7168]{2,1,0:T(8,128)(2,1)} %get-tuple-elemen, ...), custom_call_target="tpu_custom_call", output_to_operand_aliasing={{0}: (10, {}), {1}: (11, {})} | custom-call | flops 13421772800 | bytes 23592960 | tf_op jit(solution)/shard_map/dw_in/pallas_call | solution.py:410
  502.1 0.5 collective-permute-start.4
  502.6 0.0 collective-permute-done.5.refs_2_
  502.6 2.2 collective-permute-start.7
  504.9 0.1 collective-permute-start.8
  504.9 0.0 collective-permute-done.9.refs_8_
  504.9 2.6 collective-permute-start.11
  507.5 57.6 %dw_in.5 = (bf16[7168,1280]{1,0:T(8,128)(2,1)}, bf16[7168,1280]{1,0:T(8,128)(2,1)}, bf16[1280,7168]{1,0:T(8,128)(2,1)}) custom-call(bf16[2,2560,7168]{2,1,0:T(8,128)(2,1)} %get-tuple-element.39.refs_0_, bf16[2560,2560]{1,0:T(8,128)(2,1)} %get-tuple-element.40.refs_1_, ...), custom_call_target="tpu_custom_call", output_to_operand_aliasing={{0}: (3, {}), {1}: (4, {})} | custom-call | flops 46976204800 | bytes 49807360 | tf_op jit(solution)/shard_map/dw_in/pallas_call | solution.py:410
  565.1 0.0 collective-permute-done.7.refs_5_
  565.1 0.0 collective-permute-done.8.refs_7_
  565.1 51.8 %finish_dx.1 = bf16[160,7168]{1,0:T(8,128)(2,1)S(1)} custom-call(bf16[4,80,3584]{2,1,0:T(8,128)(2,1)} %get-tuple-element.38.refs_0_, bf16[3,80,3584]{2,1,0:T(8,128)(2,1)} %collective-permute-done.4.refs_1_, bf16[4,80,3584]{2,1,0:T(8,128)(2,1)} %collective-permute-done.5.refs_2_, bf16[4,80,3584]{2,1,0:T(8,128)(2,1)} %get-tuple-element.53.refs_3_, ...), custom_call_target="tpu_custom_call" | custom-call | flops 18350080 | bytes 29818880 | tf_op jit(solution)/shard_map/finish_dx/pallas_call | solution.py:535
  617.0 1.4 copy.20
  (6 shorter events, 0.0 us)
Async XLA Ops:
  380.9 51.6 %collective-permute-start = (bf16[4,80,3584]{2,1,0:T(8,128)(2,1)}, bf16[4,80,3584]{2,1,0:T(8,128)(2,1)}, u32[]{:S(2)}, u32[]{:S(2)}) collective-permute-start(bf16[4,80,3584]{2,1,0:T(8,128)(2,1)} %get-tuple-element.42), channel_id=1, source_target_pairs={{0,4},{1,5},{2,6},{3,7},{4,8},{5,9},{6,10},{7,11},{8,12},{9,13},{1... | collective-permute-start | bytes 6881288 | tf_op jit(solution)/shard_map/ppermute | solution.py:570
  381.0 51.6 %collective-permute-start.1 = (bf16[4,80,3584]{2,1,0:T(8,128)(2,1)}, bf16[4,80,3584]{2,1,0:T(8,128)(2,1)}, u32[]{:S(2)}, u32[]{:S(2)}) collective-permute-start(bf16[4,80,3584]{2,1,0:T(8,128)(2,1)} %get-tuple-element.44), channel_id=1, source_target_pairs={{0,1},{1,2},{2,3},{3,0},{4,5},{5,6},{6,7},{7,4},{8,9},{9,10},{10,1... | collective-permute-start | bytes 6881288 | tf_op jit(solution)/shard_map/ppermute | solution.py:570
  381.1 93.4 %collective-permute-start.2 = (bf16[4,80,3584]{2,1,0:T(8,128)(2,1)}, bf16[4,80,3584]{2,1,0:T(8,128)(2,1)}, u32[]{:S(2)}, u32[]{:S(2)}) collective-permute-start(bf16[4,80,3584]{2,1,0:T(8,128)(2,1)} %get-tuple-element.46), channel_id=1, source_target_pairs={{0,12},{1,13},{2,14},{3,15},{4,0},{5,1},{6,2},{7,3},{8,4},{9,5},{1... | collective-permute-start | bytes 6881288 | tf_op jit(solution)/shard_map/ppermute | solution.py:570
  383.7 92.2 %collective-permute-start.3 = (bf16[4,80,3584]{2,1,0:T(8,128)(2,1)}, bf16[4,80,3584]{2,1,0:T(8,128)(2,1)}, u32[]{:S(2)}, u32[]{:S(2)}) collective-permute-start(bf16[4,80,3584]{2,1,0:T(8,128)(2,1)} %get-tuple-element.48), channel_id=1, source_target_pairs={{0,3},{1,0},{2,1},{3,2},{4,7},{5,4},{6,5},{7,6},{8,11},{9,8},{10,9... | collective-permute-start | bytes 6881288 | tf_op jit(solution)/shard_map/ppermute | solution.py:570
  386.3 116.3 %collective-permute-start.5 = (bf16[4,80,3584]{2,1,0:T(8,128)(2,1)}, bf16[4,80,3584]{2,1,0:T(8,128)(2,1)}, u32[]{:S(2)}, u32[]{:S(2)}) collective-permute-start(bf16[4,80,3584]{2,1,0:T(8,128)(2,1)} %get-tuple-element.52), channel_id=1, source_target_pairs={{0,12},{1,13},{2,14},{3,15},{4,0},{5,1},{6,2},{7,3},{8,4},{9,5},{1... | collective-permute-start | bytes 6881288 | tf_op jit(solution)/shard_map/ppermute | solution.py:570
  432.5 72.4 %collective-permute-start.6 = (bf16[4,80,3584]{2,1,0:T(8,128)(2,1)}, bf16[4,80,3584]{2,1,0:T(8,128)(2,1)}, u32[]{:S(2)}, u32[]{:S(2)}) collective-permute-start(bf16[4,80,3584]{2,1,0:T(8,128)(2,1)} %get-tuple-element.54), channel_id=1, source_target_pairs={{0,4},{1,5},{2,6},{3,7},{4,8},{5,9},{6,10},{7,11},{8,12},{9,13},{1... | collective-permute-start | bytes 6881288 | tf_op jit(solution)/shard_map/ppermute | solution.py:570
  432.6 72.4 %collective-permute-start.9 = (bf16[4,80,3584]{2,1,0:T(8,128)(2,1)}, bf16[4,80,3584]{2,1,0:T(8,128)(2,1)}, u32[]{:S(2)}, u32[]{:S(2)}) collective-permute-start(bf16[4,80,3584]{2,1,0:T(8,128)(2,1)} %get-tuple-element.58), channel_id=1, source_target_pairs={{0,3},{1,0},{2,1},{3,2},{4,7},{5,4},{6,5},{7,6},{8,11},{9,8},{10,9... | collective-permute-start | bytes 6881288 | tf_op jit(solution)/shard_map/ppermute | solution.py:570
  474.5 90.6 %collective-permute-start.10 = (bf16[4,80,3584]{2,1,0:T(8,128)(2,1)}, bf16[4,80,3584]{2,1,0:T(8,128)(2,1)}, u32[]{:S(2)}, u32[]{:S(2)}) collective-permute-start(bf16[4,80,3584]{2,1,0:T(8,128)(2,1)} %get-tuple-element.60), channel_id=1, source_target_pairs={{0,1},{1,2},{2,3},{3,0},{4,5},{5,6},{6,7},{7,4},{8,9},{9,10},{10,1... | collective-permute-start | bytes 6881288 | tf_op jit(solution)/shard_map/ppermute | solution.py:570
  502.1 63.0 %collective-permute-start.4 = (bf16[3,80,3584]{2,1,0:T(8,128)(2,1)}, bf16[3,80,3584]{2,1,0:T(8,128)(2,1)}, u32[]{:S(2)}, u32[]{:S(2)}) collective-permute-start(bf16[3,80,3584]{2,1,0:T(8,128)(2,1)} %get-tuple-element.51), channel_id=1, source_target_pairs={{0,4},{1,5},{2,6},{3,7},{4,8},{5,9},{6,10},{7,11},{8,12},{9,13},{1... | collective-permute-start | bytes 5160968 | tf_op jit(solution)/shard_map/ppermute | solution.py:570
  502.6 62.5 %collective-permute-start.7 = (bf16[3,80,3584]{2,1,0:T(8,128)(2,1)}, bf16[3,80,3584]{2,1,0:T(8,128)(2,1)}, u32[]{:S(2)}, u32[]{:S(2)}) collective-permute-start(bf16[3,80,3584]{2,1,0:T(8,128)(2,1)} %get-tuple-element.55), channel_id=1, source_target_pairs={{0,12},{1,13},{2,14},{3,15},{4,0},{5,1},{6,2},{7,3},{8,4},{9,5},{1... | collective-permute-start | bytes 5160968 | tf_op jit(solution)/shard_map/ppermute | solution.py:570
  504.9 60.3 %collective-permute-start.8 = (bf16[3,80,3584]{2,1,0:T(8,128)(2,1)}, bf16[3,80,3584]{2,1,0:T(8,128)(2,1)}, u32[]{:S(2)}, u32[]{:S(2)}) collective-permute-start(bf16[3,80,3584]{2,1,0:T(8,128)(2,1)} %get-tuple-element.57), channel_id=1, source_target_pairs={{0,1},{1,2},{2,3},{3,0},{4,5},{5,6},{6,7},{7,4},{8,9},{9,10},{10,1... | collective-permute-start | bytes 5160968 | tf_op jit(solution)/shard_map/ppermute | solution.py:570
  504.9 60.2 %collective-permute-start.11 = (bf16[3,80,3584]{2,1,0:T(8,128)(2,1)}, bf16[3,80,3584]{2,1,0:T(8,128)(2,1)}, u32[]{:S(2)}, u32[]{:S(2)}) collective-permute-start(bf16[3,80,3584]{2,1,0:T(8,128)(2,1)} %get-tuple-element.61), channel_id=1, source_target_pairs={{0,3},{1,0},{2,1},{3,2},{4,7},{5,4},{6,5},{7,6},{8,11},{9,8},{10,9... | collective-permute-start | bytes 5160968 | tf_op jit(solution)/shard_map/ppermute | solution.py:570

commit v6 on v5

--- a/solution.py
+++ b/solution.py
@@ -399,6 +399,7 @@
     bd = tile_of(d, 256)
     n = last - first
     flat = [v for pair in pairs for v in pair]
+    resident = 2 * dgu.size
 
     def along(v):
         lead = v.shape[:-1]
@@ -413,13 +414,13 @@
         out_shape=new,
         in_specs=[
             pl.BlockSpec((pl.squeezed, tokens, bd), lambda i: (1, 0, i + first)),
-            pl.BlockSpec((tokens, 2 * ff), lambda i: (0, 0), pipeline_mode=pl.Buffered(1)),
+            pl.BlockSpec(memory_space=pltpu.VMEM),
             *[along(v) for v in (*flat, *moved)],
             *[pl.BlockSpec(memory_space=pltpu.HBM)] * len(so_far),
         ],
         out_specs=[*[pl.BlockSpec((bd, ff), lambda i: (i + first, 0))] * 2, *[along(v) for v in extra]],
         input_output_aliases={2 + len(flat) + len(moved) + i: i for i in range(len(so_far))},
-        compiler_params=pltpu.CompilerParams(vmem_limit_bytes=VMEM),
+        compiler_params=pltpu.CompilerParams(vmem_limit_bytes=VMEM - resident - 65536),
         cost_estimate=pl.CostEstimate(
             flops=4 * tokens * n * bd * ff, bytes_accessed=2 * (tokens * n * bd + 2 * ff * (tokens + n * bd)), transcendentals=0
         ),
@@ -572,15 +573,16 @@
     def device_step(x, dy, gate, up, w_gate, w_up, w_down):
         full, dgu, _, dw_down, *terms = gather(side, x, dy, gate, up, w_gate, w_up, w_down)
         t = [[terms[2 * (h * side + k) :][:2] for k in range(side)] for h in range(2)]
+        dgu = pltpu.with_memory_space_constraint(dgu, pltpu.VMEM)
         blocks = x.shape[1] // tile_of(x.shape[1], 256)
-        cuts = [0, blocks * 10 // 28, blocks * 14 // 28, blocks]
+        cuts = [0, blocks * 14 // 28, blocks * 18 // 28, blocks]
         far = [(hop(v[2][0], h, 1), hop(v[2][1], h, -1)) for h, v in enumerate(t)]
         raw = [(hop(v[1][1], h, 1), hop(v[3][0], h, -1)) for h, v in enumerate(t)]
-        dw = dw_in(full, dgu, cuts[0], cuts[1])
+        *dw, dw_down = dw_in(full, dgu, cuts[0], cuts[1], moved=[dw_down])
         pairs = [(v[1][0], f[0]) for v, f in zip(t, far)] + [(v[3][1], f[1]) for v, f in zip(t, far)]
         *dw, a0, a, b0, b, c0, c, d0, d = dw_in(full, dgu, cuts[1], cuts[2], dw, pairs)
         near = [(hop(up_, h, 1), hop(down, h, -1)) for h, (up_, down) in enumerate(((a, c), (b, d)))]
-        *dw, dw_down = dw_in(full, dgu, cuts[2], cuts[3], dw, moved=[dw_down])
+        dw = dw_in(full, dgu, cuts[2], cuts[3], dw)
         ins = []
         for v, r, n in zip(t, raw, near):
             ins += [v[0][0], n[0], r[1], v[0][1], r[0], n[1]]

time: 621 us -> 636 us (1.024)
  waiting for transfers between devices: 46.2 us -> 68.4 us
  Pallas kernels: 558 us -> 546 us
  local copies, waits for them, and re-layouts: 1.39 us -> 7.92 us
    ppermute x12, waiting for transfers between devices: 46.2 us -> 68.4 us  [hop(): return lax.ppermute(v, 'tp', pairs)]
    pallas_call x3, Pallas kernels: 126 us -> 113 us  [dw_in(): pl.pallas_call(functools.partial(dw_in_kernel, len(pairs), len(moved)), g...]
    unnamed x1 -> x7, local copies, waits for them, and re-layouts: 1.39 us -> 7.92 us
  transfers between devices with their start and end apart: 12 -> 12, of which waited for: 2 -> 3; matrix products, arithmetic and copies ran while one was open for 0% -> 0% of each run, Pallas kernels for 20% -> 18%
where the time goes in v6:
time: 636 us; the launch traced here: 634 us
  Pallas kernels  546 us (86%)
  waiting for transfers between devices  68.4 us (11%)
  starting transfers between devices  11.1 us (2%)
  local copies, waits for them, and re-layouts  7.92 us (1%)
    pallas_call x1, Pallas kernels, gather(): pl.pallas_call(functools.partial(gather_kernel, side, dt, nt), out_shape=...  380 us
    pallas_call x3, Pallas kernels, dw_in(): pl.pallas_call(functools.partial(dw_in_kernel, len(pairs), len(moved)), g...  113 us
    ppermute x12, waiting for transfers between devices, hop(): return lax.ppermute(v, 'tp', pairs)  68.4 us
    pallas_call x1, Pallas kernels, finish(): pl.pallas_call(functools.partial(finish_kernel, side), out_shape=pltpu.VM...  52.6 us
  transfers between devices with their start and end apart: 12, of which 3 were waited for; matrix products, arithmetic and copies ran while one was open for 0% of the time, Pallas kernels for 18%

profile of v6, /device:TPU:97, one launch (start us, length us, event | category | flops | bytes accessed | tf_op | source)
XLA Modules:
  0.0 634.1 jit_solution(11150450425990268313)
XLA Ops:
  0.6 380.3 %gather_and_dx.1 = (bf16[2,2560,7168]{2,1,0:T(8,128)(2,1)}, bf16[2560,2560]{1,0:T(8,128)(2,1)}, bf16[2560,1280]{1,0:T(8,128)(2,1)}, bf16[1280,7168]{1,0:T(8,128)...) custom-call(bf16[160,7168]{1,0:T(8,128)(2,1)} %x_ref.1, ...), custom_call_target="tpu_custom_call" | custom-call | flops 187904819200 | bytes 513802240 | tf_op jit(solution)/shard_map/gather_and_dx/pallas_call | solution.py:335
  380.9 0.1 collective-permute-start
  381.0 0.1 collective-permute-start.1
  381.1 2.5 collective-permute-start.2
  383.7 2.7 collective-permute-start.3
  386.3 46.0 %collective-permute-done.refs_3_ = bf16[4,80,3584]{2,1,0:T(8,128)(2,1)S(1)} collective-permute-done((bf16[4,80,3584]{2,1,0:T(8,128)(2,1)}, bf16[4,80,3584]{2,1,0:T(8,128)(2,1)S(1)}, u32[]{:S(2)}, u32[]{:S(2)}) %collective-permute-start) | collective-permute-done | bytes 2293792 | tf_op jit(solution)/shard_map/ppermute | solution.py:571
  432.4 0.1 collective-permute-done.1.refs_5_
  432.5 0.2 collective-permute-start.9
  432.7 1.1 copy-done.1
  433.7 0.7 copy-done.2
  434.5 4.7 copy-done
  439.2 53.5 %dw_in.3 = (bf16[7168,1280]{1,0:T(8,128)(2,1)}, bf16[7168,1280]{1,0:T(8,128)(2,1)}, bf16[1280,7168]{1,0:T(8,128)(2,1)}) custom-call(bf16[2,2560,7168]{2,1,0:T(8,128)(2,1)} %get-tuple-element.39.refs_0_, bf16[2560,2560]{1,0:T(8,128)(2,1)S(1)} %copy-done, bf16[1280,7168]{1,0:T(8,128)(2,1)} %get-tuple-element.49.refs_2_), custom_call_target="tpu_custom_call" | custom-call | flops 46976204800 | bytes 49807360 | tf_op jit(solution)/shard_map/dw_in/pallas_call | solution.py:411
  492.7 0.0 collective-permute-start.10
  492.7 21.6 %dw_in.4 = (bf16[7168,1280]{1,0:T(8,128)(2,1)}, bf16[7168,1280]{1,0:T(8,128)(2,1)}, bf16[1,80,3584]{2,1,0:T(8,128)(2,1)}, bf16[3,80,3584]{2,1,0:T(8,128)(2,1)}, ...) custom-call(bf16[2,2560,7168]{2,1,0:T(8,128)(2,1)} %get-tuple-elemen, ...), custom_call_target="tpu_custom_call", output_to_operand_aliasing={{0}: (10, {}), {1}: (11, {})} | custom-call | flops 13421772800 | bytes 23592960 | tf_op jit(solution)/shard_map/dw_in/pallas_call | solution.py:411
  514.4 0.1 collective-permute-start.4
  514.5 0.0 collective-permute-done.5.refs_2_
  514.5 2.6 collective-permute-start.7
  517.1 0.0 collective-permute-done.6.refs_4_
  517.1 0.8 collective-permute-start.8
  518.0 1.9 collective-permute-start.11
  519.8 38.0 %dw_in.5 = (bf16[7168,1280]{1,0:T(8,128)(2,1)}, bf16[7168,1280]{1,0:T(8,128)(2,1)}) custom-call(bf16[2,2560,7168]{2,1,0:T(8,128)(2,1)} %get-tuple-element.39.refs_0_, bf16[2560,2560]{1,0:T(8,128)(2,1)S(1)} %copy-done, bf16[7168,1280]{1,0:T(8,128)(2,1)} %get-tuple-element.67.refs_2_, ...), custom_call_target="tpu_custom_call", output_to_operand_aliasing={{0}: (2, {}), {1}: (3, {})} | custom-call | flops 33554432000 | bytes 39321600 | tf_op jit(solution)/shard_map/dw_in/pallas_call | solution.py:411
  557.9 22.3 %collective-permute-done.8.refs_7_ = bf16[3,80,3584]{2,1,0:T(8,128)(2,1)} collective-permute-done((bf16[3,80,3584]{2,1,0:T(8,128)(2,1)}, bf16[3,80,3584]{2,1,0:T(8,128)(2,1)}, u32[]{:S(2)}, u32[]{:S(2)}) %collective-permute-start.8) | collective-permute-done | bytes 1720352 | tf_op jit(solution)/shard_map/ppermute | solution.py:571
  580.2 52.6 %finish_dx.1 = bf16[160,7168]{1,0:T(8,128)(2,1)S(1)} custom-call(bf16[4,80,3584]{2,1,0:T(8,128)(2,1)} %get-tuple-element.38.refs_0_, bf16[3,80,3584]{2,1,0:T(8,128)(2,1)} %collective-permute-done.4.refs_1_, bf16[4,80,3584]{2,1,0:T(8,128)(2,1)} %collective-permute-done.5.refs_2_, bf16[4,80,3584]{2,1,0:T(8,128)(2,1)} %get-tuple-element.54.refs_3_, ...), custom_call_target="tpu_custom_call" | custom-call | flops 18350080 | bytes 29818880 | tf_op jit(solution)/shard_map/finish_dx/pallas_call | solution.py:536
  632.7 1.4 copy.20
  (12 shorter events, 0.0 us)
Async XLA Ops:
  380.9 51.4 %collective-permute-start = (bf16[4,80,3584]{2,1,0:T(8,128)(2,1)}, bf16[4,80,3584]{2,1,0:T(8,128)(2,1)S(1)}, u32[]{:S(2)}, u32[]{:S(2)}) collective-permute-start(bf16[4,80,3584]{2,1,0:T(8,128)(2,1)} %get-tuple-element.42), channel_id=1, source_target_pairs={{0,4},{1,5},{2,6},{3,7},{4,8},{5,9},{6,10},{7,11},{8,12},{9,13},{1... | collective-permute-start | bytes 6881288 | tf_op jit(solution)/shard_map/ppermute | solution.py:571
  381.0 51.4 %collective-permute-start.1 = (bf16[4,80,3584]{2,1,0:T(8,128)(2,1)}, bf16[4,80,3584]{2,1,0:T(8,128)(2,1)S(1)}, u32[]{:S(2)}, u32[]{:S(2)}) collective-permute-start(bf16[4,80,3584]{2,1,0:T(8,128)(2,1)} %get-tuple-element.44), channel_id=1, source_target_pairs={{0,1},{1,2},{2,3},{3,0},{4,5},{5,6},{6,7},{7,4},{8,9},{9,10},{10,1... | collective-permute-start | bytes 6881288 | tf_op jit(solution)/shard_map/ppermute | solution.py:571
  381.1 111.6 %collective-permute-start.2 = (bf16[4,80,3584]{2,1,0:T(8,128)(2,1)}, bf16[4,80,3584]{2,1,0:T(8,128)(2,1)}, u32[]{:S(2)}, u32[]{:S(2)}) collective-permute-start(bf16[4,80,3584]{2,1,0:T(8,128)(2,1)} %get-tuple-element.46), channel_id=1, source_target_pairs={{0,12},{1,13},{2,14},{3,15},{4,0},{5,1},{6,2},{7,3},{8,4},{9,5},{1... | collective-permute-start | bytes 6881288 | tf_op jit(solution)/shard_map/ppermute | solution.py:571
  383.7 109.1 %collective-permute-start.3 = (bf16[4,80,3584]{2,1,0:T(8,128)(2,1)}, bf16[4,80,3584]{2,1,0:T(8,128)(2,1)}, u32[]{:S(2)}, u32[]{:S(2)}) collective-permute-start(bf16[4,80,3584]{2,1,0:T(8,128)(2,1)} %get-tuple-element.48), channel_id=1, source_target_pairs={{0,3},{1,0},{2,1},{3,2},{4,7},{5,4},{6,5},{7,6},{8,11},{9,8},{10,9... | collective-permute-start | bytes 6881288 | tf_op jit(solution)/shard_map/ppermute | solution.py:571
  386.3 128.1 %collective-permute-start.5 = (bf16[4,80,3584]{2,1,0:T(8,128)(2,1)}, bf16[4,80,3584]{2,1,0:T(8,128)(2,1)}, u32[]{:S(2)}, u32[]{:S(2)}) collective-permute-start(bf16[4,80,3584]{2,1,0:T(8,128)(2,1)} %get-tuple-element.53), channel_id=1, source_target_pairs={{0,12},{1,13},{2,14},{3,15},{4,0},{5,1},{6,2},{7,3},{8,4},{9,5},{1... | collective-permute-start | bytes 6881288 | tf_op jit(solution)/shard_map/ppermute | solution.py:571
  432.3 1.4 copy-start.1
  432.4 84.8 %collective-permute-start.6 = (bf16[4,80,3584]{2,1,0:T(8,128)(2,1)}, bf16[4,80,3584]{2,1,0:T(8,128)(2,1)}, u32[]{:S(2)}, u32[]{:S(2)}) collective-permute-start(bf16[4,80,3584]{2,1,0:T(8,128)(2,1)} %get-tuple-element.55), channel_id=1, source_target_pairs={{0,4},{1,5},{2,6},{3,7},{4,8},{5,9},{6,10},{7,11},{8,12},{9,13},{1... | collective-permute-start | bytes 6881288 | tf_op jit(solution)/shard_map/ppermute | solution.py:571
  432.5 2.0 copy-start.2
  432.5 85.5 %collective-permute-start.9 = (bf16[4,80,3584]{2,1,0:T(8,128)(2,1)}, bf16[4,80,3584]{2,1,0:T(8,128)(2,1)}, u32[]{:S(2)}, u32[]{:S(2)}) collective-permute-start(bf16[4,80,3584]{2,1,0:T(8,128)(2,1)} %get-tuple-element.59), channel_id=1, source_target_pairs={{0,3},{1,0},{2,1},{3,2},{4,7},{5,4},{6,5},{7,6},{8,11},{9,8},{10,9... | collective-permute-start | bytes 6881288 | tf_op jit(solution)/shard_map/ppermute | solution.py:571
  434.5 4.7 copy-start
  492.7 65.2 %collective-permute-start.10 = (bf16[4,80,3584]{2,1,0:T(8,128)(2,1)}, bf16[4,80,3584]{2,1,0:T(8,128)(2,1)}, u32[]{:S(2)}, u32[]{:S(2)}) collective-permute-start(bf16[4,80,3584]{2,1,0:T(8,128)(2,1)} %get-tuple-element.61), channel_id=1, source_target_pairs={{0,1},{1,2},{2,3},{3,0},{4,5},{5,6},{6,7},{7,4},{8,9},{9,10},{10,1... | collective-permute-start | bytes 6881288 | tf_op jit(solution)/shard_map/ppermute | solution.py:571
  514.4 43.5 %collective-permute-start.4 = (bf16[3,80,3584]{2,1,0:T(8,128)(2,1)}, bf16[3,80,3584]{2,1,0:T(8,128)(2,1)}, u32[]{:S(2)}, u32[]{:S(2)}) collective-permute-start(bf16[3,80,3584]{2,1,0:T(8,128)(2,1)} %get-tuple-element.52), channel_id=1, source_target_pairs={{0,4},{1,5},{2,6},{3,7},{4,8},{5,9},{6,10},{7,11},{8,12},{9,13},{1... | collective-permute-start | bytes 5160968 | tf_op jit(solution)/shard_map/ppermute | solution.py:571
  514.5 43.4 %collective-permute-start.7 = (bf16[3,80,3584]{2,1,0:T(8,128)(2,1)}, bf16[3,80,3584]{2,1,0:T(8,128)(2,1)}, u32[]{:S(2)}, u32[]{:S(2)}) collective-permute-start(bf16[3,80,3584]{2,1,0:T(8,128)(2,1)} %get-tuple-element.56), channel_id=1, source_target_pairs={{0,12},{1,13},{2,14},{3,15},{4,0},{5,1},{6,2},{7,3},{8,4},{9,5},{1... | collective-permute-start | bytes 5160968 | tf_op jit(solution)/shard_map/ppermute | solution.py:571
  517.1 63.0 %collective-permute-start.8 = (bf16[3,80,3584]{2,1,0:T(8,128)(2,1)}, bf16[3,80,3584]{2,1,0:T(8,128)(2,1)}, u32[]{:S(2)}, u32[]{:S(2)}) collective-permute-start(bf16[3,80,3584]{2,1,0:T(8,128)(2,1)} %get-tuple-element.58), channel_id=1, source_target_pairs={{0,1},{1,2},{2,3},{3,0},{4,5},{5,6},{6,7},{7,4},{8,9},{9,10},{10,1... | collective-permute-start | bytes 5160968 | tf_op jit(solution)/shard_map/ppermute | solution.py:571
  518.0 62.2 %collective-permute-start.11 = (bf16[3,80,3584]{2,1,0:T(8,128)(2,1)}, bf16[3,80,3584]{2,1,0:T(8,128)(2,1)}, u32[]{:S(2)}, u32[]{:S(2)}) collective-permute-start(bf16[3,80,3584]{2,1,0:T(8,128)(2,1)} %get-tuple-element.62), channel_id=1, source_target_pairs={{0,3},{1,0},{2,1},{3,2},{4,7},{5,4},{6,5},{7,6},{8,11},{9,8},{10,9... | collective-permute-start | bytes 5160968 | tf_op jit(solution)/shard_map/ppermute | solution.py:571

commit v7 on v6

--- a/solution.py
+++ b/solution.py
@@ -13,6 +13,7 @@
 TICKS = 2
 FIRST = 7
 VMEM = 65400 * 1024
+FINISH = 54 * 1024 * 1024
 DEPTH = 4
 DEEP = 3
 PARTS = 3
@@ -438,8 +439,7 @@
 
 def finish_kernel(side, *refs):
     ins, own, rest = refs[:12], refs[12:16], refs[16:]
-    out_ref, in_v, send_v, recv_v, own_v, in_sem, send_sem, recv_sem, own_send, own_recv = rest
-    half, cols = out_ref.shape[0] // 2, out_ref.shape[1] // 2
+    sum_ref, came_ref, in_v, send_v, recv_v, own_v, in_sem, send_sem, recv_sem, own_send, own_recv = rest
     me = lax.axis_index("tp")
     at = (me // side, me % side)
 
@@ -477,7 +477,7 @@
     def message(h, step, way):
         return pltpu.make_async_remote_copy(
             src_ref=send_v.at[h, step, way],
-            dst_ref=recv_v.at[h, step, way],
+            dst_ref=recv_v.at[h, way] if step == 0 else came_ref.at[h, step - 1, way],
             send_sem=send_sem.at[h, step, way],
             recv_sem=recv_sem.at[h, step, way],
             device_id=neighbour(1 - h, 1 - 2 * way),
@@ -511,17 +511,16 @@
                 total = piece(h, j, r)
                 if step == 2:
                     message(h, 0, way).wait_recv()
-                    total += f32(recv_v[h, 0, way])
+                    total += f32(recv_v[h, way])
                 send_v[h, step, way] = bf16(total)
                 message(h, step, way).start()
     for h in range(2):
         for r in range(2):
-            total = piece(h, 0, r)
-            message(h, 1, 1 - r).wait_recv()
-            total += f32(recv_v[h, 1, 1 - r])
-            message(h, 2, r).wait_recv()
-            total += f32(recv_v[h, 2, r])
-            out_ref[r * half : (r + 1) * half, h * cols : (h + 1) * cols] = bf16(total)
+            sum_ref[h, r] = piece(h, 0, r)
+    for step in (1, 2):
+        for h in range(2):
+            for way in range(2):
+                message(h, step, way).wait_recv()
     for h in range(2):
         for way in range(2):
             own_message(h, way).wait_send()
@@ -531,17 +530,17 @@
 
 def finish(side, ins, own):
     _, half, cols = ins[0].shape
-    hbm = pl.BlockSpec(memory_space=pltpu.HBM)
+    hbm, vmem = pl.BlockSpec(memory_space=pltpu.HBM), pl.BlockSpec(memory_space=pltpu.VMEM)
     dtype = jnp.bfloat16
-    return pl.pallas_call(
+    mine, came = pl.pallas_call(
         functools.partial(finish_kernel, side),
-        out_shape=pltpu.VMEM((2 * half, 2 * cols), dtype),
+        out_shape=(pltpu.VMEM((2, 2, half, cols), jnp.float32), pltpu.VMEM((2, 2, 2, half, cols), dtype)),
         in_specs=[hbm] * (len(ins) + len(own)),
-        out_specs=pl.BlockSpec(memory_space=pltpu.VMEM),
+        out_specs=(vmem, vmem),
         scratch_shapes=[
             pltpu.VMEM((2, side, 2, 3, half, cols), dtype),
             pltpu.VMEM((2, 3, 2, half, cols), dtype),
-            pltpu.VMEM((2, 3, 2, half, cols), dtype),
+            pltpu.VMEM((2, 2, half, cols), dtype),
             pltpu.VMEM((2, 2, half, cols), dtype),
             pltpu.SemaphoreType.DMA((2, side, 2, 3)),
             pltpu.SemaphoreType.DMA((2, 3, 2)),
@@ -550,13 +549,33 @@
             pltpu.SemaphoreType.DMA((2, 2)),
         ],
         compiler_params=pltpu.CompilerParams(
-            collective_id=1, has_side_effects=True, vmem_limit_bytes=54 * 1024 * 1024
+            collective_id=1, has_side_effects=True, vmem_limit_bytes=FINISH
         ),
         cost_estimate=pl.CostEstimate(
             flops=64 * half * cols, bytes_accessed=2 * 52 * half * cols, transcendentals=0
         ),
         name="finish_dx",
     )(*ins, *own)
+
+    chunk = tile_of(cols, cols // 2)
+
+    def last_sum(mine_ref, came_ref, out_ref):
+        i = pl.program_id(0)
+        h, c = i // 2, pl.ds(pl.multiple_of(i % 2 * chunk, 128), chunk)
+        for r in range(2):
+            total = mine_ref[h, r, :, c] + f32(came_ref[h, 0, 1 - r, :, c]) + f32(came_ref[h, 1, r, :, c])
+            out_ref[r * half : (r + 1) * half, :] = bf16(total)
+
+    return pl.pallas_call(
+        last_sum,
+        grid=(4,),
+        out_shape=jax.ShapeDtypeStruct((2 * half, 2 * cols), dtype),
+        in_specs=[vmem, vmem],
+        out_specs=pl.BlockSpec((2 * half, chunk), lambda i: (0, i)),
+        compiler_params=pltpu.CompilerParams(vmem_limit_bytes=16 * 1024 * 1024),
+        cost_estimate=pl.CostEstimate(flops=8 * half * cols, bytes_accessed=16 * half * cols, transcendentals=0),
+        name="last_sum",
+    )(mine, came)
 
 
 def solution(mesh):

time: 636 us -> 635 us (level)
    pallas_call x1 -> x2, Pallas kernels: 52.6 us -> 52.6 us  [the longest x1 50.4 us: finish(): pl.pallas_call(functools.partial(finish_kernel, side), out_shape=(pltpu.V...]
where the time goes in v7:
time: 635 us; the launch traced here: 633 us
  Pallas kernels  546 us (86%)
  waiting for transfers between devices  68.4 us (11%)
  starting transfers between devices  11.1 us (2%)
  local copies, waits for them, and re-layouts  6.53 us (1%)
    pallas_call x1, Pallas kernels, gather(): pl.pallas_call(functools.partial(gather_kernel, side, dt, nt), out_shape=...  380 us
    pallas_call x3, Pallas kernels, dw_in(): pl.pallas_call(functools.partial(dw_in_kernel, len(pairs), len(moved)), g...  113 us
    ppermute x12, waiting for transfers between devices, hop(): return lax.ppermute(v, 'tp', pairs)  68.4 us
    pallas_call x1, Pallas kernels, finish(): pl.pallas_call(functools.partial(finish_kernel, side), out_shape=(pltpu.V...  50.4 us
  transfers between devices with their start and end apart: 12, of which 3 were waited for; matrix products, arithmetic and copies ran while one was open for 0% of the time, Pallas kernels for 18%

profile of v7, /device:TPU:97, one launch (start us, length us, event | category | flops | bytes accessed | tf_op | source)
XLA Modules:
  0.0 632.8 jit_solution(17793552736386665239)
XLA Ops:
  0.6 380.3 %gather_and_dx.1 = (bf16[2,2560,7168]{2,1,0:T(8,128)(2,1)}, bf16[2560,2560]{1,0:T(8,128)(2,1)}, bf16[2560,1280]{1,0:T(8,128)(2,1)}, bf16[1280,7168]{1,0:T(8,128)...) custom-call(bf16[160,7168]{1,0:T(8,128)(2,1)} %x_ref.1, ...), custom_call_target="tpu_custom_call" | custom-call | flops 187904819200 | bytes 513802240 | tf_op jit(solution)/shard_map/gather_and_dx/pallas_call | solution.py:336
  380.9 0.1 collective-permute-start
  381.0 0.1 collective-permute-start.1
  381.1 2.5 collective-permute-start.2
  383.7 2.7 collective-permute-start.3
  386.3 46.0 %collective-permute-done.refs_3_ = bf16[4,80,3584]{2,1,0:T(8,128)(2,1)S(1)} collective-permute-done((bf16[4,80,3584]{2,1,0:T(8,128)(2,1)}, bf16[4,80,3584]{2,1,0:T(8,128)(2,1)S(1)}, u32[]{:S(2)}, u32[]{:S(2)}) %collective-permute-start) | collective-permute-done | bytes 2293792 | tf_op jit(solution)/shard_map/ppermute | solution.py:590
  432.4 0.1 collective-permute-done.1.refs_5_
  432.5 0.2 collective-permute-start.9
  432.7 1.1 copy-done.1
  433.7 0.7 copy-done.2
  434.5 4.7 copy-done
  439.2 53.5 %dw_in.3 = (bf16[7168,1280]{1,0:T(8,128)(2,1)}, bf16[7168,1280]{1,0:T(8,128)(2,1)}, bf16[1280,7168]{1,0:T(8,128)(2,1)}) custom-call(bf16[2,2560,7168]{2,1,0:T(8,128)(2,1)} %get-tuple-element.41.refs_0_, bf16[2560,2560]{1,0:T(8,128)(2,1)S(1)} %copy-done, bf16[1280,7168]{1,0:T(8,128)(2,1)} %get-tuple-element.51.refs_2_), custom_call_target="tpu_custom_call" | custom-call | flops 46976204800 | bytes 49807360 | tf_op jit(solution)/shard_map/dw_in/pallas_call | solution.py:412
  492.7 0.0 collective-permute-start.10
  492.7 0.0 collective-permute-done.3.refs_9_
  492.7 21.7 %dw_in.4 = (bf16[7168,1280]{1,0:T(8,128)(2,1)}, bf16[7168,1280]{1,0:T(8,128)(2,1)}, bf16[1,80,3584]{2,1,0:T(8,128)(2,1)}, bf16[3,80,3584]{2,1,0:T(8,128)(2,1)}, ...) custom-call(bf16[2,2560,7168]{2,1,0:T(8,128)(2,1)} %get-tuple-elemen, ...), custom_call_target="tpu_custom_call", output_to_operand_aliasing={{0}: (10, {}), {1}: (11, {})} | custom-call | flops 13421772800 | bytes 23592960 | tf_op jit(solution)/shard_map/dw_in/pallas_call | solution.py:412
  514.4 0.1 collective-permute-start.4
  514.5 2.6 collective-permute-start.7
  517.2 0.8 collective-permute-start.8
  518.0 0.0 collective-permute-done.9.refs_8_
  518.0 1.9 collective-permute-start.11
  519.9 38.0 %dw_in.5 = (bf16[7168,1280]{1,0:T(8,128)(2,1)}, bf16[7168,1280]{1,0:T(8,128)(2,1)}) custom-call(bf16[2,2560,7168]{2,1,0:T(8,128)(2,1)} %get-tuple-element.41.refs_0_, bf16[2560,2560]{1,0:T(8,128)(2,1)S(1)} %copy-done, bf16[7168,1280]{1,0:T(8,128)(2,1)} %get-tuple-element.71.refs_2_, ...), custom_call_target="tpu_custom_call", output_to_operand_aliasing={{0}: (2, {}), {1}: (3, {})} | custom-call | flops 33554432000 | bytes 39321600 | tf_op jit(solution)/shard_map/dw_in/pallas_call | solution.py:412
  557.9 22.3 %collective-permute-done.8.refs_7_ = bf16[3,80,3584]{2,1,0:T(8,128)(2,1)} collective-permute-done((bf16[3,80,3584]{2,1,0:T(8,128)(2,1)}, bf16[3,80,3584]{2,1,0:T(8,128)(2,1)}, u32[]{:S(2)}, u32[]{:S(2)}) %collective-permute-start.8) | collective-permute-done | bytes 1720352 | tf_op jit(solution)/shard_map/ppermute | solution.py:590
  580.2 50.4 %finish_dx.1 = (f32[2,2,80,3584]{3,2,1,0:T(8,128)S(1)}, bf16[2,2,2,80,3584]{4,3,2,1,0:T(8,128)(2,1)S(1)}) custom-call(bf16[4,80,3584]{2,1,0:T(8,128)(2,1)} %get-tuple-element.40.refs_0_, bf16[3,80,3584]{2,1,0:T(8,128)(2,1)} %collective-permute-done.4.refs_1_, bf16[4,80,3584]{2,1,0:T(8,128)(2,1)} %collective-permute-done.5.refs_2_, ...), custom_call_target="tpu_custom_call" | custom-call | flops 18350080 | bytes 29818880 | tf_op jit(solution)/shard_map/finish_dx/pallas_call | solution.py:535
  630.6 2.2 last_sum.1
  (12 shorter events, 0.0 us)
Async XLA Ops:
  380.9 51.4 %collective-permute-start = (bf16[4,80,3584]{2,1,0:T(8,128)(2,1)}, bf16[4,80,3584]{2,1,0:T(8,128)(2,1)S(1)}, u32[]{:S(2)}, u32[]{:S(2)}) collective-permute-start(bf16[4,80,3584]{2,1,0:T(8,128)(2,1)} %get-tuple-element.44), channel_id=1, source_target_pairs={{0,4},{1,5},{2,6},{3,7},{4,8},{5,9},{6,10},{7,11},{8,12},{9,13},{1... | collective-permute-start | bytes 6881288 | tf_op jit(solution)/shard_map/ppermute | solution.py:590
  381.0 51.4 %collective-permute-start.1 = (bf16[4,80,3584]{2,1,0:T(8,128)(2,1)}, bf16[4,80,3584]{2,1,0:T(8,128)(2,1)S(1)}, u32[]{:S(2)}, u32[]{:S(2)}) collective-permute-start(bf16[4,80,3584]{2,1,0:T(8,128)(2,1)} %get-tuple-element.46), channel_id=1, source_target_pairs={{0,1},{1,2},{2,3},{3,0},{4,5},{5,6},{6,7},{7,4},{8,9},{9,10},{10,1... | collective-permute-start | bytes 6881288 | tf_op jit(solution)/shard_map/ppermute | solution.py:590
  381.1 111.6 %collective-permute-start.2 = (bf16[4,80,3584]{2,1,0:T(8,128)(2,1)}, bf16[4,80,3584]{2,1,0:T(8,128)(2,1)}, u32[]{:S(2)}, u32[]{:S(2)}) collective-permute-start(bf16[4,80,3584]{2,1,0:T(8,128)(2,1)} %get-tuple-element.48), channel_id=1, source_target_pairs={{0,12},{1,13},{2,14},{3,15},{4,0},{5,1},{6,2},{7,3},{8,4},{9,5},{1... | collective-permute-start | bytes 6881288 | tf_op jit(solution)/shard_map/ppermute | solution.py:590
  383.7 109.1 %collective-permute-start.3 = (bf16[4,80,3584]{2,1,0:T(8,128)(2,1)}, bf16[4,80,3584]{2,1,0:T(8,128)(2,1)}, u32[]{:S(2)}, u32[]{:S(2)}) collective-permute-start(bf16[4,80,3584]{2,1,0:T(8,128)(2,1)} %get-tuple-element.50), channel_id=1, source_target_pairs={{0,3},{1,0},{2,1},{3,2},{4,7},{5,4},{6,5},{7,6},{8,11},{9,8},{10,9... | collective-permute-start | bytes 6881288 | tf_op jit(solution)/shard_map/ppermute | solution.py:590
  386.3 128.2 %collective-permute-start.5 = (bf16[4,80,3584]{2,1,0:T(8,128)(2,1)}, bf16[4,80,3584]{2,1,0:T(8,128)(2,1)}, u32[]{:S(2)}, u32[]{:S(2)}) collective-permute-start(bf16[4,80,3584]{2,1,0:T(8,128)(2,1)} %get-tuple-element.55), channel_id=1, source_target_pairs={{0,12},{1,13},{2,14},{3,15},{4,0},{5,1},{6,2},{7,3},{8,4},{9,5},{1... | collective-permute-start | bytes 6881288 | tf_op jit(solution)/shard_map/ppermute | solution.py:590
  432.3 1.4 copy-start.1
  432.4 84.8 %collective-permute-start.6 = (bf16[4,80,3584]{2,1,0:T(8,128)(2,1)}, bf16[4,80,3584]{2,1,0:T(8,128)(2,1)}, u32[]{:S(2)}, u32[]{:S(2)}) collective-permute-start(bf16[4,80,3584]{2,1,0:T(8,128)(2,1)} %get-tuple-element.57), channel_id=1, source_target_pairs={{0,4},{1,5},{2,6},{3,7},{4,8},{5,9},{6,10},{7,11},{8,12},{9,13},{1... | collective-permute-start | bytes 6881288 | tf_op jit(solution)/shard_map/ppermute | solution.py:590
  432.5 2.0 copy-start.2
  432.5 85.5 %collective-permute-start.9 = (bf16[4,80,3584]{2,1,0:T(8,128)(2,1)}, bf16[4,80,3584]{2,1,0:T(8,128)(2,1)}, u32[]{:S(2)}, u32[]{:S(2)}) collective-permute-start(bf16[4,80,3584]{2,1,0:T(8,128)(2,1)} %get-tuple-element.61), channel_id=1, source_target_pairs={{0,3},{1,0},{2,1},{3,2},{4,7},{5,4},{6,5},{7,6},{8,11},{9,8},{10,9... | collective-permute-start | bytes 6881288 | tf_op jit(solution)/shard_map/ppermute | solution.py:590
  434.5 4.7 copy-start
  492.7 65.2 %collective-permute-start.10 = (bf16[4,80,3584]{2,1,0:T(8,128)(2,1)}, bf16[4,80,3584]{2,1,0:T(8,128)(2,1)}, u32[]{:S(2)}, u32[]{:S(2)}) collective-permute-start(bf16[4,80,3584]{2,1,0:T(8,128)(2,1)} %get-tuple-element.63), channel_id=1, source_target_pairs={{0,1},{1,2},{2,3},{3,0},{4,5},{5,6},{6,7},{7,4},{8,9},{9,10},{10,1... | collective-permute-start | bytes 6881288 | tf_op jit(solution)/shard_map/ppermute | solution.py:590
  514.4 43.5 %collective-permute-start.4 = (bf16[3,80,3584]{2,1,0:T(8,128)(2,1)}, bf16[3,80,3584]{2,1,0:T(8,128)(2,1)}, u32[]{:S(2)}, u32[]{:S(2)}) collective-permute-start(bf16[3,80,3584]{2,1,0:T(8,128)(2,1)} %get-tuple-element.54), channel_id=1, source_target_pairs={{0,4},{1,5},{2,6},{3,7},{4,8},{5,9},{6,10},{7,11},{8,12},{9,13},{1... | collective-permute-start | bytes 5160968 | tf_op jit(solution)/shard_map/ppermute | solution.py:590
  514.5 43.4 %collective-permute-start.7 = (bf16[3,80,3584]{2,1,0:T(8,128)(2,1)}, bf16[3,80,3584]{2,1,0:T(8,128)(2,1)}, u32[]{:S(2)}, u32[]{:S(2)}) collective-permute-start(bf16[3,80,3584]{2,1,0:T(8,128)(2,1)} %get-tuple-element.58), channel_id=1, source_target_pairs={{0,12},{1,13},{2,14},{3,15},{4,0},{5,1},{6,2},{7,3},{8,4},{9,5},{1... | collective-permute-start | bytes 5160968 | tf_op jit(solution)/shard_map/ppermute | solution.py:590
  517.2 63.0 %collective-permute-start.8 = (bf16[3,80,3584]{2,1,0:T(8,128)(2,1)}, bf16[3,80,3584]{2,1,0:T(8,128)(2,1)}, u32[]{:S(2)}, u32[]{:S(2)}) collective-permute-start(bf16[3,80,3584]{2,1,0:T(8,128)(2,1)} %get-tuple-element.60), channel_id=1, source_target_pairs={{0,1},{1,2},{2,3},{3,0},{4,5},{5,6},{6,7},{7,4},{8,9},{9,10},{10,1... | collective-permute-start | bytes 5160968 | tf_op jit(solution)/shard_map/ppermute | solution.py:590
  518.0 62.2 %collective-permute-start.11 = (bf16[3,80,3584]{2,1,0:T(8,128)(2,1)}, bf16[3,80,3584]{2,1,0:T(8,128)(2,1)}, u32[]{:S(2)}, u32[]{:S(2)}) collective-permute-start(bf16[3,80,3584]{2,1,0:T(8,128)(2,1)} %get-tuple-element.64), channel_id=1, source_target_pairs={{0,3},{1,0},{2,1},{3,2},{4,7},{5,4},{6,5},{7,6},{8,11},{9,8},{10,9... | collective-permute-start | bytes 5160968 | tf_op jit(solution)/shard_map/ppermute | solution.py:590

commit v8 on v7

--- a/solution.py
+++ b/solution.py
@@ -388,8 +388,14 @@
     for k in range(sums):
         mine, came = rest[2 * k : 2 * k + 2]
         total = bf16(f32(mine[...]) + f32(came[...]))
-        outs[2 + 2 * k][...] = total[:1]
-        outs[3 + 2 * k][...] = total[1:]
+        first, others = outs[2 + 2 * k], outs[3 + 2 * k]
+        half, away = total.shape[1], total.shape[0] - 1
+        early = half - first.shape[0]
+        for j in range(away):
+            others[j * half : (j + 1) * half, :] = total[1 + j]
+        if early:
+            others[away * half :, :] = total[0, :early]
+        first[...] = total[0, early:]
     for k in range(moved):
         outs[2 + 2 * sums + k][...] = rest[2 * sums + k][...]
 
@@ -399,15 +405,19 @@
     ff = dgu.shape[1] // 2
     bd = tile_of(d, 256)
     n = last - first
-    flat = [v for pair in pairs for v in pair]
+    flat = [v for pair in pairs for v in pair[:2]]
     resident = 2 * dgu.size
 
     def along(v):
         lead = v.shape[:-1]
         return pl.BlockSpec((*lead, v.shape[-1] // n), lambda i: (*[0] * len(lead), i))
 
-    cut = [jax.ShapeDtypeStruct((k, *a.shape[1:]), a.dtype) for a, _ in pairs for k in (1, a.shape[0] - 1)]
-    extra = [*cut, *moved]
+    extra = []
+    for v, _, early in pairs:
+        blocks, half, cols = v.shape
+        for height in (half - early, (blocks - 1) * half + early):
+            extra.append(jax.ShapeDtypeStruct((height, cols), v.dtype))
+    extra += moved
     new = [jax.ShapeDtypeStruct((d, ff), full.dtype)] * 2 + [jax.ShapeDtypeStruct(v.shape, v.dtype) for v in extra]
     return pl.pallas_call(
         functools.partial(dw_in_kernel, len(pairs), len(moved)),
@@ -437,9 +447,13 @@
     return v.astype(jnp.bfloat16)
 
 
-def finish_kernel(side, *refs):
+def finish_kernel(side, cut, *refs):
     ins, own, rest = refs[:12], refs[12:16], refs[16:]
-    sum_ref, came_ref, in_v, send_v, recv_v, own_v, in_sem, send_sem, recv_sem, own_send, own_recv = rest
+    sum_ref, came_f, came_b, in_v, send_v, far_f, far_b, own_f, own_b, near_f, near_b, *sems = rest
+    in_sem, send_sem, recv_sem, own_send, own_recv = sems
+    rows, _ = sum_ref.shape[1:]
+    half = rows // 2
+    over = cut - half
     me = lax.axis_index("tp")
     at = (me // side, me % side)
 
@@ -452,22 +466,30 @@
     for axis, sign in LINKS:
         pl.semaphore_signal(barrier, inc=1, device_id=neighbour(axis, sign), device_id_type=MESH)
 
-    order = (((2, 0), (2, 1)), ((1, 1), (3, 0)), ((1, 0), (3, 1)))
+    def late(r):
+        return 1 + r
+
+    early = ins[1].shape[0] - 3 * half
 
     def loads(h, j, r):
         copies = []
         for k in range(3):
-            late = k == 1 + r
-            if late and j == 0:
+            src, dst = ins[6 * h + 3 * r + k], in_v.at[h, j, r, k]
+            if k != late(r):
+                src = src.at[j]
+            elif j > 0:
+                src = src.at[pl.ds((j - 1) * half, half)]
+            elif r == 0:
+                src, dst = src.at[pl.ds(3 * half, early)], dst.at[pl.ds(0, early)]
+            else:
                 continue
-            src = ins[6 * h + 3 * r + k].at[j - 1 if late else j]
-            copies.append(pltpu.make_async_copy(src, in_v.at[h, j, r, k], in_sem.at[h, j, r, k]))
+            copies.append(pltpu.make_async_copy(src, dst, in_sem.at[h, j, r, k]))
         return copies
 
     def own_message(h, way):
         return pltpu.make_async_remote_copy(
-            src_ref=own[2 * h + way].at[0],
-            dst_ref=own_v.at[h, way],
+            src_ref=own[2 * h + way],
+            dst_ref=(own_f, own_b)[way].at[h],
             send_sem=own_send.at[h, way],
             recv_sem=own_recv.at[h, way],
             device_id=neighbour(h, 1 - 2 * way),
@@ -475,29 +497,30 @@
         )
 
     def message(h, step, way):
+        top = way == 0 if step != 1 else way == 1
+        block = pl.ds(0, cut) if top else pl.ds(cut, rows - cut)
+        if step < 2:
+            src = send_v.at[h, 2 if step == 0 else 1 + 2 * way, block]
+        else:
+            src = (near_f, near_b)[way].at[h]
+        dst = (far_f, far_b)[way].at[h] if step == 0 else (came_f if top else came_b).at[h, step - 1]
         return pltpu.make_async_remote_copy(
-            src_ref=send_v.at[h, step, way],
-            dst_ref=recv_v.at[h, way] if step == 0 else came_ref.at[h, step - 1, way],
+            src_ref=src,
+            dst_ref=dst,
             send_sem=send_sem.at[h, step, way],
             recv_sem=recv_sem.at[h, step, way],
             device_id=neighbour(1 - h, 1 - 2 * way),
             device_id_type=MESH,
         )
 
-    def piece(h, j, r):
-        for c in loads(h, j, r):
-            c.wait()
-        total = f32(in_v[h, j, r, 0])
-        for k in (1, 2):
-            if k == 1 + r and j == 0:
-                own_message(h, r).wait_recv()
-                total += f32(own_v[h, r])
-            else:
-                total += f32(in_v[h, j, r, k])
-        return total
-
-    pieces = [p for step in order for p in step] + [(0, 0), (0, 1)]
-    for j, r in pieces:
+    def piece(h, j, r, wait=True):
+        if wait:
+            for c in loads(h, j, r):
+                c.wait()
+        return f32(in_v[h, j, r, 0]) + f32(in_v[h, j, r, 1]) + f32(in_v[h, j, r, 2])
+
+    order = ((2, 0), (2, 1), (1, 1), (3, 0), (3, 1), (1, 0), (0, 0), (0, 1))
+    for j, r in order:
         for h in range(2):
             for c in loads(h, j, r):
                 c.start()
@@ -505,18 +528,40 @@
     for h in range(2):
         for way in range(2):
             own_message(h, way).start()
-    for step, steps in enumerate(order):
-        for h in range(2):
-            for way, (j, r) in enumerate(steps):
-                total = piece(h, j, r)
-                if step == 2:
-                    message(h, 0, way).wait_recv()
-                    total += f32(recv_v[h, way])
-                send_v[h, step, way] = bf16(total)
-                message(h, step, way).start()
+
+    def ready(h, j, r):
+        send_v[h, j, r * half : (r + 1) * half, :] = bf16(piece(h, j, r))
+
+    for h in range(2):
+        ready(h, 2, 0)
+        ready(h, 2, 1)
+        message(h, 0, 0).start()
+        message(h, 0, 1).start()
+    for h in range(2):
+        ready(h, 1, 1)
+        message(h, 1, 0).start()
+        ready(h, 3, 0)
+        ready(h, 3, 1)
+        message(h, 1, 1).start()
+    for h in range(2):
+        message(h, 0, 0).wait_recv()
+        near_f[h, :half, :] = bf16(piece(h, 1, 0) + f32(far_f[h, :half, :]))
+        near_f[h, half:, :] = bf16(piece(h, 1, 1, False)[:over] + f32(far_f[h, half:, :]))
+        message(h, 2, 0).start()
+        message(h, 0, 1).wait_recv()
+        near_b[h] = bf16(piece(h, 3, 1, False)[over:] + f32(far_b[h]))
+        message(h, 2, 1).start()
     for h in range(2):
         for r in range(2):
-            sum_ref[h, r] = piece(h, 0, r)
+            for c in loads(h, 0, r):
+                c.wait()
+        kept = f32(in_v[h, 0, 0, 0]) + f32(in_v[h, 0, 0, 2])
+        own_message(h, 0).wait_recv()
+        sum_ref[h, :early, :] = kept[:early] + f32(in_v[h, 0, 0, 1, :early, :])
+        sum_ref[h, early:half, :] = kept[early:] + f32(own_f[h])
+        kept = f32(in_v[h, 0, 1, 0]) + f32(in_v[h, 0, 1, 1])
+        own_message(h, 1).wait_recv()
+        sum_ref[h, half:, :] = kept + f32(own_b[h])
     for step in (1, 2):
         for h in range(2):
             for way in range(2):
@@ -528,20 +573,29 @@
                 message(h, step, way).wait_send()
 
 
-def finish(side, ins, own):
+def finish(side, cut, ins, own):
     _, half, cols = ins[0].shape
+    rows = 2 * half
     hbm, vmem = pl.BlockSpec(memory_space=pltpu.HBM), pl.BlockSpec(memory_space=pltpu.VMEM)
     dtype = jnp.bfloat16
-    mine, came = pl.pallas_call(
-        functools.partial(finish_kernel, side),
-        out_shape=(pltpu.VMEM((2, 2, half, cols), jnp.float32), pltpu.VMEM((2, 2, 2, half, cols), dtype)),
+    mine, came_f, came_b = pl.pallas_call(
+        functools.partial(finish_kernel, side, cut),
+        out_shape=(
+            pltpu.VMEM((2, rows, cols), jnp.float32),
+            pltpu.VMEM((2, 2, cut, cols), dtype),
+            pltpu.VMEM((2, 2, rows - cut, cols), dtype),
+        ),
         in_specs=[hbm] * (len(ins) + len(own)),
-        out_specs=(vmem, vmem),
+        out_specs=(vmem,) * 3,
         scratch_shapes=[
             pltpu.VMEM((2, side, 2, 3, half, cols), dtype),
-            pltpu.VMEM((2, 3, 2, half, cols), dtype),
-            pltpu.VMEM((2, 2, half, cols), dtype),
-            pltpu.VMEM((2, 2, half, cols), dtype),
+            pltpu.VMEM((2, side, rows, cols), dtype),
+            pltpu.VMEM((2, cut, cols), dtype),
+            pltpu.VMEM((2, rows - cut, cols), dtype),
+            pltpu.VMEM((2, *own[0].shape), dtype),
+            pltpu.VMEM((2, *own[1].shape), dtype),
+            pltpu.VMEM((2, cut, cols), dtype),
+            pltpu.VMEM((2, rows - cut, cols), dtype),
             pltpu.SemaphoreType.DMA((2, side, 2, 3)),
             pltpu.SemaphoreType.DMA((2, 3, 2)),
             pltpu.SemaphoreType.DMA((2, 3, 2)),
@@ -559,23 +613,22 @@
 
     chunk = tile_of(cols, cols // 2)
 
-    def last_sum(mine_ref, came_ref, out_ref):
+    def last_sum(mine_ref, f_ref, b_ref, out_ref):
         i = pl.program_id(0)
         h, c = i // 2, pl.ds(pl.multiple_of(i % 2 * chunk, 128), chunk)
-        for r in range(2):
-            total = mine_ref[h, r, :, c] + f32(came_ref[h, 0, 1 - r, :, c]) + f32(came_ref[h, 1, r, :, c])
-            out_ref[r * half : (r + 1) * half, :] = bf16(total)
+        for ref, block in ((f_ref, slice(0, cut)), (b_ref, slice(cut, rows))):
+            out_ref[block, :] = bf16(mine_ref[h, block, c] + f32(ref[h, 0, :, c]) + f32(ref[h, 1, :, c]))
 
     return pl.pallas_call(
         last_sum,
         grid=(4,),
-        out_shape=jax.ShapeDtypeStruct((2 * half, 2 * cols), dtype),
-        in_specs=[vmem, vmem],
-        out_specs=pl.BlockSpec((2 * half, chunk), lambda i: (0, i)),
+        out_shape=jax.ShapeDtypeStruct((rows, 2 * cols), dtype),
+        in_specs=[vmem] * 3,
+        out_specs=pl.BlockSpec((rows, chunk), lambda i: (0, i)),
         compiler_params=pltpu.CompilerParams(vmem_limit_bytes=16 * 1024 * 1024),
         cost_estimate=pl.CostEstimate(flops=8 * half * cols, bytes_accessed=16 * half * cols, transcendentals=0),
         name="last_sum",
-    )(mine, came)
+    )(mine, came_f, came_b)
 
 
 def solution(mesh):
@@ -598,14 +651,15 @@
         far = [(hop(v[2][0], h, 1), hop(v[2][1], h, -1)) for h, v in enumerate(t)]
         raw = [(hop(v[1][1], h, 1), hop(v[3][0], h, -1)) for h, v in enumerate(t)]
         *dw, dw_down = dw_in(full, dgu, cuts[0], cuts[1], moved=[dw_down])
-        pairs = [(v[1][0], f[0]) for v, f in zip(t, far)] + [(v[3][1], f[1]) for v, f in zip(t, far)]
+        half = x.shape[0] // 2
+        pairs = [(v[1][0], f[0], 2 * half // 5) for v, f in zip(t, far)] + [(v[3][1], f[1], 0) for v, f in zip(t, far)]
         *dw, a0, a, b0, b, c0, c, d0, d = dw_in(full, dgu, cuts[1], cuts[2], dw, pairs)
         near = [(hop(up_, h, 1), hop(down, h, -1)) for h, (up_, down) in enumerate(((a, c), (b, d)))]
         dw = dw_in(full, dgu, cuts[2], cuts[3], dw)
         ins = []
         for v, r, n in zip(t, raw, near):
             ins += [v[0][0], n[0], r[1], v[0][1], r[0], n[1]]
-        dx = finish(side, ins, [a0, c0, b0, d0])
+        dx = finish(side, half + half // 5, ins, [a0, c0, b0, d0])
         return dx, *dw, dw_down
 
     rows, both, cols = P(("dp", "tp"), None), P("dp", "tp"), P(None, "tp")

time: 635 us -> 637 us (level)
  transfers between devices with their start and end apart: 12 -> 12, of which waited for: 3 -> 4; matrix products, arithmetic and copies ran while one was open for 0% -> 0% of each run, Pallas kernels for 18% -> 18%
where the time goes in v8:
time: 637 us; the launch traced here: 635 us
  Pallas kernels  544 us (85%)
  waiting for transfers between devices  74.1 us (12%)
  starting transfers between devices  10.4 us (2%)
  local copies, waits for them, and re-layouts  6.53 us (1%)
    pallas_call x1, Pallas kernels, gather(): pl.pallas_call(functools.partial(gather_kernel, side, dt, nt), out_shape=...  380 us
    pallas_call x3, Pallas kernels, dw_in(): pl.pallas_call(functools.partial(dw_in_kernel, len(pairs), len(moved)), g...  113 us
    ppermute x12, waiting for transfers between devices, hop(): return lax.ppermute(v, 'tp', pairs)  74.1 us
    pallas_call x1, Pallas kernels, finish(): pl.pallas_call(functools.partial(finish_kernel, side, cut), out_shape=(pl...  47.9 us
  transfers between devices with their start and end apart: 12, of which 4 were waited for; matrix products, arithmetic and copies ran while one was open for 0% of the time, Pallas kernels for 18%

profile of v8, /device:TPU:97, one launch (start us, length us, event | category | flops | bytes accessed | tf_op | source)
XLA Modules:
  0.0 635.3 jit_solution(415289388781115844)
XLA Ops:
  0.6 380.3 %gather_and_dx.1 = (bf16[2,2560,7168]{2,1,0:T(8,128)(2,1)}, bf16[2560,2560]{1,0:T(8,128)(2,1)}, bf16[2560,1280]{1,0:T(8,128)(2,1)}, bf16[1280,7168]{1,0:T(8,128)...) custom-call(bf16[160,7168]{1,0:T(8,128)(2,1)} %x_ref.1, ...), custom_call_target="tpu_custom_call" | custom-call | flops 187904819200 | bytes 513802240 | tf_op jit(solution)/shard_map/gather_and_dx/pallas_call | solution.py:336
  380.9 0.1 collective-permute-start
  381.0 0.1 collective-permute-start.1
  381.1 2.5 collective-permute-start.2
  383.7 2.7 collective-permute-start.3
  386.3 46.0 %collective-permute-done.refs_3_ = bf16[4,80,3584]{2,1,0:T(8,128)(2,1)S(1)} collective-permute-done((bf16[4,80,3584]{2,1,0:T(8,128)(2,1)}, bf16[4,80,3584]{2,1,0:T(8,128)(2,1)S(1)}, u32[]{:S(2)}, u32[]{:S(2)}) %collective-permute-start) | collective-permute-done | bytes 2293792 | tf_op jit(solution)/shard_map/ppermute | solution.py:643
  432.4 0.1 collective-permute-done.1.refs_5_
  432.5 0.2 collective-permute-start.9
  432.7 1.1 copy-done.1
  433.7 0.7 copy-done.2
  434.5 4.7 copy-done
  439.2 53.5 %dw_in.3 = (bf16[7168,1280]{1,0:T(8,128)(2,1)}, bf16[7168,1280]{1,0:T(8,128)(2,1)}, bf16[1280,7168]{1,0:T(8,128)(2,1)}) custom-call(bf16[2,2560,7168]{2,1,0:T(8,128)(2,1)} %get-tuple-element.42.refs_0_, bf16[2560,2560]{1,0:T(8,128)(2,1)S(1)} %copy-done, bf16[1280,7168]{1,0:T(8,128)(2,1)} %get-tuple-element.52.refs_2_), custom_call_target="tpu_custom_call" | custom-call | flops 46976204800 | bytes 49807360 | tf_op jit(solution)/shard_map/dw_in/pallas_call | solution.py:422
  492.7 0.0 collective-permute-start.10
  492.7 0.0 collective-permute-done.3.refs_9_
  492.7 21.6 %dw_in.4 = (bf16[7168,1280]{1,0:T(8,128)(2,1)}, bf16[7168,1280]{1,0:T(8,128)(2,1)}, bf16[48,3584]{1,0:T(8,128)(2,1)}, bf16[272,3584]{1,0:T(8,128)(2,1)}, bf16[48...) custom-call(bf16[2,2560,7168]{2,1,0:T(8,128)(2,1)} %get-tuple-elemen, ...), custom_call_target="tpu_custom_call", output_to_operand_aliasing={{0}: (10, {}), {1}: (11, {})} | custom-call | flops 13421772800 | bytes 23592960 | tf_op jit(solution)/shard_map/dw_in/pallas_call | solution.py:422
  514.4 2.1 collective-permute-start.7
  516.4 0.0 collective-permute-done.5.refs_2_
  516.4 2.6 collective-permute-start.11
  519.0 0.1 collective-permute-start.8
  519.1 38.0 %dw_in.5 = (bf16[7168,1280]{1,0:T(8,128)(2,1)}, bf16[7168,1280]{1,0:T(8,128)(2,1)}) custom-call(bf16[2,2560,7168]{2,1,0:T(8,128)(2,1)} %get-tuple-element.42.refs_0_, bf16[2560,2560]{1,0:T(8,128)(2,1)S(1)} %copy-done, bf16[7168,1280]{1,0:T(8,128)(2,1)} %get-tuple-element.73.refs_2_, ...), custom_call_target="tpu_custom_call", output_to_operand_aliasing={{0}: (2, {}), {1}: (3, {})} | custom-call | flops 33554432000 | bytes 39321600 | tf_op jit(solution)/shard_map/dw_in/pallas_call | solution.py:422
  557.2 4.0 collective-permute-done.4.refs_1_
  561.1 24.0 %collective-permute-done.8.refs_7_ = bf16[272,3584]{1,0:T(8,128)(2,1)} collective-permute-done((bf16[272,3584]{1,0:T(8,128)(2,1)}, bf16[272,3584]{1,0:T(8,128)(2,1)}, u32[]{:S(2)}, u32[]{:S(2)}) %collective-permute-start.8) | collective-permute-done | bytes 1949728 | tf_op jit(solution)/shard_map/ppermute | solution.py:643
  585.1 47.9 %finish_dx.1 = (f32[2,160,3584]{2,1,0:T(8,128)S(1)}, bf16[2,2,96,3584]{3,2,1,0:T(8,128)(2,1)S(1)}, bf16[2,2,64,3584]{3,2,1,0:T(8,128)(2,1)S(1)}) custom-call(bf16[4,80,3584]{2,1,0:T(8,128)(2,1)} %get-tuple-element.41.refs_0_, bf16[272,3584]{1,0:T(8,128)(2,1)} %collective-permute-done.4.refs_1_, bf16[4,80,3584]{2,1,0:T(8,128)(2,1)} %collective-permute-done.5.refs_2_, ...), custom_call_target="tpu_custom_call" | custom-call | flops 18350080 | bytes 29818880 | tf_op jit(solution)/shard_map/finish_dx/pallas_call | solution.py:581
  633.1 2.2 last_sum.1
  (12 shorter events, 0.0 us)
Async XLA Ops:
  380.9 51.4 %collective-permute-start = (bf16[4,80,3584]{2,1,0:T(8,128)(2,1)}, bf16[4,80,3584]{2,1,0:T(8,128)(2,1)S(1)}, u32[]{:S(2)}, u32[]{:S(2)}) collective-permute-start(bf16[4,80,3584]{2,1,0:T(8,128)(2,1)} %get-tuple-element.45), channel_id=1, source_target_pairs={{0,4},{1,5},{2,6},{3,7},{4,8},{5,9},{6,10},{7,11},{8,12},{9,13},{1... | collective-permute-start | bytes 6881288 | tf_op jit(solution)/shard_map/ppermute | solution.py:643
  381.0 51.4 %collective-permute-start.1 = (bf16[4,80,3584]{2,1,0:T(8,128)(2,1)}, bf16[4,80,3584]{2,1,0:T(8,128)(2,1)S(1)}, u32[]{:S(2)}, u32[]{:S(2)}) collective-permute-start(bf16[4,80,3584]{2,1,0:T(8,128)(2,1)} %get-tuple-element.47), channel_id=1, source_target_pairs={{0,1},{1,2},{2,3},{3,0},{4,5},{5,6},{6,7},{7,4},{8,9},{9,10},{10,1... | collective-permute-start | bytes 6881288 | tf_op jit(solution)/shard_map/ppermute | solution.py:643
  381.1 111.6 %collective-permute-start.2 = (bf16[4,80,3584]{2,1,0:T(8,128)(2,1)}, bf16[4,80,3584]{2,1,0:T(8,128)(2,1)}, u32[]{:S(2)}, u32[]{:S(2)}) collective-permute-start(bf16[4,80,3584]{2,1,0:T(8,128)(2,1)} %get-tuple-element.49), channel_id=1, source_target_pairs={{0,12},{1,13},{2,14},{3,15},{4,0},{5,1},{6,2},{7,3},{8,4},{9,5},{1... | collective-permute-start | bytes 6881288 | tf_op jit(solution)/shard_map/ppermute | solution.py:643
  383.7 109.1 %collective-permute-start.3 = (bf16[4,80,3584]{2,1,0:T(8,128)(2,1)}, bf16[4,80,3584]{2,1,0:T(8,128)(2,1)}, u32[]{:S(2)}, u32[]{:S(2)}) collective-permute-start(bf16[4,80,3584]{2,1,0:T(8,128)(2,1)} %get-tuple-element.51), channel_id=1, source_target_pairs={{0,3},{1,0},{2,1},{3,2},{4,7},{5,4},{6,5},{7,6},{8,11},{9,8},{10,9... | collective-permute-start | bytes 6881288 | tf_op jit(solution)/shard_map/ppermute | solution.py:643
  386.3 130.1 %collective-permute-start.5 = (bf16[4,80,3584]{2,1,0:T(8,128)(2,1)}, bf16[4,80,3584]{2,1,0:T(8,128)(2,1)}, u32[]{:S(2)}, u32[]{:S(2)}) collective-permute-start(bf16[4,80,3584]{2,1,0:T(8,128)(2,1)} %get-tuple-element.56), channel_id=1, source_target_pairs={{0,12},{1,13},{2,14},{3,15},{4,0},{5,1},{6,2},{7,3},{8,4},{9,5},{1... | collective-permute-start | bytes 6881288 | tf_op jit(solution)/shard_map/ppermute | solution.py:643
  432.3 1.4 copy-start.1
  432.4 86.7 %collective-permute-start.6 = (bf16[4,80,3584]{2,1,0:T(8,128)(2,1)}, bf16[4,80,3584]{2,1,0:T(8,128)(2,1)}, u32[]{:S(2)}, u32[]{:S(2)}) collective-permute-start(bf16[4,80,3584]{2,1,0:T(8,128)(2,1)} %get-tuple-element.58), channel_id=1, source_target_pairs={{0,4},{1,5},{2,6},{3,7},{4,8},{5,9},{6,10},{7,11},{8,12},{9,13},{1... | collective-permute-start | bytes 6881288 | tf_op jit(solution)/shard_map/ppermute | solution.py:643
  432.5 2.0 copy-start.2
  432.5 86.6 %collective-permute-start.9 = (bf16[4,80,3584]{2,1,0:T(8,128)(2,1)}, bf16[4,80,3584]{2,1,0:T(8,128)(2,1)}, u32[]{:S(2)}, u32[]{:S(2)}) collective-permute-start(bf16[4,80,3584]{2,1,0:T(8,128)(2,1)} %get-tuple-element.62), channel_id=1, source_target_pairs={{0,3},{1,0},{2,1},{3,2},{4,7},{5,4},{6,5},{7,6},{8,11},{9,8},{10,9... | collective-permute-start | bytes 6881288 | tf_op jit(solution)/shard_map/ppermute | solution.py:643
  434.5 4.7 copy-start
  492.7 64.5 %collective-permute-start.10 = (bf16[4,80,3584]{2,1,0:T(8,128)(2,1)}, bf16[4,80,3584]{2,1,0:T(8,128)(2,1)}, u32[]{:S(2)}, u32[]{:S(2)}) collective-permute-start(bf16[4,80,3584]{2,1,0:T(8,128)(2,1)} %get-tuple-element.64), channel_id=1, source_target_pairs={{0,1},{1,2},{2,3},{3,0},{4,5},{5,6},{6,7},{7,4},{8,9},{9,10},{10,1... | collective-permute-start | bytes 6881288 | tf_op jit(solution)/shard_map/ppermute | solution.py:643
  514.4 42.8 %collective-permute-start.7 = (bf16[240,3584]{1,0:T(8,128)(2,1)}, bf16[240,3584]{1,0:T(8,128)(2,1)}, u32[]{:S(2)}, u32[]{:S(2)}) collective-permute-start(bf16[240,3584]{1,0:T(8,128)(2,1)} %get-tuple-element.59), channel_id=1, source_target_pairs={{0,12},{1,13},{2,14},{3,15},{4,0},{5,1},{6,2},{7,3},{8,4},{9,5},{1... | collective-permute-start | bytes 5160968 | tf_op jit(solution)/shard_map/ppermute | solution.py:643
  516.4 40.7 %collective-permute-start.11 = (bf16[240,3584]{1,0:T(8,128)(2,1)}, bf16[240,3584]{1,0:T(8,128)(2,1)}, u32[]{:S(2)}, u32[]{:S(2)}) collective-permute-start(bf16[240,3584]{1,0:T(8,128)(2,1)} %get-tuple-element.65), channel_id=1, source_target_pairs={{0,3},{1,0},{2,1},{3,2},{4,7},{5,4},{6,5},{7,6},{8,11},{9,8},{10,9... | collective-permute-start | bytes 5160968 | tf_op jit(solution)/shard_map/ppermute | solution.py:643
  519.0 42.1 %collective-permute-start.4 = (bf16[272,3584]{1,0:T(8,128)(2,1)}, bf16[272,3584]{1,0:T(8,128)(2,1)}, u32[]{:S(2)}, u32[]{:S(2)}) collective-permute-start(bf16[272,3584]{1,0:T(8,128)(2,1)} %get-tuple-element.55), channel_id=1, source_target_pairs={{0,4},{1,5},{2,6},{3,7},{4,8},{5,9},{6,10},{7,11},{8,12},{9,13},{1... | collective-permute-start | bytes 5849096 | tf_op jit(solution)/shard_map/ppermute | solution.py:643
  519.0 66.1 %collective-permute-start.8 = (bf16[272,3584]{1,0:T(8,128)(2,1)}, bf16[272,3584]{1,0:T(8,128)(2,1)}, u32[]{:S(2)}, u32[]{:S(2)}) collective-permute-start(bf16[272,3584]{1,0:T(8,128)(2,1)} %get-tuple-element.61), channel_id=1, source_target_pairs={{0,1},{1,2},{2,3},{3,0},{4,5},{5,6},{6,7},{7,4},{8,9},{9,10},{10,1... | collective-permute-start | bytes 5849096 | tf_op jit(solution)/shard_map/ppermute | solution.py:643
